TPU v7x, 8 devices: a whole 2x2x1 slice. The times are simulated.
8 devices in a mesh: dp: 1 (over z), ei: 2 (over y), eo: 4 (over x, core).
Axes of the slice: x: 2, y: 2, z: 1, core: 2. Of those that a mesh axis runs over, the one named last changes fastest.
Arguments:
- x_tokens: bfloat16 [512, 1536], P(('dp', 'ei', 'eo'))
- expert_idx: int32 [512, 8], P(('dp', 'ei', 'eo'))
- gate_vals: float32 [512, 8], P(('dp', 'ei', 'eo'))
- dy_tokens: bfloat16 [512, 1536], P(('dp', 'ei', 'eo'))
- w_gate: bfloat16 [40, 1536, 512], P(('ei', 'eo'))
- w_up: bfloat16 [40, 1536, 512], P(('ei', 'eo'))
- w_down: bfloat16 [40, 512, 1536], P(('ei', 'eo'))
- x_attn: bfloat16 [8, 64, 1536], P(('dp', 'ei', 'eo'))
- w_query: bfloat16 [1536, 24, 64], P(None, ('ei', 'eo'))
- w_key: bfloat16 [1536, 8, 64], P(None, ('ei', 'eo'))
- w_value: bfloat16 [1536, 8, 64], P(None, ('ei', 'eo'))
- w_out: bfloat16 [24, 64, 1536], P(('ei', 'eo'))
Outputs:
- output 1: bfloat16 [512, 1536], P(('dp', 'ei', 'eo'))
- output 2: bfloat16 [512, 1536], P(('dp', 'ei', 'eo'))
- output 3: float32 [512, 8], P(('dp', 'ei', 'eo'))
- output 4: float32 [40, 1536, 512], P(('dp', 'ei', 'eo'))
- output 5: float32 [40, 1536, 512], P(('dp', 'ei', 'eo'))
- output 6: float32 [40, 512, 1536], P(('dp', 'ei', 'eo'))
- output 7: bfloat16 [8, 64, 1536], P(('dp', 'ei', 'eo'))
All inputs are finite; a program needn't handle non-finite values.
Results may differ from a plain program's by a relative error of at most 0.013551.
Values are sent between devices in bfloat16 or wider.
A program may use at most 1 GiB of HBM per device.

v0:
```python
import jax
import jax.numpy as jnp
from jax import lax
from jax.experimental import pallas as pl
from jax.experimental.pallas import tpu as pltpu
from jax.sharding import PartitionSpec as P

GROUP_AXES = ('ei', 'eo')
TOKEN_AXES = ('dp', 'ei', 'eo')
F32 = jnp.float32
BF16 = jnp.bfloat16
MESH_ID = pl.DeviceIdType.MESH
HALVES = 2
NUM_DEV = 8
LANES = 128


def dot_nn(lhs, rhs):
    return jnp.dot(lhs, rhs, preferred_element_type=F32)


def dot_nt(lhs, rhs):
    return lax.dot_general(lhs, rhs, (((1,), (1,)), ((), ())), preferred_element_type=F32)


def dot_tn(lhs, rhs):
    return lax.dot_general(lhs, rhs, (((0,), (0,)), ((), ())), preferred_element_type=F32)


class Place:
    def __init__(self):
        i = lax.axis_index('ei')
        o = lax.axis_index('eo')
        x = lax.div(o, 2)
        c = lax.rem(o, 2)
        self.core = c
        self.chip = i * 2 + x
        self.dev = {}
        self.block = {}
        for flip_y in (0, 1):
            for flip_x in (0, 1):
                for flip_c in (0, 1):
                    yy = 1 - i if flip_y else i
                    xx = 1 - x if flip_x else x
                    cc = 1 - c if flip_c else c
                    name = ('y' if flip_y else '') + ('x' if flip_x else '') + ('c' if flip_c else '')
                    self.dev[name] = (0, yy, xx * 2 + cc)
                    self.block[name] = cc * 4 + yy * 2 + xx
        self.chips = {'': self.chip, 'x': i * 2 + 1 - x, 'y': (1 - i) * 2 + x, 'yx': (1 - i) * 2 + 1 - x}


class Link:
    def __init__(self, pool, src, dst, land, device):
        send, recv = pool.take()
        self.out = pltpu.make_async_remote_copy(src_ref=src, dst_ref=dst, send_sem=send, recv_sem=recv, device_id=device, device_id_type=MESH_ID)
        self.inn = pltpu.make_async_remote_copy(src_ref=land, dst_ref=land, send_sem=send, recv_sem=recv, device_id=device, device_id_type=MESH_ID)

    def start(self):
        self.out.start()

    def arrive(self):
        self.inn.wait_recv()

    def sent(self):
        self.out.wait_send()


class Pool:
    def __init__(self, sends, recvs):
        self.sends, self.recvs, self.used = sends, recvs, 0

    def take(self):
        k = self.used
        self.used += 1
        return self.sends.at[k], self.recvs.at[k]


class Gather:
    def __init__(self, pool, place, buf, rows):
        def at(name, lo=0, n=rows):
            return buf.at[pl.ds(pl.multiple_of(place.block[name] * rows + lo, 8), n), :]

        half = rows // 2
        own = at('')
        dev = place.dev
        self.to_x = Link(pool, own, own, at('x'), dev['x'])
        self.to_y = Link(pool, own, own, at('y'), dev['y'])
        self.to_c = Link(pool, own, own, at('c'), dev['c'])
        self.relay_x = Link(pool, at('y', 0, half), at('y', 0, half), at('yx', 0, half), dev['x'])
        self.relay_y = Link(pool, at('x', half, half), at('x', half, half), at('yx', half, half), dev['y'])
        self.core_x = Link(pool, at('x'), at('x'), at('xc'), dev['c'])
        self.core_y = Link(pool, at('y'), at('y'), at('yc'), dev['c'])
        self.core_d = Link(pool, at('yx'), at('yx'), at('yxc'), dev['c'])
        self.links = (self.to_x, self.to_y, self.to_c, self.relay_x, self.relay_y, self.core_x, self.core_y, self.core_d)

    def begin(self):
        self.to_x.start()
        self.to_y.start()
        self.to_c.start()

    def relay(self):
        self.to_y.arrive()
        self.relay_x.start()
        self.to_x.arrive()
        self.relay_y.start()
        self.core_y.start()
        self.core_x.start()

    def last(self):
        self.relay_x.arrive()
        self.relay_y.arrive()
        self.core_d.start()

    def finish(self):
        self.to_c.arrive()
        self.core_x.arrive()
        self.core_y.arrive()
        self.core_d.arrive()

    def drain(self):
        for link in self.links:
            link.sent()


class Scatter:
    def __init__(self, pool, place, part, from_core, from_x, from_y, last_x, last_y, rows):
        half = rows // 2
        self.half, self.part, self.rows, self.place = half, part, rows, place
        self.from_core, self.from_x, self.from_y, self.last_x, self.last_y = from_core, from_x, from_y, last_x, last_y
        four = 4 * rows
        self.mine = pl.multiple_of(place.core * four, 8)
        other = part.at[pl.ds(pl.multiple_of((1 - place.core) * four, 8), four), :]
        dev = place.dev
        self.core = Link(pool, other, from_core, from_core, dev['c'])
        self.x0 = Link(pool, self.at('x', 0), from_x.at[0], from_x.at[0], dev['x'])
        self.x1 = Link(pool, self.at('yx', 0), from_x.at[1], from_x.at[1], dev['x'])
        self.y0 = Link(pool, self.at('y', half), from_y.at[0], from_y.at[0], dev['y'])
        self.y1 = Link(pool, self.at('yx', half), from_y.at[1], from_y.at[1], dev['y'])
        self.end_y = Link(pool, self.at('y', 0), last_y, last_y, dev['y'])
        self.end_x = Link(pool, self.at('x', half), last_x, last_x, dev['x'])
        self.links = (self.core, self.x0, self.x1, self.y0, self.y1, self.end_y, self.end_x)

    def at(self, name, lo):
        return self.part.at[pl.ds(pl.multiple_of(self.place.block[name] * self.rows + lo, 8), self.half), :]

    def begin(self):
        self.core.start()

    def middle(self):
        self.core.arrive()
        mine = pl.ds(self.mine, 4 * self.rows)
        self.part[mine, :] = self.part[mine, :] + self.from_core[...]
        self.x1.start()
        self.y1.start()
        self.x0.start()
        self.y0.start()

    def late(self):
        self.x1.arrive()
        here = self.at('y', 0)
        here[...] = here[...] + self.from_x[1]
        self.end_y.start()
        self.y1.arrive()
        here = self.at('x', self.half)
        here[...] = here[...] + self.from_y[1]
        self.end_x.start()

    def finish(self, out):
        half = self.half
        self.x0.arrive()
        self.y0.arrive()
        self.end_y.arrive()
        self.end_x.arrive()
        out[0:half, :] = (self.at('', 0)[...] + self.from_x[0] + self.last_y[...]).astype(BF16)
        out[half:2 * half, :] = (self.at('', half)[...] + self.from_y[0] + self.last_x[...]).astype(BF16)

    def drain(self):
        for link in self.links:
            link.sent()


def scatter_shapes(rows, width):
    half = rows // 2
    return [pltpu.VMEM((4 * rows, width), F32), pltpu.VMEM((2, half, width), F32), pltpu.VMEM((2, half, width), F32),
            pltpu.VMEM((half, width), F32), pltpu.VMEM((half, width), F32)]


NUM_LINKS = 7 + 14 + 8 * 5 + 7 * 5


def attention(xa, wqkv, wo, ctx, part, dims):
    seq, kv_dim, heads, head_dim = dims
    q_dim = heads * head_dim
    rows = xa.shape[0]
    pair = 2 * seq
    row = lax.broadcasted_iota(jnp.int32, (pair, pair), 0)
    col = lax.broadcasted_iota(jnp.int32, (pair, pair), 1)
    causal = (row >= col) & ((row >= seq) == (col >= seq))
    for p in range(rows // pair):
        qkv = dot_nn(xa[p * pair:(p + 1) * pair, :], wqkv[...]).astype(BF16)
        keys = qkv[:, q_dim:q_dim + kv_dim]
        vals = qkv[:, q_dim + kv_dim:q_dim + 2 * kv_dim]
        outs = []
        for h in range(heads):
            scores = dot_nt(qkv[:, h * head_dim:(h + 1) * head_dim], keys) * head_dim ** -0.5
            scores = jnp.where(causal, scores, -1e30)
            top = jnp.max(scores, axis=1, keepdims=True)
            ex = jnp.exp(scores - top)
            probs = (ex / jnp.sum(ex, axis=1, keepdims=True)).astype(BF16)
            outs.append(dot_nn(probs, vals).astype(BF16))
        ctx[p * pair:(p + 1) * pair, :] = jnp.concatenate(outs, axis=1)
    for p in range(rows // pair):
        part[p * pair:(p + 1) * pair, :] = dot_nn(ctx[p * pair:(p + 1) * pair, :], wo[...])


def make_layer_kernel(tok, d_model, d_ff, exp_loc, attn_dims):
    r = tok // HALVES
    m = r * NUM_DEV
    tile = 512
    units = HALVES * exp_loc

    def kernel(x_in, dy_in, xa_in, gt_in, wg_in, wu_in, wd_in, wqkv, wo,
               y_out, dx_out, attn_out, dg_out, x_all, dy_all, da_all, db_all, h_all, gates_out,
               xb, dyb, xab, gtb, gcol, wg, wu, wd, y_part, dx_part, at_part, ctx, s1, s2, d_o, dgc, dgt, stage,
               ry0, ry1, ry2, ry3, ry4, rd0, rd1, rd2, rd3, rd4, ra0, ra1, ra2, ra3, ra4,
               send_sems, recv_sems, w_sems, in_sems, out_sems, stage_sems):
        place = Place()
        pool = Pool(send_sems, recv_sems)
        dev, block = place.dev, place.block
        me = block['']

        def own_rows(buf, rows):
            return buf.at[pl.ds(pl.multiple_of(me * rows, 8), rows), :]

        loads = []
        for h in range(HALVES):
            loads.append(pltpu.make_async_copy(x_in.at[h * r:(h + 1) * r, :], own_rows(xb.at[h], r), in_sems.at[h]))
            loads.append(pltpu.make_async_copy(dy_in.at[h * r:(h + 1) * r, :], own_rows(dyb.at[h], r), in_sems.at[2 + h]))
        loads.append(pltpu.make_async_copy(xa_in, own_rows(xab, tok), in_sems.at[4]))
        for load in loads:
            load.start()
        weights = []
        for e in range(exp_loc):
            weights.append([pltpu.make_async_copy(src.at[e], dst.at[e], w_sems.at[e, k]) for k, (src, dst) in enumerate(((wg_in, wg), (wu_in, wu), (wd_in, wd)))])
        for ws in weights:
            for w in ws:
                w.start()

        barrier = pltpu.get_barrier_semaphore()
        peers = [name for name in dev if name]
        for name in peers:
            pl.semaphore_signal(barrier, inc=1, device_id=dev[name], device_id_type=MESH_ID)
        pl.semaphore_wait(barrier, len(peers))

        routes = [Link(pool, gt_in.at[block[name]], gtb.at[me], gtb.at[block[name]], dev[name]) for name in peers]
        gx = [Gather(pool, place, xb.at[h], r) for h in range(HALVES)]
        gdy = [Gather(pool, place, dyb.at[h], r) for h in range(HALVES)]
        gxa = Gather(pool, place, xab, tok)
        sy = [Scatter(pool, place, y_part.at[h], ry0.at[h], ry1.at[h], ry2.at[h], ry3.at[h], ry4.at[h], r) for h in range(HALVES)]
        sdx = [Scatter(pool, place, dx_part.at[h], rd0.at[h], rd1.at[h], rd2.at[h], rd3.at[h], rd4.at[h], r) for h in range(HALVES)]
        sat = Scatter(pool, place, at_part, ra0, ra1, ra2, ra3, ra4, tok)
        dg_links = [[Link(pool, dgt.at[h, 1 - place.core if 'c' in name else place.core], dg_out.at[me, h], dg_out.at[block[name], h], dev[name]) for name in peers] for h in range(HALVES)]

        for link in routes:
            link.start()
        gtb[me] = gt_in[me]
        for load in loads:
            load.wait()
        gx[0].begin()
        gdy[0].begin()
        gx[1].begin()
        gdy[1].begin()
        gxa.begin()
        y_part[...] = jnp.zeros_like(y_part)
        dx_part[...] = jnp.zeros_like(dx_part)
        dgc[...] = jnp.zeros_like(dgc)
        gcol[...] = jnp.zeros_like(gcol)
        for link in routes:
            link.arrive()
        wide = jnp.concatenate([gtb[...].reshape(NUM_DEV * 8, LANES), jnp.zeros((LANES - NUM_DEV * 8, LANES), F32)], axis=0).T
        for h in range(HALVES):
            for b in range(NUM_DEV):
                gcol[h, b * r:(b + 1) * r, 0:8] = wide[h * r:(h + 1) * r, b * 8:(b + 1) * 8]
        for g in (gx[0], gdy[0], gx[1], gdy[1], gxa):
            g.relay()
        for g in (gx[0], gdy[0], gx[1], gdy[1], gxa):
            g.last()
        for g in (gx[0], gdy[0], gx[1], gdy[1], gxa):
            g.finish()
        attention(xab, wqkv, wo, ctx, at_part, attn_dims)
        sat.begin()

        def staged(u, k):
            h, e = lax.div(u, exp_loc), lax.rem(u, exp_loc)
            slot = lax.rem(u, 2)
            dst = (da_all, db_all, h_all)[k].at[e, pl.ds(pl.multiple_of(h * m, 8), m), :]
            return pltpu.make_async_copy(stage.at[slot, k], dst, stage_sems.at[slot, k])

        lane = lax.broadcasted_iota(jnp.int32, (m, LANES), 1)

        def unit(u, _):
            h, e = lax.div(u, exp_loc), lax.rem(u, exp_loc)
            slot = lax.rem(u, 2)

            @pl.when(u < exp_loc)
            def _():
                for k, (src, dst) in enumerate(((wg_in, wg), (wu_in, wu), (wd_in, wd))):
                    pltpu.make_async_copy(src.at[e], dst.at[e], w_sems.at[e, k]).wait()

            @pl.when(u >= 2)
            def _():
                for k in range(3):
                    staged(u - 2, k).wait()

            @pl.when(u == 1)
            def _():
                sat.middle()

            @pl.when(u == 5)
            def _():
                sy[0].begin()
                sdx[0].begin()
                sat.late()

            @pl.when(u == 6)
            def _():
                sy[0].middle()
                sdx[0].middle()

            @pl.when(u == 8)
            def _():
                sy[0].late()
                sdx[0].late()

            gate = jnp.sum(jnp.where(lane == e, gcol[h], 0.0), axis=1, keepdims=True)
            mask = gate > 0.0
            a = jnp.where(mask, dot_nn(xb[h], wg[e]), 0.0)
            b = jnp.where(mask, dot_nn(xb[h], wu[e]), 0.0)
            sig = jax.nn.sigmoid(a)
            act = a * sig
            stage[slot, 2] = (act * b).astype(BF16)
            s1[...] = b * sig * (1.0 + a * (1.0 - sig))
            s2[...] = act
            dots = jnp.zeros((m, LANES), F32)
            for n in range(d_model // tile):
                cols = pl.ds(n * tile, tile)
                o = dot_nn(stage[slot, 2], wd[e, :, cols]).astype(BF16).astype(F32)
                dy = dyb[h, :, cols].astype(F32)
                y_part[h, :, cols] += gate * o
                prod = dy * o
                for k in range(tile // LANES):
                    dots += prod[:, k * LANES:(k + 1) * LANES]
                d_o[:, cols] = (gate * dy).astype(BF16)
            dgc[h] = jnp.where(lane == e, jnp.sum(dots, axis=1, keepdims=True), dgc[h])
            dh = dot_nt(d_o[...], wd[e]).astype(BF16).astype(F32)
            stage[slot, 0] = (dh * s1[...]).astype(BF16)
            stage[slot, 1] = (dh * s2[...]).astype(BF16)
            for k in range(3):
                staged(u, k).start()
            for n in range(d_model // tile):
                cols = pl.ds(n * tile, tile)
                dxe = dot_nt(stage[slot, 0], wg[e, cols, :]) + dot_nt(stage[slot, 1], wu[e, cols, :])
                dx_part[h, :, cols] += dxe.astype(BF16).astype(F32)
            return 0

        lax.fori_loop(0, units, unit, 0)

        sy[1].begin()
        sdx[1].begin()
        for h in range(HALVES):
            turned = dgc[h].T
            for c in range(2):
                dgt[h, c] = turned[0:8, c * LANES:(c + 1) * LANES]
        saves = [pltpu.make_async_copy(xb, x_all, out_sems.at[0]), pltpu.make_async_copy(dyb, dy_all, out_sems.at[1]), pltpu.make_async_copy(gcol, gates_out, out_sems.at[2])]
        for save in saves:
            save.start()
        for h in range(HALVES):
            for link in dg_links[h]:
                link.start()
            dg_out[me, h] = dgt[h, place.core]
        sy[1].middle()
        sdx[1].middle()
        sat.finish(attn_out)
        for s, out in ((sy[0], y_out), (sdx[0], dx_out)):
            s.finish(out.at[0:r, :])
        sy[1].late()
        sdx[1].late()
        for h in range(HALVES):
            for link in dg_links[h]:
                link.arrive()
        for s, out in ((sy[1], y_out), (sdx[1], dx_out)):
            s.finish(out.at[r:2 * r, :])
        for u in (units - 2, units - 1):
            for k in range(3):
                staged(jnp.int32(u), k).wait()
        for save in saves:
            save.wait()
        for item in gx + gdy + [gxa] + sy + sdx + [sat]:
            item.drain()
        for link in routes + dg_links[0] + dg_links[1]:
            link.sent()
        assert pool.used == NUM_LINKS

    return kernel, r, m


def weight_grads(x_ref, dy_ref, gates_ref, da_ref, db_ref, h_ref, dwg_ref, dwu_ref, dwd_ref, d_o):
    e = pl.program_id(0)
    n = pl.program_id(1)

    @pl.when(n == 0)
    def _():
        lane = lax.broadcasted_iota(jnp.int32, gates_ref.shape, 1)
        gate = jnp.sum(jnp.where(lane == e, gates_ref[...], 0.0), axis=1, keepdims=True)
        d_o[...] = (gate * dy_ref[...].astype(F32)).astype(BF16)

    width = dwg_ref.shape[0]
    cols = pl.ds(pl.multiple_of(n * width, LANES), width)
    xt = x_ref[:, cols]
    dwg_ref[...] = dot_tn(xt, da_ref[...])
    dwu_ref[...] = dot_tn(xt, db_ref[...])
    dwd_ref[...] = dot_tn(h_ref[...], d_o[:, cols])


def solution(mesh):
    num_dev = mesh.shape['ei'] * mesh.shape['eo']
    assert num_dev == NUM_DEV

    def local_step(x_tokens, expert_idx, gate_vals, dy_tokens, w_gate, w_up, w_down, x_attn, w_query, w_key, w_value, w_out):
        tok, d_model = x_tokens.shape
        top_k = expert_idx.shape[1]
        exp_loc, _, d_ff = w_gate.shape
        seq = x_attn.shape[1]
        heads, head_dim = w_query.shape[1], w_query.shape[2]
        kv_dim = w_key.shape[1] * head_dim
        q_dim = heads * head_dim
        ids = jnp.arange(NUM_DEV * exp_loc, dtype=jnp.int32).reshape(NUM_DEV, exp_loc, 1, 1)
        table = jnp.sum(jnp.where(expert_idx.T[None, None] == ids, gate_vals.T[None, None], 0.0), axis=2)
        table = jnp.pad(table, ((0, 0), (0, 8 - exp_loc), (0, LANES - tok)))
        gt = table.reshape(4, 2, 8, LANES).transpose(1, 0, 2, 3).reshape(NUM_DEV, 8, LANES)
        pad = -(q_dim + 2 * kv_dim) % LANES
        wqkv = jnp.concatenate([w_query.reshape(d_model, q_dim), w_key.reshape(d_model, kv_dim), w_value.reshape(d_model, kv_dim), jnp.zeros((d_model, pad), BF16)], axis=1)
        wo = w_out.reshape(q_dim, d_model)
        kernel, r, m = make_layer_kernel(tok, d_model, d_ff, exp_loc, (seq, kv_dim, heads, head_dim))
        any_spec = pl.BlockSpec(memory_space=pl.ANY)
        vmem_spec = pl.BlockSpec(memory_space=pltpu.VMEM)
        shape = jax.ShapeDtypeStruct
        total = tok * NUM_DEV

        def half_shapes():
            return [pltpu.VMEM((HALVES,) + s.shape, s.dtype) for s in scatter_shapes(r, d_model)]

        y, dx, attn, dgt, x_all, dy_all, da, db, hid, gates = pl.pallas_call(
            kernel,
            out_shape=(shape((tok, d_model), BF16), shape((tok, d_model), BF16), shape((tok, d_model), BF16), shape((NUM_DEV, HALVES, 8, LANES), F32),
                       shape((HALVES, m, d_model), BF16), shape((HALVES, m, d_model), BF16),
                       shape((exp_loc, total, d_ff), BF16), shape((exp_loc, total, d_ff), BF16), shape((exp_loc, total, d_ff), BF16), shape((HALVES, m, LANES), F32)),
            in_specs=[any_spec, any_spec, any_spec, vmem_spec, any_spec, any_spec, any_spec, vmem_spec, vmem_spec],
            out_specs=(vmem_spec,) * 4 + (any_spec,) * 6,
            scratch_shapes=[pltpu.VMEM((HALVES, m, d_model), BF16), pltpu.VMEM((HALVES, m, d_model), BF16), pltpu.VMEM((total, d_model), BF16),
                            pltpu.VMEM((NUM_DEV, 8, LANES), F32), pltpu.VMEM((HALVES, m, LANES), F32),
                            pltpu.VMEM((exp_loc, d_model, d_ff), BF16), pltpu.VMEM((exp_loc, d_model, d_ff), BF16), pltpu.VMEM((exp_loc, d_ff, d_model), BF16),
                            pltpu.VMEM((HALVES, m, d_model), F32), pltpu.VMEM((HALVES, m, d_model), F32), pltpu.VMEM((total, d_model), F32), pltpu.VMEM((total, q_dim), BF16),
                            pltpu.VMEM((m, d_ff), F32), pltpu.VMEM((m, d_ff), F32), pltpu.VMEM((m, d_model), BF16),
                            pltpu.VMEM((HALVES, m, LANES), F32), pltpu.VMEM((HALVES, 2, 8, LANES), F32), pltpu.VMEM((2, 3, m, d_ff), BF16)]
            + half_shapes() + half_shapes() + scatter_shapes(tok, d_model)
            + [pltpu.SemaphoreType.DMA((NUM_LINKS,)), pltpu.SemaphoreType.DMA((NUM_LINKS,)), pltpu.SemaphoreType.DMA((exp_loc, 3)),
               pltpu.SemaphoreType.DMA((5,)), pltpu.SemaphoreType.DMA((3,)), pltpu.SemaphoreType.DMA((2, 3))],
            compiler_params=pltpu.CompilerParams(collective_id=0, has_side_effects=True, vmem_limit_bytes=67000000),
            name='layer',
        )(x_tokens, dy_tokens, x_attn.reshape(tok, d_model), gt, w_gate, w_up, w_down, wqkv, wo)

        width = 512
        steps = d_model // width
        dw_gate, dw_up, dw_down = pl.pallas_call(
            weight_grads,
            grid=(exp_loc, steps),
            out_shape=(shape((exp_loc, d_model, d_ff), F32), shape((exp_loc, d_model, d_ff), F32), shape((exp_loc, d_ff, d_model), F32)),
            in_specs=[pl.BlockSpec((total, d_model), lambda e, n: (0, 0)), pl.BlockSpec((total, d_model), lambda e, n: (0, 0)), pl.BlockSpec((total, LANES), lambda e, n: (0, 0)),
                      pl.BlockSpec((None, total, d_ff), lambda e, n: (e, 0, 0)), pl.BlockSpec((None, total, d_ff), lambda e, n: (e, 0, 0)), pl.BlockSpec((None, total, d_ff), lambda e, n: (e, 0, 0))],
            out_specs=(pl.BlockSpec((None, width, d_ff), lambda e, n: (e, n, 0)), pl.BlockSpec((None, width, d_ff), lambda e, n: (e, n, 0)), pl.BlockSpec((None, d_ff, width), lambda e, n: (e, 0, n))),
            scratch_shapes=[pltpu.VMEM((total, d_model), BF16)],
            compiler_params=pltpu.CompilerParams(vmem_limit_bytes=60000000),
            cost_estimate=pl.CostEstimate(flops=3 * 2 * total * d_model * d_ff * exp_loc, bytes_accessed=3 * 4 * exp_loc * d_model * d_ff, transcendentals=0),
            name='weight_grads',
        )(x_all.reshape(total, d_model), dy_all.reshape(total, d_model), gates.reshape(total, LANES), da, db, hid)

        chip = lax.axis_index('ei') * 2 + lax.div(lax.axis_index('eo'), 2)
        mine = lax.dynamic_slice_in_dim(dgt, chip * r, r, axis=3)[:, :, :exp_loc]
        mine = mine.reshape(2, 4, HALVES, exp_loc, r).transpose(1, 0, 3, 2, 4).reshape(NUM_DEV * exp_loc, 1, tok)
        ids = jnp.arange(NUM_DEV * exp_loc, dtype=jnp.int32)[:, None, None]
        d_gates = jnp.sum(jnp.where(expert_idx.T[None] == ids, mine, 0.0), axis=0).T
        return y, dx, d_gates, dw_gate, dw_up, dw_down, attn.reshape(x_attn.shape)

    spec_rows = P(TOKEN_AXES, None)
    spec_seqs = P(TOKEN_AXES, None, None)
    spec_experts = P(GROUP_AXES, None, None)
    spec_heads = P(None, GROUP_AXES, None)
    return jax.shard_map(local_step, mesh=mesh,
                         in_specs=(spec_rows, spec_rows, spec_rows, spec_rows, spec_experts, spec_experts, spec_experts, spec_seqs, spec_heads, spec_heads, spec_heads, spec_experts),
                         out_specs=(spec_rows, spec_rows, spec_rows, spec_seqs, spec_seqs, spec_seqs, spec_seqs),
                         check_vma=False)
```

profile of v0, /device:TPU:0, one launch (start us, length us, event | category | flops | bytes accessed | tf_op | source)
XLA Modules:
  0.0 129.9 jit_solution(9394525908367246133)
XLA Ops:
  0.7 0.1 pad.8.clone
  0.7 0.8 select_reduce_fusion.1
  1.6 0.6 copy.27
  2.2 1.1 copy.28
  3.4 1.2 copy.29
  4.5 1.3 %copy.30 = bf16[1536,192]{1,0:T(8,128)(2,1)S(1)} copy(bf16[1536,192]{0,1:T(8,128)(2,1)} %bitcast.23) | data formatting | bytes 1179648 | tf_op jit(solution)/shard_map/reshape | solution.py:442
  5.9 1.5 %maximum_maximum_fusion.wqkv = bf16[1536,384]{1,0:T(8,128)(2,1)} fusion(bf16[1536,64]{1,0:T(8,128)(2,1)S(1)} %bitcast.21, bf16[1536,64]{1,0:T(8,128)(2,1)S(1)} %bitcast.20, bf16[1536,192]{1,0:T(8,128)(2,1)S(1)} %copy.30, bf16[384]{0:T(512)(128)(2,1)S(1)} %pad.8.clone), kind=kLoop, calls=%fused_computation | loop fusion | flops 4718592 | bytes 2163456 | tf_op jit(solution)/shard_map/concatenate | solution.py:442
  7.4 0.0 copy-start.3
  7.4 92.1 %layer.1 = (bf16[64,1536]{1,0:T(8,128)(2,1)}, bf16[64,1536]{1,0:T(8,128)(2,1)}, bf16[64,1536]{1,0:T(8,128)(2,1)}, f32[8,2,8,128]{3,2,1,0:T(8,128)}, bf16[2,256,1...) custom-call(bf16[64,1536]{1,0:T(8,128)(2,1)} %x_in.1, ...), custom_call_target="tpu_custom_call" | custom-call | tf_op jit(solution)/shard_map/layer/pallas_call | solution.py:453
  99.5 0.9 constant_dynamic-slice_fusion
  100.4 0.1 broadcast_in_dim.36
  100.5 0.0 copy-done.3
  100.5 0.6 select_reduce_fusion
  101.2 0.0 copy-start.2
  101.2 0.0 copy-start.1
  101.2 0.0 copy-start
  101.2 26.7 %weight_grads.1 = (f32[5,1536,512]{2,1,0:T(8,128)}, f32[5,1536,512]{2,1,0:T(8,128)}, f32[5,512,1536]{2,1,0:T(8,128)}) custom-call(bf16[512,1536]{1,0:T(8,128)(2,1)} %bitcast.34, bf16[512,1536]{1,0:T(8,128)(2,1)} %bitcast.35, f32[512,128]{1,0:T(8,128)} %bitcast.36, bf16[5,512,512]{2,1,0:T(8,128)(2,1)} %get-tuple-element.26.da_ref, ...), custom_call_target="tpu_custom_call" | custom-call | flops 12079595520 | bytes 47185920 | tf_op jit(solution)/shard_map/weight_grads/pallas_call | solution.py:475
  127.9 0.0 copy-done.2
  127.9 0.7 copy.37
  128.5 0.0 copy-done.1
  128.5 0.7 copy.38
  129.2 0.0 copy-done
  129.2 0.7 copy.39
  (4 shorter events, 0.0 us)
Async XLA Ops:
  7.4 93.2 %copy-start.3 = (s32[64,8]{0,1:T(8,128)S(1)}, s32[64,8]{0,1:T(8,128)}, u32[]{:S(2)}) copy-start(s32[64,8]{0,1:T(8,128)} %param.13) | copy-start | bytes 6148
  101.2 26.7 %copy-start.2 = (bf16[64,1536]{1,0:T(8,128)(2,1)S(1)}, bf16[64,1536]{1,0:T(8,128)(2,1)}, u32[]{:S(2)}) copy-start(bf16[64,1536]{1,0:T(8,128)(2,1)} %get-tuple-element.40) | copy-start | bytes 589828
  101.2 27.4 %copy-start.1 = (bf16[64,1536]{1,0:T(8,128)(2,1)S(1)}, bf16[64,1536]{1,0:T(8,128)(2,1)}, u32[]{:S(2)}) copy-start(bf16[64,1536]{1,0:T(8,128)(2,1)} %get-tuple-element.41) | copy-start | bytes 589828
  101.2 28.1 %copy-start = (bf16[64,1536]{1,0:T(8,128)(2,1)S(1)}, bf16[64,1536]{1,0:T(8,128)(2,1)}, u32[]{:S(2)}) copy-start(bf16[64,1536]{1,0:T(8,128)(2,1)} %get-tuple-element.32) | copy-start | bytes 589828
where the time goes:
time: 130 us
  Pallas kernels  119 us (92%)
  local copies, waits for them, and re-layouts  7.43 us (6%)
  other arithmetic  2.97 us (2%)
    pallas_call x1, Pallas kernels, local_step(): pl.pallas_call(kernel, out_shape=(shape((tok, d_model), BF16), shape((tok...  92.1 us
    pallas_call x1, Pallas kernels, local_step(): pl.pallas_call(weight_grads, grid=(exp_loc, steps), out_shape=(shape((exp...  26.7 us
    unnamed x13, local copies, waits for them, and re-layouts  4.34 us

commit v1 on v0

--- a/solution.py
+++ b/solution.py
@@ -220,8 +220,8 @@
     units = HALVES * exp_loc
 
     def kernel(x_in, dy_in, xa_in, gt_in, wg_in, wu_in, wd_in, wqkv, wo,
-               y_out, dx_out, attn_out, dg_out, x_all, dy_all, da_all, db_all, h_all, gates_out,
-               xb, dyb, xab, gtb, gcol, wg, wu, wd, y_part, dx_part, at_part, ctx, s1, s2, d_o, dgc, dgt, stage,
+               y_out, dx_out, attn_out, dg_out, xt_all, dy_all, da_all, db_all, ht_all, gates_out,
+               xb, dyb, xab, gtb, gcol, wg, wu, wd, y_part, dx_part, at_part, ctx, s1, s2, d_o, dgc, dgt, stage, hid, stage_t, xt,
                ry0, ry1, ry2, ry3, ry4, rd0, rd1, rd2, rd3, rd4, ra0, ra1, ra2, ra3, ra4,
                send_sems, recv_sems, w_sems, in_sems, out_sems, stage_sems):
         place = Place()
@@ -268,35 +268,67 @@
             load.wait()
         gx[0].begin()
         gdy[0].begin()
-        gx[1].begin()
-        gdy[1].begin()
-        gxa.begin()
         y_part[...] = jnp.zeros_like(y_part)
         dx_part[...] = jnp.zeros_like(dx_part)
         dgc[...] = jnp.zeros_like(dgc)
         gcol[...] = jnp.zeros_like(gcol)
+        gx[0].relay()
+        gx[1].begin()
+        gdy[0].relay()
+        gdy[1].begin()
         for link in routes:
             link.arrive()
         wide = jnp.concatenate([gtb[...].reshape(NUM_DEV * 8, LANES), jnp.zeros((LANES - NUM_DEV * 8, LANES), F32)], axis=0).T
         for h in range(HALVES):
             for b in range(NUM_DEV):
                 gcol[h, b * r:(b + 1) * r, 0:8] = wide[h * r:(h + 1) * r, b * 8:(b + 1) * 8]
-        for g in (gx[0], gdy[0], gx[1], gdy[1], gxa):
-            g.relay()
-        for g in (gx[0], gdy[0], gx[1], gdy[1], gxa):
-            g.last()
-        for g in (gx[0], gdy[0], gx[1], gdy[1], gxa):
-            g.finish()
-        attention(xab, wqkv, wo, ctx, at_part, attn_dims)
-        sat.begin()
+        gx[0].last()
+        gx[0].finish()
 
         def staged(u, k):
             h, e = lax.div(u, exp_loc), lax.rem(u, exp_loc)
             slot = lax.rem(u, 2)
-            dst = (da_all, db_all, h_all)[k].at[e, pl.ds(pl.multiple_of(h * m, 8), m), :]
-            return pltpu.make_async_copy(stage.at[slot, k], dst, stage_sems.at[slot, k])
+            part = pl.ds(pl.multiple_of(h * m, LANES), m)
+            if k == 2:
+                return pltpu.make_async_copy(stage_t.at[slot], ht_all.at[e, :, part], stage_sems.at[slot, k])
+            return pltpu.make_async_copy(stage.at[slot, k], (da_all, db_all)[k].at[e, part, :], stage_sems.at[slot, k])
 
         lane = lax.broadcasted_iota(jnp.int32, (m, LANES), 1)
+
+        def at1():
+            gdy[1].relay()
+
+        def at2():
+            gx[1].last()
+
+        def at3():
+            gdy[1].last()
+            gx[1].finish()
+
+        def at4():
+            gxa.relay()
+            gdy[1].finish()
+
+        def at5():
+            sy[0].begin()
+            sdx[0].begin()
+            gxa.last()
+
+        def at6():
+            sy[0].middle()
+            sdx[0].middle()
+            gxa.finish()
+
+        def at8():
+            sy[0].late()
+
+        early = {1: at1, 2: at2, 3: at3, 4: at4, 5: at5, 6: at6, 8: at8}
+
+        def mid0():
+            gdy[0].last()
+            gdy[0].finish()
+            gx[1].relay()
+            gxa.begin()
 
         def unit(u, _):
             h, e = lax.div(u, exp_loc), lax.rem(u, exp_loc)
@@ -312,25 +344,8 @@
                 for k in range(3):
                     staged(u - 2, k).wait()
 
-            @pl.when(u == 1)
-            def _():
-                sat.middle()
-
-            @pl.when(u == 5)
-            def _():
-                sy[0].begin()
-                sdx[0].begin()
-                sat.late()
-
-            @pl.when(u == 6)
-            def _():
-                sy[0].middle()
-                sdx[0].middle()
-
-            @pl.when(u == 8)
-            def _():
-                sy[0].late()
-                sdx[0].late()
+            for k, events in early.items():
+                pl.when(u == k)(events)
 
             gate = jnp.sum(jnp.where(lane == e, gcol[h], 0.0), axis=1, keepdims=True)
             mask = gate > 0.0
@@ -338,13 +353,15 @@
             b = jnp.where(mask, dot_nn(xb[h], wu[e]), 0.0)
             sig = jax.nn.sigmoid(a)
             act = a * sig
-            stage[slot, 2] = (act * b).astype(BF16)
+            hid[...] = (act * b).astype(BF16)
+            stage_t[slot] = hid[...].T
             s1[...] = b * sig * (1.0 + a * (1.0 - sig))
             s2[...] = act
+            pl.when(u == 0)(mid0)
             dots = jnp.zeros((m, LANES), F32)
             for n in range(d_model // tile):
                 cols = pl.ds(n * tile, tile)
-                o = dot_nn(stage[slot, 2], wd[e, :, cols]).astype(BF16).astype(F32)
+                o = dot_nn(hid[...], wd[e, :, cols]).astype(BF16).astype(F32)
                 dy = dyb[h, :, cols].astype(F32)
                 y_part[h, :, cols] += gate * o
                 prod = dy * o
@@ -367,29 +384,35 @@
 
         sy[1].begin()
         sdx[1].begin()
+        sdx[0].late()
+        sy[1].middle()
+        sdx[1].middle()
+        attention(xab, wqkv, wo, ctx, at_part, attn_dims)
+        sat.begin()
         for h in range(HALVES):
             turned = dgc[h].T
             for c in range(2):
                 dgt[h, c] = turned[0:8, c * LANES:(c + 1) * LANES]
-        saves = [pltpu.make_async_copy(xb, x_all, out_sems.at[0]), pltpu.make_async_copy(dyb, dy_all, out_sems.at[1]), pltpu.make_async_copy(gcol, gates_out, out_sems.at[2])]
+            xt[:, h * m:(h + 1) * m] = xb[h].T
+        saves = [pltpu.make_async_copy(xt, xt_all, out_sems.at[0]), pltpu.make_async_copy(dyb, dy_all, out_sems.at[1]), pltpu.make_async_copy(gcol, gates_out, out_sems.at[2])]
         for save in saves:
             save.start()
         for h in range(HALVES):
             for link in dg_links[h]:
                 link.start()
             dg_out[me, h] = dgt[h, place.core]
-        sy[1].middle()
-        sdx[1].middle()
-        sat.finish(attn_out)
+        sat.middle()
         for s, out in ((sy[0], y_out), (sdx[0], dx_out)):
             s.finish(out.at[0:r, :])
         sy[1].late()
         sdx[1].late()
+        sat.late()
         for h in range(HALVES):
             for link in dg_links[h]:
                 link.arrive()
         for s, out in ((sy[1], y_out), (sdx[1], dx_out)):
             s.finish(out.at[r:2 * r, :])
+        sat.finish(attn_out)
         for u in (units - 2, units - 1):
             for k in range(3):
                 staged(jnp.int32(u), k).wait()
@@ -404,22 +427,13 @@
     return kernel, r, m
 
 
-def weight_grads(x_ref, dy_ref, gates_ref, da_ref, db_ref, h_ref, dwg_ref, dwu_ref, dwd_ref, d_o):
-    e = pl.program_id(0)
-    n = pl.program_id(1)
-
-    @pl.when(n == 0)
-    def _():
-        lane = lax.broadcasted_iota(jnp.int32, gates_ref.shape, 1)
-        gate = jnp.sum(jnp.where(lane == e, gates_ref[...], 0.0), axis=1, keepdims=True)
-        d_o[...] = (gate * dy_ref[...].astype(F32)).astype(BF16)
-
-    width = dwg_ref.shape[0]
-    cols = pl.ds(pl.multiple_of(n * width, LANES), width)
-    xt = x_ref[:, cols]
-    dwg_ref[...] = dot_tn(xt, da_ref[...])
-    dwu_ref[...] = dot_tn(xt, db_ref[...])
-    dwd_ref[...] = dot_tn(h_ref[...], d_o[:, cols])
+def weight_grads(xt_ref, dy_ref, gates_ref, da_ref, db_ref, ht_ref, dwg_ref, dwu_ref, dwd_ref):
+    lane = lax.broadcasted_iota(jnp.int32, gates_ref.shape, 1)
+    gate = jnp.sum(jnp.where(lane == pl.program_id(0), gates_ref[...], 0.0), axis=1, keepdims=True)
+    d_o = (gate * dy_ref[...].astype(F32)).astype(BF16)
+    dwg_ref[...] = dot_nn(xt_ref[...], da_ref[...])
+    dwu_ref[...] = dot_nn(xt_ref[...], db_ref[...])
+    dwd_ref[...] = dot_nn(ht_ref[...], d_o)
 
 
 def solution(mesh):
@@ -450,11 +464,11 @@
         def half_shapes():
             return [pltpu.VMEM((HALVES,) + s.shape, s.dtype) for s in scatter_shapes(r, d_model)]
 
-        y, dx, attn, dgt, x_all, dy_all, da, db, hid, gates = pl.pallas_call(
+        y, dx, attn, dgt, xt, dy_all, da, db, ht, gates = pl.pallas_call(
             kernel,
             out_shape=(shape((tok, d_model), BF16), shape((tok, d_model), BF16), shape((tok, d_model), BF16), shape((NUM_DEV, HALVES, 8, LANES), F32),
-                       shape((HALVES, m, d_model), BF16), shape((HALVES, m, d_model), BF16),
-                       shape((exp_loc, total, d_ff), BF16), shape((exp_loc, total, d_ff), BF16), shape((exp_loc, total, d_ff), BF16), shape((HALVES, m, LANES), F32)),
+                       shape((d_model, total), BF16), shape((HALVES, m, d_model), BF16),
+                       shape((exp_loc, total, d_ff), BF16), shape((exp_loc, total, d_ff), BF16), shape((exp_loc, d_ff, total), BF16), shape((HALVES, m, LANES), F32)),
             in_specs=[any_spec, any_spec, any_spec, vmem_spec, any_spec, any_spec, any_spec, vmem_spec, vmem_spec],
             out_specs=(vmem_spec,) * 4 + (any_spec,) * 6,
             scratch_shapes=[pltpu.VMEM((HALVES, m, d_model), BF16), pltpu.VMEM((HALVES, m, d_model), BF16), pltpu.VMEM((total, d_model), BF16),
@@ -462,7 +476,8 @@
                             pltpu.VMEM((exp_loc, d_model, d_ff), BF16), pltpu.VMEM((exp_loc, d_model, d_ff), BF16), pltpu.VMEM((exp_loc, d_ff, d_model), BF16),
                             pltpu.VMEM((HALVES, m, d_model), F32), pltpu.VMEM((HALVES, m, d_model), F32), pltpu.VMEM((total, d_model), F32), pltpu.VMEM((total, q_dim), BF16),
                             pltpu.VMEM((m, d_ff), F32), pltpu.VMEM((m, d_ff), F32), pltpu.VMEM((m, d_model), BF16),
-                            pltpu.VMEM((HALVES, m, LANES), F32), pltpu.VMEM((HALVES, 2, 8, LANES), F32), pltpu.VMEM((2, 3, m, d_ff), BF16)]
+                            pltpu.VMEM((HALVES, m, LANES), F32), pltpu.VMEM((HALVES, 2, 8, LANES), F32), pltpu.VMEM((2, 2, m, d_ff), BF16),
+                            pltpu.VMEM((m, d_ff), BF16), pltpu.VMEM((2, d_ff, m), BF16), pltpu.VMEM((d_model, total), BF16)]
             + half_shapes() + half_shapes() + scatter_shapes(tok, d_model)
             + [pltpu.SemaphoreType.DMA((NUM_LINKS,)), pltpu.SemaphoreType.DMA((NUM_LINKS,)), pltpu.SemaphoreType.DMA((exp_loc, 3)),
                pltpu.SemaphoreType.DMA((5,)), pltpu.SemaphoreType.DMA((3,)), pltpu.SemaphoreType.DMA((2, 3))],
@@ -476,14 +491,13 @@
             weight_grads,
             grid=(exp_loc, steps),
             out_shape=(shape((exp_loc, d_model, d_ff), F32), shape((exp_loc, d_model, d_ff), F32), shape((exp_loc, d_ff, d_model), F32)),
-            in_specs=[pl.BlockSpec((total, d_model), lambda e, n: (0, 0)), pl.BlockSpec((total, d_model), lambda e, n: (0, 0)), pl.BlockSpec((total, LANES), lambda e, n: (0, 0)),
-                      pl.BlockSpec((None, total, d_ff), lambda e, n: (e, 0, 0)), pl.BlockSpec((None, total, d_ff), lambda e, n: (e, 0, 0)), pl.BlockSpec((None, total, d_ff), lambda e, n: (e, 0, 0))],
+            in_specs=[pl.BlockSpec((width, total), lambda e, n: (n, 0)), pl.BlockSpec((total, width), lambda e, n: (0, n)), pl.BlockSpec((total, LANES), lambda e, n: (0, 0)),
+                      pl.BlockSpec((None, total, d_ff), lambda e, n: (e, 0, 0)), pl.BlockSpec((None, total, d_ff), lambda e, n: (e, 0, 0)), pl.BlockSpec((None, d_ff, total), lambda e, n: (e, 0, 0))],
             out_specs=(pl.BlockSpec((None, width, d_ff), lambda e, n: (e, n, 0)), pl.BlockSpec((None, width, d_ff), lambda e, n: (e, n, 0)), pl.BlockSpec((None, d_ff, width), lambda e, n: (e, 0, n))),
-            scratch_shapes=[pltpu.VMEM((total, d_model), BF16)],
             compiler_params=pltpu.CompilerParams(vmem_limit_bytes=60000000),
             cost_estimate=pl.CostEstimate(flops=3 * 2 * total * d_model * d_ff * exp_loc, bytes_accessed=3 * 4 * exp_loc * d_model * d_ff, transcendentals=0),
             name='weight_grads',
-        )(x_all.reshape(total, d_model), dy_all.reshape(total, d_model), gates.reshape(total, LANES), da, db, hid)
+        )(xt, dy_all.reshape(total, d_model), gates.reshape(total, LANES), da, db, ht)
 
         chip = lax.axis_index('ei') * 2 + lax.div(lax.axis_index('eo'), 2)
         mine = lax.dynamic_slice_in_dim(dgt, chip * r, r, axis=3)[:, :, :exp_loc]

time: 130 us -> 131 us (level)
    pallas_call x1, Pallas kernels: 26.7 us -> 29.8 us  [local_step(): pl.pallas_call(weight_grads, grid=(exp_loc, steps), out_shape=(shape((exp...]
    pallas_call x1, Pallas kernels: 92.1 us -> 89.9 us  [local_step(): pl.pallas_call(kernel, out_shape=(shape((tok, d_model), BF16), shape((tok...]
where the time goes in v1:
time: 131 us
  Pallas kernels  120 us (92%)
  local copies, waits for them, and re-layouts  7.43 us (6%)
  other arithmetic  2.97 us (2%)
    pallas_call x1, Pallas kernels, local_step(): pl.pallas_call(kernel, out_shape=(shape((tok, d_model), BF16), shape((tok...  89.9 us
    pallas_call x1, Pallas kernels, local_step(): pl.pallas_call(weight_grads, grid=(exp_loc, steps), out_shape=(shape((exp...  29.8 us
    unnamed x13, local copies, waits for them, and re-layouts  4.34 us

profile of v1, /device:TPU:0, one launch (start us, length us, event | category | flops | bytes accessed | tf_op | source)
XLA Modules:
  0.0 130.8 jit_solution(351105543145724768)
XLA Ops:
  0.7 0.1 pad.8.clone
  0.7 0.8 select_reduce_fusion.1
  1.6 0.6 copy.27
  2.2 1.1 copy.28
  3.4 1.2 copy.29
  4.5 1.3 %copy.30 = bf16[1536,192]{1,0:T(8,128)(2,1)S(1)} copy(bf16[1536,192]{0,1:T(8,128)(2,1)} %bitcast.22) | data formatting | bytes 1179648 | tf_op jit(solution)/shard_map/reshape | solution.py:456
  5.9 1.5 %maximum_maximum_fusion.wqkv = bf16[1536,384]{1,0:T(8,128)(2,1)} fusion(bf16[1536,64]{1,0:T(8,128)(2,1)S(1)} %bitcast.20, bf16[1536,64]{1,0:T(8,128)(2,1)S(1)} %bitcast.19, bf16[1536,192]{1,0:T(8,128)(2,1)S(1)} %copy.30, bf16[384]{0:T(512)(128)(2,1)S(1)} %pad.8.clone), kind=kLoop, calls=%fused_computation | loop fusion | flops 4718592 | bytes 2163456 | tf_op jit(solution)/shard_map/concatenate | solution.py:456
  7.4 0.0 copy-start.3
  7.4 89.9 %layer.1 = (bf16[64,1536]{1,0:T(8,128)(2,1)}, bf16[64,1536]{1,0:T(8,128)(2,1)}, bf16[64,1536]{1,0:T(8,128)(2,1)}, f32[8,2,8,128]{3,2,1,0:T(8,128)}, bf16[1536,51...) custom-call(bf16[64,1536]{1,0:T(8,128)(2,1)} %x_in.1, ...), custom_call_target="tpu_custom_call" | custom-call | tf_op jit(solution)/shard_map/layer/pallas_call | solution.py:467
  97.3 0.9 constant_dynamic-slice_fusion
  98.2 0.1 broadcast_in_dim.36
  98.3 0.0 copy-done.3
  98.3 0.6 select_reduce_fusion
  99.0 0.0 copy-start.2
  99.0 0.0 copy-start.1
  99.0 0.0 copy-start
  99.0 29.8 %weight_grads.1 = (f32[5,1536,512]{2,1,0:T(8,128)}, f32[5,1536,512]{2,1,0:T(8,128)}, f32[5,512,1536]{2,1,0:T(8,128)}) custom-call(bf16[1536,512]{1,0:T(8,128)(2,1)} %get-tuple-element.23.xt_ref, bf16[512,1536]{1,0:T(8,128)(2,1)} %bitcast.33, f32[512,128]{1,0:T(8,128)} %bitcast.34, bf16[5,512,512]{2,1,0:T(8,128)(2,1)} %get-tuple-element.26.da_ref, ...), custom_call_target="tpu_custom_call" | custom-call | flops 12079595520 | bytes 47185920 | tf_op jit(solution)/shard_map/weight_grads/pallas_call | solution.py:490
  128.8 0.0 copy-done.2
  128.8 0.7 copy.37
  129.5 0.0 copy-done.1
  129.5 0.7 copy.38
  130.1 0.0 copy-done
  130.1 0.7 copy.39
  (4 shorter events, 0.0 us)
Async XLA Ops:
  7.4 91.0 %copy-start.3 = (s32[64,8]{0,1:T(8,128)S(1)}, s32[64,8]{0,1:T(8,128)}, u32[]{:S(2)}) copy-start(s32[64,8]{0,1:T(8,128)} %param.13) | copy-start | bytes 6148
  99.0 29.8 %copy-start.2 = (bf16[64,1536]{1,0:T(8,128)(2,1)S(1)}, bf16[64,1536]{1,0:T(8,128)(2,1)}, u32[]{:S(2)}) copy-start(bf16[64,1536]{1,0:T(8,128)(2,1)} %get-tuple-element.40) | copy-start | bytes 589828
  99.0 30.5 %copy-start.1 = (bf16[64,1536]{1,0:T(8,128)(2,1)S(1)}, bf16[64,1536]{1,0:T(8,128)(2,1)}, u32[]{:S(2)}) copy-start(bf16[64,1536]{1,0:T(8,128)(2,1)} %get-tuple-element.41) | copy-start | bytes 589828
  99.0 31.2 %copy-start = (bf16[64,1536]{1,0:T(8,128)(2,1)S(1)}, bf16[64,1536]{1,0:T(8,128)(2,1)}, u32[]{:S(2)}) copy-start(bf16[64,1536]{1,0:T(8,128)(2,1)} %get-tuple-element.32) | copy-start | bytes 589828

commit v2 on v1

--- a/solution.py
+++ b/solution.py
@@ -1,3 +1,5 @@
+import functools
+
 import jax
 import jax.numpy as jnp
 from jax import lax
@@ -37,6 +39,7 @@
         self.chip = i * 2 + x
         self.dev = {}
         self.block = {}
+        self.flat = {}
         for flip_y in (0, 1):
             for flip_x in (0, 1):
                 for flip_c in (0, 1):
@@ -46,7 +49,7 @@
                     name = ('y' if flip_y else '') + ('x' if flip_x else '') + ('c' if flip_c else '')
                     self.dev[name] = (0, yy, xx * 2 + cc)
                     self.block[name] = cc * 4 + yy * 2 + xx
-        self.chips = {'': self.chip, 'x': i * 2 + 1 - x, 'y': (1 - i) * 2 + x, 'yx': (1 - i) * 2 + 1 - x}
+                    self.flat[name] = yy * 4 + xx * 2 + cc
 
 
 class Link:
@@ -188,29 +191,26 @@
 NUM_LINKS = 7 + 14 + 8 * 5 + 7 * 5
 
 
-def attention(xa, wqkv, wo, ctx, part, dims):
+def attention_pair(xa, wqkv, wo, part, first, dims):
     seq, kv_dim, heads, head_dim = dims
     q_dim = heads * head_dim
-    rows = xa.shape[0]
     pair = 2 * seq
+    rows = pl.ds(pl.multiple_of(first, pair), pair)
     row = lax.broadcasted_iota(jnp.int32, (pair, pair), 0)
     col = lax.broadcasted_iota(jnp.int32, (pair, pair), 1)
     causal = (row >= col) & ((row >= seq) == (col >= seq))
-    for p in range(rows // pair):
-        qkv = dot_nn(xa[p * pair:(p + 1) * pair, :], wqkv[...]).astype(BF16)
-        keys = qkv[:, q_dim:q_dim + kv_dim]
-        vals = qkv[:, q_dim + kv_dim:q_dim + 2 * kv_dim]
-        outs = []
-        for h in range(heads):
-            scores = dot_nt(qkv[:, h * head_dim:(h + 1) * head_dim], keys) * head_dim ** -0.5
-            scores = jnp.where(causal, scores, -1e30)
-            top = jnp.max(scores, axis=1, keepdims=True)
-            ex = jnp.exp(scores - top)
-            probs = (ex / jnp.sum(ex, axis=1, keepdims=True)).astype(BF16)
-            outs.append(dot_nn(probs, vals).astype(BF16))
-        ctx[p * pair:(p + 1) * pair, :] = jnp.concatenate(outs, axis=1)
-    for p in range(rows // pair):
-        part[p * pair:(p + 1) * pair, :] = dot_nn(ctx[p * pair:(p + 1) * pair, :], wo[...])
+    qkv = dot_nt(xa[rows, :], wqkv[...]).astype(BF16)
+    keys = qkv[:, q_dim:q_dim + kv_dim]
+    vals = qkv[:, q_dim + kv_dim:q_dim + 2 * kv_dim]
+    outs = []
+    for h in range(heads):
+        scores = dot_nt(qkv[:, h * head_dim:(h + 1) * head_dim], keys) * head_dim ** -0.5
+        scores = jnp.where(causal, scores, -1e30)
+        top = jnp.max(scores, axis=1, keepdims=True)
+        ex = jnp.exp(scores - top)
+        probs = (ex / jnp.sum(ex, axis=1, keepdims=True)).astype(BF16)
+        outs.append(dot_nn(probs, vals).astype(BF16))
+    part[rows, :] = dot_nn(jnp.concatenate(outs, axis=1), wo[...])
 
 
 def make_layer_kernel(tok, d_model, d_ff, exp_loc, attn_dims):
@@ -219,11 +219,11 @@
     tile = 512
     units = HALVES * exp_loc
 
-    def kernel(x_in, dy_in, xa_in, gt_in, wg_in, wu_in, wd_in, wqkv, wo,
+    def kernel(x_in, dy_in, xa_in, gt_in, idx_in, wg_in, wu_in, wd_in, wq_in, wk_in, wv_in, wo_in,
                y_out, dx_out, attn_out, dg_out, xt_all, dy_all, da_all, db_all, ht_all, gates_out,
-               xb, dyb, xab, gtb, gcol, wg, wu, wd, y_part, dx_part, at_part, ctx, s1, s2, d_o, dgc, dgt, stage, hid, stage_t, xt,
+               xb, dyb, xab, gtb, gcol, wg, wu, wd, y_part, dx_part, at_part, wqkv, wo, s1, s2, d_o, dgc, dgt, stage, hid, stage_t, xt, dgl,
                ry0, ry1, ry2, ry3, ry4, rd0, rd1, rd2, rd3, rd4, ra0, ra1, ra2, ra3, ra4,
-               send_sems, recv_sems, w_sems, in_sems, out_sems, stage_sems):
+               send_sems, recv_sems, w_sems, in_sems, aw_sems, out_sems, stage_sems):
         place = Place()
         pool = Pool(send_sems, recv_sems)
         dev, block = place.dev, place.block
@@ -239,6 +239,11 @@
         loads.append(pltpu.make_async_copy(xa_in, own_rows(xab, tok), in_sems.at[4]))
         for load in loads:
             load.start()
+        q_dim, kv_dim = wq_in.shape[0], wk_in.shape[0]
+        attn_loads = [pltpu.make_async_copy(wq_in, wqkv.at[0:q_dim, :], aw_sems.at[0]), pltpu.make_async_copy(wk_in, wqkv.at[q_dim:q_dim + kv_dim, :], aw_sems.at[1]),
+                      pltpu.make_async_copy(wv_in, wqkv.at[q_dim + kv_dim:q_dim + 2 * kv_dim, :], aw_sems.at[2]), pltpu.make_async_copy(wo_in, wo, aw_sems.at[3])]
+        for load in attn_loads:
+            load.start()
         weights = []
         for e in range(exp_loc):
             weights.append([pltpu.make_async_copy(src.at[e], dst.at[e], w_sems.at[e, k]) for k, (src, dst) in enumerate(((wg_in, wg), (wu_in, wu), (wd_in, wd)))])
@@ -252,37 +257,55 @@
             pl.semaphore_signal(barrier, inc=1, device_id=dev[name], device_id_type=MESH_ID)
         pl.semaphore_wait(barrier, len(peers))
 
-        routes = [Link(pool, gt_in.at[block[name]], gtb.at[me], gtb.at[block[name]], dev[name]) for name in peers]
+        routes = [Link(pool, gt_in.at[place.flat[name]], gtb.at[me], gtb.at[block[name]], dev[name]) for name in peers]
         gx = [Gather(pool, place, xb.at[h], r) for h in range(HALVES)]
         gdy = [Gather(pool, place, dyb.at[h], r) for h in range(HALVES)]
         gxa = Gather(pool, place, xab, tok)
         sy = [Scatter(pool, place, y_part.at[h], ry0.at[h], ry1.at[h], ry2.at[h], ry3.at[h], ry4.at[h], r) for h in range(HALVES)]
         sdx = [Scatter(pool, place, dx_part.at[h], rd0.at[h], rd1.at[h], rd2.at[h], rd3.at[h], rd4.at[h], r) for h in range(HALVES)]
         sat = Scatter(pool, place, at_part, ra0, ra1, ra2, ra3, ra4, tok)
-        dg_links = [[Link(pool, dgt.at[h, 1 - place.core if 'c' in name else place.core], dg_out.at[me, h], dg_out.at[block[name], h], dev[name]) for name in peers] for h in range(HALVES)]
+        dg_links = [[Link(pool, dgt.at[h, 1 - place.core if 'c' in name else place.core], dgl.at[me, h], dgl.at[block[name], h], dev[name]) for name in peers] for h in range(HALVES)]
 
         for link in routes:
             link.start()
-        gtb[me] = gt_in[me]
+        gtb[me] = gt_in[place.flat['']]
         for load in loads:
             load.wait()
+        gxa.begin()
         gx[0].begin()
         gdy[0].begin()
+        dgc[...] = jnp.zeros_like(dgc)
+        gcol[...] = jnp.zeros_like(gcol)
         y_part[...] = jnp.zeros_like(y_part)
         dx_part[...] = jnp.zeros_like(dx_part)
-        dgc[...] = jnp.zeros_like(dgc)
-        gcol[...] = jnp.zeros_like(gcol)
+        for load in attn_loads:
+            load.wait()
+
+        def pair(name):
+            attention_pair(xab, wqkv, wo, at_part, lax.div(block[name], 2) * (2 * tok), attn_dims)
+
+        gxa.relay()
+        pair('')
         gx[0].relay()
+        gxa.to_c.arrive()
+        gxa.core_x.arrive()
+        pair('c')
+        gdy[0].relay()
         gx[1].begin()
-        gdy[0].relay()
         gdy[1].begin()
+        gxa.last()
+        pair('y')
+        gx[0].last()
+        gxa.core_y.arrive()
+        gxa.core_d.arrive()
+        pair('yc')
+        sat.begin()
         for link in routes:
             link.arrive()
         wide = jnp.concatenate([gtb[...].reshape(NUM_DEV * 8, LANES), jnp.zeros((LANES - NUM_DEV * 8, LANES), F32)], axis=0).T
         for h in range(HALVES):
             for b in range(NUM_DEV):
                 gcol[h, b * r:(b + 1) * r, 0:8] = wide[h * r:(h + 1) * r, b * 8:(b + 1) * 8]
-        gx[0].last()
         gx[0].finish()
 
         def staged(u, k):
@@ -295,9 +318,6 @@
 
         lane = lax.broadcasted_iota(jnp.int32, (m, LANES), 1)
 
-        def at1():
-            gdy[1].relay()
-
         def at2():
             gx[1].last()
 
@@ -306,29 +326,30 @@
             gx[1].finish()
 
         def at4():
-            gxa.relay()
             gdy[1].finish()
 
         def at5():
             sy[0].begin()
             sdx[0].begin()
-            gxa.last()
 
         def at6():
             sy[0].middle()
             sdx[0].middle()
-            gxa.finish()
 
         def at8():
-            sy[0].late()
-
-        early = {1: at1, 2: at2, 3: at3, 4: at4, 5: at5, 6: at6, 8: at8}
+            sat.finish(attn_out)
+
+        early = {1: gx[1].relay, 2: at2, 3: at3, 4: at4, 5: at5, 6: at6, 8: at8}
 
         def mid0():
             gdy[0].last()
             gdy[0].finish()
-            gx[1].relay()
-            gxa.begin()
+
+        def mid1():
+            gdy[1].relay()
+            sat.middle()
+
+        mid = {0: mid0, 1: mid1, 5: sat.late, 9: sy[0].late}
 
         def unit(u, _):
             h, e = lax.div(u, exp_loc), lax.rem(u, exp_loc)
@@ -357,7 +378,8 @@
             stage_t[slot] = hid[...].T
             s1[...] = b * sig * (1.0 + a * (1.0 - sig))
             s2[...] = act
-            pl.when(u == 0)(mid0)
+            for k, events in mid.items():
+                pl.when(u == k)(events)
             dots = jnp.zeros((m, LANES), F32)
             for n in range(d_model // tile):
                 cols = pl.ds(n * tile, tile)
@@ -384,35 +406,42 @@
 
         sy[1].begin()
         sdx[1].begin()
-        sdx[0].late()
-        sy[1].middle()
-        sdx[1].middle()
-        attention(xab, wqkv, wo, ctx, at_part, attn_dims)
-        sat.begin()
         for h in range(HALVES):
             turned = dgc[h].T
             for c in range(2):
                 dgt[h, c] = turned[0:8, c * LANES:(c + 1) * LANES]
+        sdx[0].late()
+        sy[1].middle()
+        sdx[1].middle()
+        for h in range(HALVES):
+            for link in dg_links[h]:
+                link.start()
+            dgl[me, h] = dgt[h, place.core]
             xt[:, h * m:(h + 1) * m] = xb[h].T
         saves = [pltpu.make_async_copy(xt, xt_all, out_sems.at[0]), pltpu.make_async_copy(dyb, dy_all, out_sems.at[1]), pltpu.make_async_copy(gcol, gates_out, out_sems.at[2])]
         for save in saves:
             save.start()
-        for h in range(HALVES):
-            for link in dg_links[h]:
-                link.start()
-            dg_out[me, h] = dgt[h, place.core]
-        sat.middle()
         for s, out in ((sy[0], y_out), (sdx[0], dx_out)):
             s.finish(out.at[0:r, :])
-        sy[1].late()
-        sdx[1].late()
-        sat.late()
         for h in range(HALVES):
             for link in dg_links[h]:
                 link.arrive()
+        for h in range(HALVES):
+            slots = idx_in[:, h * r:(h + 1) * r]
+            total = jnp.zeros(slots.shape, F32)
+            for b in range(NUM_DEV):
+                first = ((b // 2) % 2 * 4 + b % 2 * 2 + b // 4) * exp_loc
+                rows = dgl[b, h]
+                mine = jnp.zeros((8, r), F32)
+                for q in range(LANES // r):
+                    mine = jnp.where(place.chip == q, rows[:, q * r:(q + 1) * r], mine)
+                for e in range(exp_loc):
+                    total = jnp.where(slots == first + e, mine[e:e + 1, :], total)
+            dg_out[:, h * r:(h + 1) * r] = total
+        sy[1].late()
+        sdx[1].late()
         for s, out in ((sy[1], y_out), (sdx[1], dx_out)):
             s.finish(out.at[r:2 * r, :])
-        sat.finish(attn_out)
         for u in (units - 2, units - 1):
             for k in range(3):
                 staged(jnp.int32(u), k).wait()
@@ -427,13 +456,105 @@
     return kernel, r, m
 
 
-def weight_grads(xt_ref, dy_ref, gates_ref, da_ref, db_ref, ht_ref, dwg_ref, dwu_ref, dwd_ref):
-    lane = lax.broadcasted_iota(jnp.int32, gates_ref.shape, 1)
-    gate = jnp.sum(jnp.where(lane == pl.program_id(0), gates_ref[...], 0.0), axis=1, keepdims=True)
-    d_o = (gate * dy_ref[...].astype(F32)).astype(BF16)
-    dwg_ref[...] = dot_nn(xt_ref[...], da_ref[...])
-    dwu_ref[...] = dot_nn(xt_ref[...], db_ref[...])
-    dwd_ref[...] = dot_nn(ht_ref[...], d_o)
+def weight_grads(width, slots, xt_in, dy_in, g_in, da_in, db_in, ht_in, y_in, dx_in, at_in, dg_in,
+                 dwg, dwu, dwd, y_out, dx_out, at_out, dg_out,
+                 xt, dy, g, da, db, ht, sg, su, sd, y, dx, at, dg, x_sems, d_sems, g_sem, e_sems, o_sems, p_sems):
+    exp_loc = da.shape[0]
+    steps = dy.shape[1] // width
+
+    def load(e, k):
+        src, dst = ((da_in, da), (db_in, db), (ht_in, ht))[k]
+        return pltpu.make_async_copy(src.at[e], dst.at[e], e_sems.at[e, k])
+
+    def x_load(n):
+        rows = slice(n * width, (n + 1) * width)
+        return pltpu.make_async_copy(xt_in.at[rows, :], xt.at[rows, :], x_sems.at[n])
+
+    def dy_load(n):
+        cols = slice(n * width, (n + 1) * width)
+        return pltpu.make_async_copy(dy_in.at[:, cols], dy.at[:, cols], d_sems.at[n])
+
+    g_load = pltpu.make_async_copy(g_in, g, g_sem)
+    for copy in (x_load(0), load(0, 0), load(0, 1), load(0, 2), dy_load(0), g_load):
+        copy.start()
+    for n in range(1, steps):
+        x_load(n).start()
+        dy_load(n).start()
+    for e in range(1, exp_loc):
+        for k in range(3):
+            load(e, k).start()
+    passing = ((y_in, y, y_out), (dx_in, dx, dx_out), (at_in, at, at_out), (dg_in, dg, dg_out))
+    take = [pltpu.make_async_copy(src, mid, p_sems.at[k, 0]) for k, (src, mid, _) in enumerate(passing)]
+    give = [pltpu.make_async_copy(mid, dst, p_sems.at[k, 1]) for k, (_, mid, dst) in enumerate(passing)]
+    for copy in take:
+        copy.start()
+
+    def store(s, k):
+        e, n = lax.div(s, steps), lax.rem(s, steps)
+        slot = lax.rem(s, slots)
+        part = pl.ds(pl.multiple_of(n * width, LANES), width)
+        if k == 2:
+            return pltpu.make_async_copy(sd.at[slot], dwd.at[e, :, part], o_sems.at[slot, k])
+        return pltpu.make_async_copy((sg, su)[k].at[slot], (dwg, dwu)[k].at[e, part, :], o_sems.at[slot, k])
+
+    lane = lax.broadcasted_iota(jnp.int32, g.shape, 1)
+
+    def step(s, _):
+        e, n = lax.div(s, steps), lax.rem(s, steps)
+        slot = lax.rem(s, slots)
+        for k in range(steps):
+            @pl.when(s == k)
+            def _():
+                x_load(k).wait()
+
+        @pl.when(n == 0)
+        def _():
+            load(e, 0).wait()
+            load(e, 1).wait()
+
+        @pl.when(s >= slots)
+        def _():
+            for k in range(3):
+                store(s - slots, k).wait()
+
+        part = pl.ds(pl.multiple_of(n * width, LANES), width)
+        sg[slot] = dot_nn(xt[part, :], da[e])
+        store(s, 0).start()
+        su[slot] = dot_nn(xt[part, :], db[e])
+        store(s, 1).start()
+
+        @pl.when(n == 0)
+        def _():
+            load(e, 2).wait()
+
+        @pl.when(s == 0)
+        def _():
+            g_load.wait()
+
+        @pl.when(s == 3)
+        def _():
+            for copy in take:
+                copy.wait()
+            for copy in give:
+                copy.start()
+
+        for k in range(steps):
+            @pl.when(s == k)
+            def _():
+                dy_load(k).wait()
+
+        gate = jnp.sum(jnp.where(lane == e, g[...], 0.0), axis=1, keepdims=True)
+        d_o = (gate * dy[:, part].astype(F32)).astype(BF16)
+        sd[slot] = dot_nn(ht[e], d_o)
+        store(s, 2).start()
+        return 0
+
+    lax.fori_loop(0, exp_loc * steps, step, 0)
+    for s in range(exp_loc * steps - slots, exp_loc * steps):
+        for k in range(3):
+            store(jnp.int32(s), k).wait()
+    for copy in give:
+        copy.wait()
 
 
 def solution(mesh):
@@ -451,9 +572,9 @@
         ids = jnp.arange(NUM_DEV * exp_loc, dtype=jnp.int32).reshape(NUM_DEV, exp_loc, 1, 1)
         table = jnp.sum(jnp.where(expert_idx.T[None, None] == ids, gate_vals.T[None, None], 0.0), axis=2)
         table = jnp.pad(table, ((0, 0), (0, 8 - exp_loc), (0, LANES - tok)))
-        gt = table.reshape(4, 2, 8, LANES).transpose(1, 0, 2, 3).reshape(NUM_DEV, 8, LANES)
-        pad = -(q_dim + 2 * kv_dim) % LANES
-        wqkv = jnp.concatenate([w_query.reshape(d_model, q_dim), w_key.reshape(d_model, kv_dim), w_value.reshape(d_model, kv_dim), jnp.zeros((d_model, pad), BF16)], axis=1)
+        wq = w_query.transpose(1, 2, 0).reshape(q_dim, d_model)
+        wk = w_key.transpose(1, 2, 0).reshape(kv_dim, d_model)
+        wv = w_value.transpose(1, 2, 0).reshape(kv_dim, d_model)
         wo = w_out.reshape(q_dim, d_model)
         kernel, r, m = make_layer_kernel(tok, d_model, d_ff, exp_loc, (seq, kv_dim, heads, head_dim))
         any_spec = pl.BlockSpec(memory_space=pl.ANY)
@@ -466,45 +587,43 @@
 
         y, dx, attn, dgt, xt, dy_all, da, db, ht, gates = pl.pallas_call(
             kernel,
-            out_shape=(shape((tok, d_model), BF16), shape((tok, d_model), BF16), shape((tok, d_model), BF16), shape((NUM_DEV, HALVES, 8, LANES), F32),
+            out_shape=(shape((tok, d_model), BF16), shape((tok, d_model), BF16), shape((tok, d_model), BF16), shape((top_k, tok), F32),
                        shape((d_model, total), BF16), shape((HALVES, m, d_model), BF16),
                        shape((exp_loc, total, d_ff), BF16), shape((exp_loc, total, d_ff), BF16), shape((exp_loc, d_ff, total), BF16), shape((HALVES, m, LANES), F32)),
-            in_specs=[any_spec, any_spec, any_spec, vmem_spec, any_spec, any_spec, any_spec, vmem_spec, vmem_spec],
+            in_specs=[any_spec, any_spec, any_spec, vmem_spec, vmem_spec] + [any_spec] * 7,
             out_specs=(vmem_spec,) * 4 + (any_spec,) * 6,
             scratch_shapes=[pltpu.VMEM((HALVES, m, d_model), BF16), pltpu.VMEM((HALVES, m, d_model), BF16), pltpu.VMEM((total, d_model), BF16),
                             pltpu.VMEM((NUM_DEV, 8, LANES), F32), pltpu.VMEM((HALVES, m, LANES), F32),
                             pltpu.VMEM((exp_loc, d_model, d_ff), BF16), pltpu.VMEM((exp_loc, d_model, d_ff), BF16), pltpu.VMEM((exp_loc, d_ff, d_model), BF16),
-                            pltpu.VMEM((HALVES, m, d_model), F32), pltpu.VMEM((HALVES, m, d_model), F32), pltpu.VMEM((total, d_model), F32), pltpu.VMEM((total, q_dim), BF16),
+                            pltpu.VMEM((HALVES, m, d_model), F32), pltpu.VMEM((HALVES, m, d_model), F32), pltpu.VMEM((total, d_model), F32), pltpu.VMEM((q_dim + 2 * kv_dim, d_model), BF16), pltpu.VMEM((q_dim, d_model), BF16),
                             pltpu.VMEM((m, d_ff), F32), pltpu.VMEM((m, d_ff), F32), pltpu.VMEM((m, d_model), BF16),
                             pltpu.VMEM((HALVES, m, LANES), F32), pltpu.VMEM((HALVES, 2, 8, LANES), F32), pltpu.VMEM((2, 2, m, d_ff), BF16),
-                            pltpu.VMEM((m, d_ff), BF16), pltpu.VMEM((2, d_ff, m), BF16), pltpu.VMEM((d_model, total), BF16)]
+                            pltpu.VMEM((m, d_ff), BF16), pltpu.VMEM((2, d_ff, m), BF16), pltpu.VMEM((d_model, total), BF16), pltpu.VMEM((NUM_DEV, HALVES, 8, LANES), F32)]
             + half_shapes() + half_shapes() + scatter_shapes(tok, d_model)
             + [pltpu.SemaphoreType.DMA((NUM_LINKS,)), pltpu.SemaphoreType.DMA((NUM_LINKS,)), pltpu.SemaphoreType.DMA((exp_loc, 3)),
-               pltpu.SemaphoreType.DMA((5,)), pltpu.SemaphoreType.DMA((3,)), pltpu.SemaphoreType.DMA((2, 3))],
+               pltpu.SemaphoreType.DMA((5,)), pltpu.SemaphoreType.DMA((4,)), pltpu.SemaphoreType.DMA((3,)), pltpu.SemaphoreType.DMA((2, 3))],
             compiler_params=pltpu.CompilerParams(collective_id=0, has_side_effects=True, vmem_limit_bytes=67000000),
             name='layer',
-        )(x_tokens, dy_tokens, x_attn.reshape(tok, d_model), gt, w_gate, w_up, w_down, wqkv, wo)
-
-        width = 512
+        )(x_tokens, dy_tokens, x_attn.reshape(tok, d_model), table, expert_idx.T, w_gate, w_up, w_down, wq, wk, wv, wo)
+
+        width, slots = 512, 4
         steps = d_model // width
-        dw_gate, dw_up, dw_down = pl.pallas_call(
-            weight_grads,
-            grid=(exp_loc, steps),
-            out_shape=(shape((exp_loc, d_model, d_ff), F32), shape((exp_loc, d_model, d_ff), F32), shape((exp_loc, d_ff, d_model), F32)),
-            in_specs=[pl.BlockSpec((width, total), lambda e, n: (n, 0)), pl.BlockSpec((total, width), lambda e, n: (0, n)), pl.BlockSpec((total, LANES), lambda e, n: (0, 0)),
-                      pl.BlockSpec((None, total, d_ff), lambda e, n: (e, 0, 0)), pl.BlockSpec((None, total, d_ff), lambda e, n: (e, 0, 0)), pl.BlockSpec((None, d_ff, total), lambda e, n: (e, 0, 0))],
-            out_specs=(pl.BlockSpec((None, width, d_ff), lambda e, n: (e, n, 0)), pl.BlockSpec((None, width, d_ff), lambda e, n: (e, n, 0)), pl.BlockSpec((None, d_ff, width), lambda e, n: (e, 0, n))),
-            compiler_params=pltpu.CompilerParams(vmem_limit_bytes=60000000),
-            cost_estimate=pl.CostEstimate(flops=3 * 2 * total * d_model * d_ff * exp_loc, bytes_accessed=3 * 4 * exp_loc * d_model * d_ff, transcendentals=0),
+        small = (y, dx, attn, dgt)
+        dw_gate, dw_up, dw_down, y, dx, attn, dgt = pl.pallas_call(
+            functools.partial(weight_grads, width, slots),
+            out_shape=(shape((exp_loc, d_model, d_ff), F32), shape((exp_loc, d_model, d_ff), F32), shape((exp_loc, d_ff, d_model), F32)) + tuple(shape(v.shape, v.dtype) for v in small),
+            in_specs=[any_spec] * 10,
+            out_specs=(any_spec,) * 7,
+            scratch_shapes=[pltpu.VMEM((d_model, total), BF16), pltpu.VMEM((total, d_model), BF16), pltpu.VMEM((total, LANES), F32),
+                            pltpu.VMEM((exp_loc, total, d_ff), BF16), pltpu.VMEM((exp_loc, total, d_ff), BF16), pltpu.VMEM((exp_loc, d_ff, total), BF16),
+                            pltpu.VMEM((slots, width, d_ff), F32), pltpu.VMEM((slots, width, d_ff), F32), pltpu.VMEM((slots, d_ff, width), F32)]
+            + [pltpu.VMEM(v.shape, v.dtype) for v in small]
+            + [pltpu.SemaphoreType.DMA((steps,)), pltpu.SemaphoreType.DMA((steps,)), pltpu.SemaphoreType.DMA(()), pltpu.SemaphoreType.DMA((exp_loc, 3)),
+               pltpu.SemaphoreType.DMA((slots, 3)), pltpu.SemaphoreType.DMA((4, 2))],
+            compiler_params=pltpu.CompilerParams(vmem_limit_bytes=66000000),
             name='weight_grads',
-        )(xt, dy_all.reshape(total, d_model), gates.reshape(total, LANES), da, db, ht)
-
-        chip = lax.axis_index('ei') * 2 + lax.div(lax.axis_index('eo'), 2)
-        mine = lax.dynamic_slice_in_dim(dgt, chip * r, r, axis=3)[:, :, :exp_loc]
-        mine = mine.reshape(2, 4, HALVES, exp_loc, r).transpose(1, 0, 3, 2, 4).reshape(NUM_DEV * exp_loc, 1, tok)
-        ids = jnp.arange(NUM_DEV * exp_loc, dtype=jnp.int32)[:, None, None]
-        d_gates = jnp.sum(jnp.where(expert_idx.T[None] == ids, mine, 0.0), axis=0).T
-        return y, dx, d_gates, dw_gate, dw_up, dw_down, attn.reshape(x_attn.shape)
+        )(xt, dy_all.reshape(total, d_model), gates.reshape(total, LANES), da, db, ht, y, dx, attn, dgt)
+        return y, dx, dgt.T, dw_gate, dw_up, dw_down, attn.reshape(x_attn.shape)
 
     spec_rows = P(TOKEN_AXES, None)
     spec_seqs = P(TOKEN_AXES, None, None)

time: 131 us -> 113 us (0.86)
  Pallas kernels: 120 us -> 110 us
  local copies, waits for them, and re-layouts: 7.43 us -> 0.62 us
  other arithmetic: 2.97 us -> 0.84 us
    pallas_call x1, Pallas kernels: 29.8 us -> 23.2 us  [local_step(): pl.pallas_call(functools.partial(weight_grads, width, slots), out_shape=(...]
    unnamed x13 -> x0, local copies, waits for them, and re-layouts: 4.34 us -> none
    pallas_call x1, Pallas kernels: 89.9 us -> 87.1 us  [local_step(): pl.pallas_call(kernel, out_shape=(shape((tok, d_model), BF16), shape((tok...]
    concatenate x1 -> x0, other arithmetic: 1.5 us -> none  [local_step(): jnp.concatenate([w_query.reshape(d_model, q_dim), w_key.reshape(d_model,...]
    reshape x2 -> x0, local copies, waits for them, and re-layouts: 1.36 us -> none  [the longest x1 1.34 us: local_step(): w_query.reshape(d_model, q_dim)]
where the time goes in v2:
time: 113 us; the launch traced here: 112 us
  Pallas kernels  110 us (97%)
    pallas_call x1, Pallas kernels, local_step(): pl.pallas_call(kernel, out_shape=(shape((tok, d_model), BF16), shape((tok...  87.1 us
    pallas_call x1, Pallas kernels, local_step(): pl.pallas_call(functools.partial(weight_grads, width, slots), out_shape=(...  23.2 us

profile of v2, /device:TPU:0, one launch (start us, length us, event | category | flops | bytes accessed | tf_op | source)
XLA Modules:
  0.0 112.4 jit_solution(16803763722899367056)
XLA Ops:
  0.6 0.8 select_reduce_fusion
  1.5 0.6 pad.4.gt_in
  2.1 87.1 %layer.1 = (bf16[64,1536]{1,0:T(8,128)(2,1)}, bf16[64,1536]{1,0:T(8,128)(2,1)}, bf16[64,1536]{1,0:T(8,128)(2,1)}, f32[8,64]{1,0:T(8,128)}, bf16[1536,512]{1,0:T(...) custom-call(bf16[64,1536]{1,0:T(8,128)(2,1)} %x_in.1, ...), custom_call_target="tpu_custom_call" | custom-call | tf_op jit(solution)/shard_map/layer/pallas_call | solution.py:588
  89.2 23.2 %weight_grads.1 = (f32[5,1536,512]{2,1,0:T(8,128)}, f32[5,1536,512]{2,1,0:T(8,128)}, f32[5,512,1536]{2,1,0:T(8,128)}, bf16[64,1536]{1,0:T(8,128)(2,1)}, bf16[64,...) custom-call(bf16[1536,512]{1,0:T(8,128)(2,1)} %get-tuple-element.24.xt_in, ...), custom_call_target="tpu_custom_call" | custom-call | tf_op jit(solution)/shard_map/weight_grads/pallas_call | solution.py:612
  (1 shorter events, 0.0 us)

commit v3 on v2

--- a/solution.py
+++ b/solution.py
@@ -40,6 +40,8 @@
         self.dev = {}
         self.block = {}
         self.flat = {}
+        self.pair = {}
+        self.chips = {}
         for flip_y in (0, 1):
             for flip_x in (0, 1):
                 for flip_c in (0, 1):
@@ -50,6 +52,8 @@
                     self.dev[name] = (0, yy, xx * 2 + cc)
                     self.block[name] = cc * 4 + yy * 2 + xx
                     self.flat[name] = yy * 4 + xx * 2 + cc
+                    self.pair[name] = (yy * 2 + xx) * 2 + cc
+                    self.chips[name] = yy * 2 + xx
 
 
 class Link:
@@ -79,9 +83,9 @@
 
 
 class Gather:
-    def __init__(self, pool, place, buf, rows):
+    def __init__(self, pool, place, buf, rows, index):
         def at(name, lo=0, n=rows):
-            return buf.at[pl.ds(pl.multiple_of(place.block[name] * rows + lo, 8), n), :]
+            return buf.at[pl.ds(pl.multiple_of(index[name] * rows + lo, 8), n), :]
 
         half = rows // 2
         own = at('')
@@ -94,20 +98,26 @@
         self.core_x = Link(pool, at('x'), at('x'), at('xc'), dev['c'])
         self.core_y = Link(pool, at('y'), at('y'), at('yc'), dev['c'])
         self.core_d = Link(pool, at('yx'), at('yx'), at('yxc'), dev['c'])
+        self.early = None
         self.links = (self.to_x, self.to_y, self.to_c, self.relay_x, self.relay_y, self.core_x, self.core_y, self.core_d)
 
     def begin(self):
         self.to_x.start()
         self.to_y.start()
         self.to_c.start()
+
+    def after(self):
+        self.early = True
+        self.to_x.sent()
+        self.to_y.sent()
 
     def relay(self):
         self.to_y.arrive()
         self.relay_x.start()
         self.to_x.arrive()
         self.relay_y.start()
+        self.core_x.start()
         self.core_y.start()
-        self.core_x.start()
 
     def last(self):
         self.relay_x.arrive()
@@ -121,7 +131,7 @@
         self.core_d.arrive()
 
     def drain(self):
-        for link in self.links:
+        for link in self.links[0 if self.early is None else 2:]:
             link.sent()
 
 
@@ -191,11 +201,11 @@
 NUM_LINKS = 7 + 14 + 8 * 5 + 7 * 5
 
 
-def attention_pair(xa, wqkv, wo, part, first, dims):
+def attention_pair(xa, wqkv, wo, part, chip, chips, dims):
     seq, kv_dim, heads, head_dim = dims
     q_dim = heads * head_dim
     pair = 2 * seq
-    rows = pl.ds(pl.multiple_of(first, pair), pair)
+    rows = pl.ds(pl.multiple_of(chip * pair, pair), pair)
     row = lax.broadcasted_iota(jnp.int32, (pair, pair), 0)
     col = lax.broadcasted_iota(jnp.int32, (pair, pair), 1)
     causal = (row >= col) & ((row >= seq) == (col >= seq))
@@ -210,14 +220,15 @@
         ex = jnp.exp(scores - top)
         probs = (ex / jnp.sum(ex, axis=1, keepdims=True)).astype(BF16)
         outs.append(dot_nn(probs, vals).astype(BF16))
-    part[rows, :] = dot_nn(jnp.concatenate(outs, axis=1), wo[...])
+    out = dot_nn(jnp.concatenate(outs, axis=1), wo[...])
+    for c in range(2):
+        part[pl.ds(pl.multiple_of((c * chips + chip) * seq, seq), seq), :] = out[c * seq:(c + 1) * seq, :]
 
 
 def make_layer_kernel(tok, d_model, d_ff, exp_loc, attn_dims):
     r = tok // HALVES
     m = r * NUM_DEV
     tile = 512
-    units = HALVES * exp_loc
 
     def kernel(x_in, dy_in, xa_in, gt_in, idx_in, wg_in, wu_in, wd_in, wq_in, wk_in, wv_in, wo_in,
                y_out, dx_out, attn_out, dg_out, xt_all, dy_all, da_all, db_all, ht_all, gates_out,
@@ -229,14 +240,14 @@
         dev, block = place.dev, place.block
         me = block['']
 
-        def own_rows(buf, rows):
-            return buf.at[pl.ds(pl.multiple_of(me * rows, 8), rows), :]
+        def own_rows(buf, rows, index=me):
+            return buf.at[pl.ds(pl.multiple_of(index * rows, 8), rows), :]
 
         loads = []
         for h in range(HALVES):
             loads.append(pltpu.make_async_copy(x_in.at[h * r:(h + 1) * r, :], own_rows(xb.at[h], r), in_sems.at[h]))
             loads.append(pltpu.make_async_copy(dy_in.at[h * r:(h + 1) * r, :], own_rows(dyb.at[h], r), in_sems.at[2 + h]))
-        loads.append(pltpu.make_async_copy(xa_in, own_rows(xab, tok), in_sems.at[4]))
+        loads.append(pltpu.make_async_copy(xa_in, own_rows(xab, tok, place.pair['']), in_sems.at[4]))
         for load in loads:
             load.start()
         q_dim, kv_dim = wq_in.shape[0], wk_in.shape[0]
@@ -247,10 +258,6 @@
         weights = []
         for e in range(exp_loc):
             weights.append([pltpu.make_async_copy(src.at[e], dst.at[e], w_sems.at[e, k]) for k, (src, dst) in enumerate(((wg_in, wg), (wu_in, wu), (wd_in, wd)))])
-        for ws in weights:
-            for w in ws:
-                w.start()
-
         barrier = pltpu.get_barrier_semaphore()
         peers = [name for name in dev if name]
         for name in peers:
@@ -258,22 +265,23 @@
         pl.semaphore_wait(barrier, len(peers))
 
         routes = [Link(pool, gt_in.at[place.flat[name]], gtb.at[me], gtb.at[block[name]], dev[name]) for name in peers]
-        gx = [Gather(pool, place, xb.at[h], r) for h in range(HALVES)]
-        gdy = [Gather(pool, place, dyb.at[h], r) for h in range(HALVES)]
-        gxa = Gather(pool, place, xab, tok)
+        gx = [Gather(pool, place, xb.at[h], r, block) for h in range(HALVES)]
+        gdy = [Gather(pool, place, dyb.at[h], r, block) for h in range(HALVES)]
+        gxa = Gather(pool, place, xab, tok, place.pair)
         sy = [Scatter(pool, place, y_part.at[h], ry0.at[h], ry1.at[h], ry2.at[h], ry3.at[h], ry4.at[h], r) for h in range(HALVES)]
         sdx = [Scatter(pool, place, dx_part.at[h], rd0.at[h], rd1.at[h], rd2.at[h], rd3.at[h], rd4.at[h], r) for h in range(HALVES)]
         sat = Scatter(pool, place, at_part, ra0, ra1, ra2, ra3, ra4, tok)
         dg_links = [[Link(pool, dgt.at[h, 1 - place.core if 'c' in name else place.core], dgl.at[me, h], dgl.at[block[name], h], dev[name]) for name in peers] for h in range(HALVES)]
 
+        for load in loads:
+            load.wait()
+        gxa.begin()
         for link in routes:
             link.start()
         gtb[me] = gt_in[place.flat['']]
-        for load in loads:
-            load.wait()
-        gxa.begin()
-        gx[0].begin()
-        gdy[0].begin()
+        for ws in weights:
+            for w in ws:
+                w.start()
         dgc[...] = jnp.zeros_like(dgc)
         gcol[...] = jnp.zeros_like(gcol)
         y_part[...] = jnp.zeros_like(y_part)
@@ -282,23 +290,26 @@
             load.wait()
 
         def pair(name):
-            attention_pair(xab, wqkv, wo, at_part, lax.div(block[name], 2) * (2 * tok), attn_dims)
-
+            attention_pair(xab, wqkv, wo, at_part, place.chips[name], NUM_DEV // 2, attn_dims)
+
+        gxa.to_c.arrive()
+        pair('')
+        gxa.after()
+        gx[0].begin()
         gxa.relay()
-        pair('')
+        gdy[0].begin()
+        gxa.core_x.arrive()
+        pair('x')
         gx[0].relay()
-        gxa.to_c.arrive()
-        gxa.core_x.arrive()
-        pair('c')
+        gxa.core_y.arrive()
+        pair('y')
+        gx[1].begin()
+        gxa.last()
         gdy[0].relay()
-        gx[1].begin()
         gdy[1].begin()
-        gxa.last()
-        pair('y')
         gx[0].last()
-        gxa.core_y.arrive()
         gxa.core_d.arrive()
-        pair('yc')
+        pair('yx')
         sat.begin()
         for link in routes:
             link.arrive()
@@ -306,123 +317,139 @@
         for h in range(HALVES):
             for b in range(NUM_DEV):
                 gcol[h, b * r:(b + 1) * r, 0:8] = wide[h * r:(h + 1) * r, b * 8:(b + 1) * 8]
+        gdy[0].last()
         gx[0].finish()
-
-        def staged(u, k):
-            h, e = lax.div(u, exp_loc), lax.rem(u, exp_loc)
-            slot = lax.rem(u, 2)
-            part = pl.ds(pl.multiple_of(h * m, LANES), m)
+        gdy[0].finish()
+
+        def staged(h, e, k):
+            slot = h * 2 + lax.rem(e, 2)
+            part = pl.ds(h * m, m)
             if k == 2:
                 return pltpu.make_async_copy(stage_t.at[slot], ht_all.at[e, :, part], stage_sems.at[slot, k])
             return pltpu.make_async_copy(stage.at[slot, k], (da_all, db_all)[k].at[e, part, :], stage_sems.at[slot, k])
 
         lane = lax.broadcasted_iota(jnp.int32, (m, LANES), 1)
 
-        def at2():
-            gx[1].last()
-
-        def at3():
-            gdy[1].last()
-            gx[1].finish()
-
-        def at4():
-            gdy[1].finish()
-
-        def at5():
-            sy[0].begin()
-            sdx[0].begin()
-
-        def at6():
-            sy[0].middle()
-            sdx[0].middle()
-
-        def at8():
-            sat.finish(attn_out)
-
-        early = {1: gx[1].relay, 2: at2, 3: at3, 4: at4, 5: at5, 6: at6, 8: at8}
-
-        def mid0():
-            gdy[0].last()
-            gdy[0].finish()
-
-        def mid1():
-            gdy[1].relay()
-            sat.middle()
-
-        mid = {0: mid0, 1: mid1, 5: sat.late, 9: sy[0].late}
-
-        def unit(u, _):
-            h, e = lax.div(u, exp_loc), lax.rem(u, exp_loc)
-            slot = lax.rem(u, 2)
-
-            @pl.when(u < exp_loc)
-            def _():
+        def gate_of(h, e):
+            return jnp.sum(jnp.where(lane == e, gcol[h], 0.0), axis=1, keepdims=True)
+
+        def phase(h, events, step, kinds):
+            def body(e, _):
+                for k, event in events.items():
+                    pl.when(e == k)(event)
+
+                @pl.when(e >= 2)
+                def _():
+                    for k in kinds:
+                        staged(h, e - 2, k).wait()
+
+                step(h, e)
+                for k in kinds:
+                    staged(h, e, k).start()
+                return 0
+
+            lax.fori_loop(0, exp_loc, body, 0)
+
+        def forward(h, e):
+            if h == 0:
                 for k, (src, dst) in enumerate(((wg_in, wg), (wu_in, wu), (wd_in, wd))):
                     pltpu.make_async_copy(src.at[e], dst.at[e], w_sems.at[e, k]).wait()
-
-            @pl.when(u >= 2)
-            def _():
-                for k in range(3):
-                    staged(u - 2, k).wait()
-
-            for k, events in early.items():
-                pl.when(u == k)(events)
-
-            gate = jnp.sum(jnp.where(lane == e, gcol[h], 0.0), axis=1, keepdims=True)
+            gate = gate_of(h, e)
             mask = gate > 0.0
             a = jnp.where(mask, dot_nn(xb[h], wg[e]), 0.0)
             b = jnp.where(mask, dot_nn(xb[h], wu[e]), 0.0)
             sig = jax.nn.sigmoid(a)
             act = a * sig
             hid[...] = (act * b).astype(BF16)
-            stage_t[slot] = hid[...].T
-            s1[...] = b * sig * (1.0 + a * (1.0 - sig))
-            s2[...] = act
-            for k, events in mid.items():
-                pl.when(u == k)(events)
+            stage_t[h * 2 + lax.rem(e, 2)] = hid[...].T
+            s1[e] = b * sig * (1.0 + a * (1.0 - sig))
+            s2[e] = act
             dots = jnp.zeros((m, LANES), F32)
             for n in range(d_model // tile):
                 cols = pl.ds(n * tile, tile)
                 o = dot_nn(hid[...], wd[e, :, cols]).astype(BF16).astype(F32)
-                dy = dyb[h, :, cols].astype(F32)
                 y_part[h, :, cols] += gate * o
-                prod = dy * o
+                prod = dyb[h, :, cols].astype(F32) * o
                 for k in range(tile // LANES):
                     dots += prod[:, k * LANES:(k + 1) * LANES]
-                d_o[:, cols] = (gate * dy).astype(BF16)
             dgc[h] = jnp.where(lane == e, jnp.sum(dots, axis=1, keepdims=True), dgc[h])
+
+        def backward(h, e):
+            slot = h * 2 + lax.rem(e, 2)
+            gate = gate_of(h, e)
+            for n in range(d_model // tile):
+                cols = pl.ds(n * tile, tile)
+                d_o[:, cols] = (gate * dyb[h, :, cols].astype(F32)).astype(BF16)
             dh = dot_nt(d_o[...], wd[e]).astype(BF16).astype(F32)
-            stage[slot, 0] = (dh * s1[...]).astype(BF16)
-            stage[slot, 1] = (dh * s2[...]).astype(BF16)
-            for k in range(3):
-                staged(u, k).start()
+            stage[slot, 0] = (dh * s1[e]).astype(BF16)
+            stage[slot, 1] = (dh * s2[e]).astype(BF16)
             for n in range(d_model // tile):
                 cols = pl.ds(n * tile, tile)
                 dxe = dot_nt(stage[slot, 0], wg[e, cols, :]) + dot_nt(stage[slot, 1], wu[e, cols, :])
                 dx_part[h, :, cols] += dxe.astype(BF16).astype(F32)
-            return 0
-
-        lax.fori_loop(0, units, unit, 0)
-
-        sy[1].begin()
-        sdx[1].begin()
-        for h in range(HALVES):
+
+        def send_dg(h):
             turned = dgc[h].T
             for c in range(2):
                 dgt[h, c] = turned[0:8, c * LANES:(c + 1) * LANES]
-        sdx[0].late()
-        sy[1].middle()
-        sdx[1].middle()
-        for h in range(HALVES):
             for link in dg_links[h]:
                 link.start()
             dgl[me, h] = dgt[h, place.core]
+
+        def fa1():
+            gx[1].relay()
+            sat.middle()
+
+        def fa2():
+            gdy[1].relay()
+
+        def fa3():
+            gx[1].last()
+
+        phase(0, {1: fa1, 2: fa2, 3: fa3}, forward, (2,))
+        sy[0].begin()
+        send_dg(0)
+        gx[1].finish()
+
+        def ba1():
+            gdy[1].last()
+            sy[0].middle()
+
+        def ba2():
+            sat.late()
+
+        phase(0, {1: ba1, 2: ba2}, backward, (0, 1))
+        gdy[1].finish()
+        sdx[0].begin()
+
+        def fb1():
+            sdx[0].middle()
+            sy[0].late()
+
+        def fb2():
+            sat.finish(attn_out)
+
+        phase(1, {1: fb1, 2: fb2}, forward, (2,))
+        sy[1].begin()
+        send_dg(1)
+
+        def bb1():
+            sy[1].middle()
+            sdx[0].late()
+
+        def bb3():
+            sy[0].finish(y_out.at[0:r, :])
+
+        phase(1, {1: bb1, 3: bb3}, backward, (0, 1))
+        sdx[1].begin()
+        sy[1].late()
+        for h in range(HALVES):
             xt[:, h * m:(h + 1) * m] = xb[h].T
+        sdx[1].middle()
         saves = [pltpu.make_async_copy(xt, xt_all, out_sems.at[0]), pltpu.make_async_copy(dyb, dy_all, out_sems.at[1]), pltpu.make_async_copy(gcol, gates_out, out_sems.at[2])]
         for save in saves:
             save.start()
-        for s, out in ((sy[0], y_out), (sdx[0], dx_out)):
-            s.finish(out.at[0:r, :])
+        sdx[0].finish(dx_out.at[0:r, :])
         for h in range(HALVES):
             for link in dg_links[h]:
                 link.arrive()
@@ -438,15 +465,15 @@
                 for e in range(exp_loc):
                     total = jnp.where(slots == first + e, mine[e:e + 1, :], total)
             dg_out[:, h * r:(h + 1) * r] = total
-        sy[1].late()
         sdx[1].late()
         for s, out in ((sy[1], y_out), (sdx[1], dx_out)):
             s.finish(out.at[r:2 * r, :])
-        for u in (units - 2, units - 1):
-            for k in range(3):
-                staged(jnp.int32(u), k).wait()
         for save in saves:
             save.wait()
+        for h in range(HALVES):
+            for e in (exp_loc - 2, exp_loc - 1):
+                for k in range(3):
+                    staged(h, jnp.int32(e), k).wait()
         for item in gx + gdy + [gxa] + sy + sdx + [sat]:
             item.drain()
         for link in routes + dg_links[0] + dg_links[1]:
@@ -596,12 +623,12 @@
                             pltpu.VMEM((NUM_DEV, 8, LANES), F32), pltpu.VMEM((HALVES, m, LANES), F32),
                             pltpu.VMEM((exp_loc, d_model, d_ff), BF16), pltpu.VMEM((exp_loc, d_model, d_ff), BF16), pltpu.VMEM((exp_loc, d_ff, d_model), BF16),
                             pltpu.VMEM((HALVES, m, d_model), F32), pltpu.VMEM((HALVES, m, d_model), F32), pltpu.VMEM((total, d_model), F32), pltpu.VMEM((q_dim + 2 * kv_dim, d_model), BF16), pltpu.VMEM((q_dim, d_model), BF16),
-                            pltpu.VMEM((m, d_ff), F32), pltpu.VMEM((m, d_ff), F32), pltpu.VMEM((m, d_model), BF16),
-                            pltpu.VMEM((HALVES, m, LANES), F32), pltpu.VMEM((HALVES, 2, 8, LANES), F32), pltpu.VMEM((2, 2, m, d_ff), BF16),
-                            pltpu.VMEM((m, d_ff), BF16), pltpu.VMEM((2, d_ff, m), BF16), pltpu.VMEM((d_model, total), BF16), pltpu.VMEM((NUM_DEV, HALVES, 8, LANES), F32)]
+                            pltpu.VMEM((exp_loc, m, d_ff), F32), pltpu.VMEM((exp_loc, m, d_ff), F32), pltpu.VMEM((m, d_model), BF16),
+                            pltpu.VMEM((HALVES, m, LANES), F32), pltpu.VMEM((HALVES, 2, 8, LANES), F32), pltpu.VMEM((2 * HALVES, 2, m, d_ff), BF16),
+                            pltpu.VMEM((m, d_ff), BF16), pltpu.VMEM((2 * HALVES, d_ff, m), BF16), pltpu.VMEM((d_model, total), BF16), pltpu.VMEM((NUM_DEV, HALVES, 8, LANES), F32)]
             + half_shapes() + half_shapes() + scatter_shapes(tok, d_model)
             + [pltpu.SemaphoreType.DMA((NUM_LINKS,)), pltpu.SemaphoreType.DMA((NUM_LINKS,)), pltpu.SemaphoreType.DMA((exp_loc, 3)),
-               pltpu.SemaphoreType.DMA((5,)), pltpu.SemaphoreType.DMA((4,)), pltpu.SemaphoreType.DMA((3,)), pltpu.SemaphoreType.DMA((2, 3))],
+               pltpu.SemaphoreType.DMA((5,)), pltpu.SemaphoreType.DMA((4,)), pltpu.SemaphoreType.DMA((3,)), pltpu.SemaphoreType.DMA((2 * HALVES, 3))],
             compiler_params=pltpu.CompilerParams(collective_id=0, has_side_effects=True, vmem_limit_bytes=67000000),
             name='layer',
         )(x_tokens, dy_tokens, x_attn.reshape(tok, d_model), table, expert_idx.T, w_gate, w_up, w_down, wq, wk, wv, wo)

time: 113 us -> 101 us (0.89)
  Pallas kernels: 110 us -> 98.7 us
    pallas_call x1, Pallas kernels: 87.1 us -> 75.5 us  [local_step(): pl.pallas_call(kernel, out_shape=(shape((tok, d_model), BF16), shape((tok...]
where the time goes in v3:
time: 101 us
  Pallas kernels  98.7 us (98%)
    pallas_call x1, Pallas kernels, local_step(): pl.pallas_call(kernel, out_shape=(shape((tok, d_model), BF16), shape((tok...  75.5 us
    pallas_call x1, Pallas kernels, local_step(): pl.pallas_call(functools.partial(weight_grads, width, slots), out_shape=(...  23.2 us

profile of v3, /device:TPU:0, one launch (start us, length us, event | category | flops | bytes accessed | tf_op | source)
XLA Modules:
  0.0 100.8 jit_solution(98782156303102206)
XLA Ops:
  0.6 0.8 select_reduce_fusion
  1.5 0.6 pad.4.gt_in
  2.1 75.5 %layer.1 = (bf16[64,1536]{1,0:T(8,128)(2,1)}, bf16[64,1536]{1,0:T(8,128)(2,1)}, bf16[64,1536]{1,0:T(8,128)(2,1)}, f32[8,64]{1,0:T(8,128)}, bf16[1536,512]{1,0:T(...) custom-call(bf16[64,1536]{1,0:T(8,128)(2,1)} %x_in.1, ...), custom_call_target="tpu_custom_call" | custom-call | tf_op jit(solution)/shard_map/layer/pallas_call | solution.py:615
  77.7 23.2 %weight_grads.1 = (f32[5,1536,512]{2,1,0:T(8,128)}, f32[5,1536,512]{2,1,0:T(8,128)}, f32[5,512,1536]{2,1,0:T(8,128)}, bf16[64,1536]{1,0:T(8,128)(2,1)}, bf16[64,...) custom-call(bf16[1536,512]{1,0:T(8,128)(2,1)} %get-tuple-element.24.xt_in, ...), custom_call_target="tpu_custom_call" | custom-call | tf_op jit(solution)/shard_map/weight_grads/pallas_call | solution.py:639
  (1 shorter events, 0.0 us)

commit v4 on v3

--- a/solution.py
+++ b/solution.py
@@ -136,13 +136,14 @@
 
 
 class Scatter:
-    def __init__(self, pool, place, part, from_core, from_x, from_y, last_x, last_y, rows):
+    def __init__(self, pool, place, part, from_core, from_x, from_y, last_x, last_y, rows, first=0):
         half = rows // 2
         self.half, self.part, self.rows, self.place = half, part, rows, place
         self.from_core, self.from_x, self.from_y, self.last_x, self.last_y = from_core, from_x, from_y, last_x, last_y
         four = 4 * rows
         self.mine = pl.multiple_of(place.core * four, 8)
-        other = part.at[pl.ds(pl.multiple_of((1 - place.core) * four, 8), four), :]
+        self.cols = pl.ds(first, from_core.shape[-1])
+        other = part.at[pl.ds(pl.multiple_of((1 - place.core) * four, 8), four), self.cols]
         dev = place.dev
         self.core = Link(pool, other, from_core, from_core, dev['c'])
         self.x0 = Link(pool, self.at('x', 0), from_x.at[0], from_x.at[0], dev['x'])
@@ -154,7 +155,7 @@
         self.links = (self.core, self.x0, self.x1, self.y0, self.y1, self.end_y, self.end_x)
 
     def at(self, name, lo):
-        return self.part.at[pl.ds(pl.multiple_of(self.place.block[name] * self.rows + lo, 8), self.half), :]
+        return self.part.at[pl.ds(pl.multiple_of(self.place.block[name] * self.rows + lo, 8), self.half), self.cols]
 
     def begin(self):
         self.core.start()
@@ -162,7 +163,7 @@
     def middle(self):
         self.core.arrive()
         mine = pl.ds(self.mine, 4 * self.rows)
-        self.part[mine, :] = self.part[mine, :] + self.from_core[...]
+        self.part[mine, self.cols] = self.part[mine, self.cols] + self.from_core[...]
         self.x1.start()
         self.y1.start()
         self.x0.start()
@@ -178,14 +179,14 @@
         here[...] = here[...] + self.from_y[1]
         self.end_x.start()
 
-    def finish(self, out):
+    def finish(self, out, row=0):
         half = self.half
         self.x0.arrive()
         self.y0.arrive()
         self.end_y.arrive()
         self.end_x.arrive()
-        out[0:half, :] = (self.at('', 0)[...] + self.from_x[0] + self.last_y[...]).astype(BF16)
-        out[half:2 * half, :] = (self.at('', half)[...] + self.from_y[0] + self.last_x[...]).astype(BF16)
+        out[row:row + half, self.cols] = (self.at('', 0)[...] + self.from_x[0] + self.last_y[...]).astype(BF16)
+        out[row + half:row + 2 * half, self.cols] = (self.at('', half)[...] + self.from_y[0] + self.last_x[...]).astype(BF16)
 
     def drain(self):
         for link in self.links:
@@ -198,18 +199,21 @@
             pltpu.VMEM((half, width), F32), pltpu.VMEM((half, width), F32)]
 
 
-NUM_LINKS = 7 + 14 + 8 * 5 + 7 * 5
-
-
-def attention_pair(xa, wqkv, wo, part, chip, chips, dims):
+NUM_LINKS = 7 + 14 + 8 * 5 + 7 * 13
+
+
+def attention_qkv(xa, wqkv, qkv, chip, seq):
+    pair = 2 * seq
+    qkv[...] = dot_nt(xa[pl.ds(pl.multiple_of(chip * pair, pair), pair), :], wqkv[...]).astype(BF16)
+
+
+def attention_out(qkv, wo, part, chip, chips, dims):
     seq, kv_dim, heads, head_dim = dims
     q_dim = heads * head_dim
     pair = 2 * seq
-    rows = pl.ds(pl.multiple_of(chip * pair, pair), pair)
     row = lax.broadcasted_iota(jnp.int32, (pair, pair), 0)
     col = lax.broadcasted_iota(jnp.int32, (pair, pair), 1)
     causal = (row >= col) & ((row >= seq) == (col >= seq))
-    qkv = dot_nt(xa[rows, :], wqkv[...]).astype(BF16)
     keys = qkv[:, q_dim:q_dim + kv_dim]
     vals = qkv[:, q_dim + kv_dim:q_dim + 2 * kv_dim]
     outs = []
@@ -229,12 +233,13 @@
     r = tok // HALVES
     m = r * NUM_DEV
     tile = 512
-
-    def kernel(x_in, dy_in, xa_in, gt_in, idx_in, wg_in, wu_in, wd_in, wq_in, wk_in, wv_in, wo_in,
+    tiles = d_model // tile
+
+    def kernel(x_in, dy_in, xa_in, idx_in, gate_in, wg_in, wu_in, wd_in, wq_in, wk_in, wv_in, wo_in,
                y_out, dx_out, attn_out, dg_out, xt_all, dy_all, da_all, db_all, ht_all, gates_out,
-               xb, dyb, xab, gtb, gcol, wg, wu, wd, y_part, dx_part, at_part, wqkv, wo, s1, s2, d_o, dgc, dgt, stage, hid, stage_t, xt, dgl,
+               xb, dyb, xab, gtb, gcol, wg, wu, wd, y_part, dx_part, at_part, wqkv, wo, qkv, s1, s2, d_o, dgc, dgt, da, db, hid, stage_t, xt, dgl, gtab, gfull,
                ry0, ry1, ry2, ry3, ry4, rd0, rd1, rd2, rd3, rd4, ra0, ra1, ra2, ra3, ra4,
-               send_sems, recv_sems, w_sems, in_sems, aw_sems, out_sems, stage_sems):
+               send_sems, recv_sems, w_sems, in_sems, aw_sems, out_sems, stage_sems, grad_sems):
         place = Place()
         pool = Pool(send_sems, recv_sems)
         dev, block = place.dev, place.block
@@ -262,14 +267,18 @@
         peers = [name for name in dev if name]
         for name in peers:
             pl.semaphore_signal(barrier, inc=1, device_id=dev[name], device_id_type=MESH_ID)
+        gtab[...] = jnp.zeros_like(gtab)
+        for g in range(NUM_DEV):
+            for e in range(exp_loc):
+                gtab[g, e:e + 1, 0:tok] = jnp.sum(jnp.where(idx_in[...] == g * exp_loc + e, gate_in[...], 0.0), axis=0, keepdims=True)
         pl.semaphore_wait(barrier, len(peers))
 
-        routes = [Link(pool, gt_in.at[place.flat[name]], gtb.at[me], gtb.at[block[name]], dev[name]) for name in peers]
+        routes = [Link(pool, gtab.at[place.flat[name]], gtb.at[me], gtb.at[block[name]], dev[name]) for name in peers]
         gx = [Gather(pool, place, xb.at[h], r, block) for h in range(HALVES)]
         gdy = [Gather(pool, place, dyb.at[h], r, block) for h in range(HALVES)]
         gxa = Gather(pool, place, xab, tok, place.pair)
-        sy = [Scatter(pool, place, y_part.at[h], ry0.at[h], ry1.at[h], ry2.at[h], ry3.at[h], ry4.at[h], r) for h in range(HALVES)]
-        sdx = [Scatter(pool, place, dx_part.at[h], rd0.at[h], rd1.at[h], rd2.at[h], rd3.at[h], rd4.at[h], r) for h in range(HALVES)]
+        sy = [[Scatter(pool, place, y_part.at[h], ry0.at[h, n], ry1.at[h, n], ry2.at[h, n], ry3.at[h, n], ry4.at[h, n], r, n * tile) for n in range(tiles)] for h in range(HALVES)]
+        sdx = [[Scatter(pool, place, dx_part.at[h], rd0.at[h, n], rd1.at[h, n], rd2.at[h, n], rd3.at[h, n], rd4.at[h, n], r, n * tile) for n in range(tiles)] for h in range(HALVES)]
         sat = Scatter(pool, place, at_part, ra0, ra1, ra2, ra3, ra4, tok)
         dg_links = [[Link(pool, dgt.at[h, 1 - place.core if 'c' in name else place.core], dgl.at[me, h], dgl.at[block[name], h], dev[name]) for name in peers] for h in range(HALVES)]
 
@@ -278,19 +287,20 @@
         gxa.begin()
         for link in routes:
             link.start()
-        gtb[me] = gt_in[place.flat['']]
+        gtb[me] = gtab[place.flat['']]
         for ws in weights:
             for w in ws:
                 w.start()
         dgc[...] = jnp.zeros_like(dgc)
         gcol[...] = jnp.zeros_like(gcol)
-        y_part[...] = jnp.zeros_like(y_part)
-        dx_part[...] = jnp.zeros_like(dx_part)
         for load in attn_loads:
             load.wait()
 
-        def pair(name):
-            attention_pair(xab, wqkv, wo, at_part, place.chips[name], NUM_DEV // 2, attn_dims)
+        def pair(name, between=None):
+            attention_qkv(xab, wqkv, qkv, place.chips[name], tok)
+            if between is not None:
+                between()
+            attention_out(qkv, wo, at_part, place.chips[name], NUM_DEV // 2, attn_dims)
 
         gxa.to_c.arrive()
         pair('')
@@ -300,16 +310,13 @@
         gdy[0].begin()
         gxa.core_x.arrive()
         pair('x')
-        gx[0].relay()
         gxa.core_y.arrive()
-        pair('y')
+        pair('y', gx[0].relay)
         gx[1].begin()
         gxa.last()
         gdy[0].relay()
-        gdy[1].begin()
-        gx[0].last()
         gxa.core_d.arrive()
-        pair('yx')
+        pair('yx', gx[0].last)
         sat.begin()
         for link in routes:
             link.arrive()
@@ -317,76 +324,96 @@
         for h in range(HALVES):
             for b in range(NUM_DEV):
                 gcol[h, b * r:(b + 1) * r, 0:8] = wide[h * r:(h + 1) * r, b * 8:(b + 1) * 8]
-        gdy[0].last()
+            for e in range(exp_loc):
+                gfull[h, e] = jnp.broadcast_to(gcol[h][:, e:e + 1], (m, LANES))
         gx[0].finish()
-        gdy[0].finish()
 
         def staged(h, e, k):
-            slot = h * 2 + lax.rem(e, 2)
             part = pl.ds(h * m, m)
             if k == 2:
-                return pltpu.make_async_copy(stage_t.at[slot], ht_all.at[e, :, part], stage_sems.at[slot, k])
-            return pltpu.make_async_copy(stage.at[slot, k], (da_all, db_all)[k].at[e, part, :], stage_sems.at[slot, k])
+                slot = h * 2 + lax.rem(e, 2)
+                return pltpu.make_async_copy(stage_t.at[slot], ht_all.at[e, :, part], stage_sems.at[slot])
+            return pltpu.make_async_copy((da, db)[k].at[e], (da_all, db_all)[k].at[e, part, :], grad_sems.at[e, k])
 
         lane = lax.broadcasted_iota(jnp.int32, (m, LANES), 1)
 
         def gate_of(h, e):
-            return jnp.sum(jnp.where(lane == e, gcol[h], 0.0), axis=1, keepdims=True)
-
-        def phase(h, events, step, kinds):
-            def body(e, _):
-                for k, event in events.items():
-                    pl.when(e == k)(event)
+            return jnp.concatenate([gfull[h, e]] * (tile // LANES), axis=1)
+
+        def loop(count, events, body):
+            def step(k, _):
+                for at, event in events.items():
+                    pl.when(k == at)(event)
+                body(k)
+                return 0
+
+            lax.fori_loop(0, count, step, 0)
+
+        def hidden(h):
+            def body(e):
+                if h == 0:
+                    for k, (src, dst) in enumerate(((wg_in, wg), (wu_in, wu), (wd_in, wd))):
+                        pltpu.make_async_copy(src.at[e], dst.at[e], w_sems.at[e, k]).wait()
 
                 @pl.when(e >= 2)
                 def _():
-                    for k in kinds:
-                        staged(h, e - 2, k).wait()
-
-                step(h, e)
-                for k in kinds:
+                    staged(h, e - 2, 2).wait()
+
+                mask = gate_of(h, e) > 0.0
+                a = jnp.where(mask, dot_nn(xb[h], wg[e]), 0.0)
+                b = jnp.where(mask, dot_nn(xb[h], wu[e]), 0.0)
+                sig = jax.nn.sigmoid(a)
+                act = a * sig
+                hid[e] = (act * b).astype(BF16)
+                stage_t[h * 2 + lax.rem(e, 2)] = hid[e].T
+                s1[e] = b * sig * (1.0 + a * (1.0 - sig))
+                s2[e] = act
+                staged(h, e, 2).start()
+
+            return body
+
+        def outputs(h):
+            def body(n):
+                cols = pl.ds(pl.multiple_of(n * tile, tile), tile)
+                dy = dyb[h, :, cols].astype(F32)
+                sums = dgc[h]
+                for e in range(exp_loc):
+                    o = dot_nn(hid[e], wd[e, :, cols]).astype(BF16).astype(F32)
+                    y = gate_of(h, e) * o
+                    y_part[h, :, cols] = y if e == 0 else y_part[h, :, cols] + y
+                    prod = dy * o
+                    dots = prod[:, 0:LANES]
+                    for k in range(1, tile // LANES):
+                        dots += prod[:, k * LANES:(k + 1) * LANES]
+                    sums += jnp.where(lane == e, jnp.sum(dots, axis=1, keepdims=True), 0.0)
+                dgc[h] = sums
+
+            return body
+
+        def hidden_grads(h):
+            def body(e):
+                if h:
+                    for k in range(2):
+                        staged(h - 1, e, k).wait()
+                for n in range(tiles):
+                    cols = pl.ds(n * tile, tile)
+                    d_o[:, cols] = (gate_of(h, e) * dyb[h, :, cols].astype(F32)).astype(BF16)
+                dh = dot_nt(d_o[...], wd[e]).astype(BF16).astype(F32)
+                da[e] = (dh * s1[e]).astype(BF16)
+                db[e] = (dh * s2[e]).astype(BF16)
+                for k in range(2):
                     staged(h, e, k).start()
-                return 0
-
-            lax.fori_loop(0, exp_loc, body, 0)
-
-        def forward(h, e):
-            if h == 0:
-                for k, (src, dst) in enumerate(((wg_in, wg), (wu_in, wu), (wd_in, wd))):
-                    pltpu.make_async_copy(src.at[e], dst.at[e], w_sems.at[e, k]).wait()
-            gate = gate_of(h, e)
-            mask = gate > 0.0
-            a = jnp.where(mask, dot_nn(xb[h], wg[e]), 0.0)
-            b = jnp.where(mask, dot_nn(xb[h], wu[e]), 0.0)
-            sig = jax.nn.sigmoid(a)
-            act = a * sig
-            hid[...] = (act * b).astype(BF16)
-            stage_t[h * 2 + lax.rem(e, 2)] = hid[...].T
-            s1[e] = b * sig * (1.0 + a * (1.0 - sig))
-            s2[e] = act
-            dots = jnp.zeros((m, LANES), F32)
-            for n in range(d_model // tile):
-                cols = pl.ds(n * tile, tile)
-                o = dot_nn(hid[...], wd[e, :, cols]).astype(BF16).astype(F32)
-                y_part[h, :, cols] += gate * o
-                prod = dyb[h, :, cols].astype(F32) * o
-                for k in range(tile // LANES):
-                    dots += prod[:, k * LANES:(k + 1) * LANES]
-            dgc[h] = jnp.where(lane == e, jnp.sum(dots, axis=1, keepdims=True), dgc[h])
-
-        def backward(h, e):
-            slot = h * 2 + lax.rem(e, 2)
-            gate = gate_of(h, e)
-            for n in range(d_model // tile):
-                cols = pl.ds(n * tile, tile)
-                d_o[:, cols] = (gate * dyb[h, :, cols].astype(F32)).astype(BF16)
-            dh = dot_nt(d_o[...], wd[e]).astype(BF16).astype(F32)
-            stage[slot, 0] = (dh * s1[e]).astype(BF16)
-            stage[slot, 1] = (dh * s2[e]).astype(BF16)
-            for n in range(d_model // tile):
-                cols = pl.ds(n * tile, tile)
-                dxe = dot_nt(stage[slot, 0], wg[e, cols, :]) + dot_nt(stage[slot, 1], wu[e, cols, :])
-                dx_part[h, :, cols] += dxe.astype(BF16).astype(F32)
+
+            return body
+
+        def input_grads(h):
+            def body(n):
+                cols = pl.ds(pl.multiple_of(n * tile, tile), tile)
+                for e in range(exp_loc):
+                    dxe = (dot_nt(da[e], wg[e, cols, :]) + dot_nt(db[e], wu[e, cols, :])).astype(BF16).astype(F32)
+                    dx_part[h, :, cols] = dxe if e == 0 else dx_part[h, :, cols] + dxe
+
+            return body
 
         def send_dg(h):
             turned = dgc[h].T
@@ -396,60 +423,44 @@
                 link.start()
             dgl[me, h] = dgt[h, place.core]
 
-        def fa1():
-            gx[1].relay()
-            sat.middle()
-
-        def fa2():
-            gdy[1].relay()
-
-        def fa3():
-            gx[1].last()
-
-        phase(0, {1: fa1, 2: fa2, 3: fa3}, forward, (2,))
-        sy[0].begin()
+        def seq(*calls):
+            def run():
+                for call in calls:
+                    call()
+
+            return run
+
+        loop(exp_loc, {0: gdy[1].begin, 1: seq(gdy[0].last, gx[1].relay), 2: sat.middle, 4: seq(gdy[1].relay, gx[1].last)}, hidden(0))
+        gdy[0].finish()
+        loop(tiles, {1: sy[0][0].begin, 2: sy[0][1].begin}, outputs(0))
+        sy[0][2].begin()
         send_dg(0)
         gx[1].finish()
-
-        def ba1():
-            gdy[1].last()
-            sy[0].middle()
-
-        def ba2():
-            sat.late()
-
-        phase(0, {1: ba1, 2: ba2}, backward, (0, 1))
-        gdy[1].finish()
-        sdx[0].begin()
-
-        def fb1():
-            sdx[0].middle()
-            sy[0].late()
-
-        def fb2():
-            sat.finish(attn_out)
-
-        phase(1, {1: fb1, 2: fb2}, forward, (2,))
-        sy[1].begin()
+        loop(exp_loc, {1: sy[0][0].middle, 3: sy[0][1].middle, 4: sy[0][2].middle}, hidden_grads(0))
+        loop(tiles, {1: sdx[0][0].begin, 2: seq(sdx[0][1].begin, sat.late)}, input_grads(0))
+        sdx[0][2].begin()
+        loop(exp_loc, {0: gdy[1].last, 1: seq(sdx[0][0].middle, sdx[0][1].middle, sy[0][0].late), 2: seq(gdy[1].finish, sdx[0][2].middle, sy[0][1].late),
+                       3: sy[0][2].late, 4: functools.partial(sat.finish, attn_out)}, hidden(1))
+        loop(tiles, {1: sy[1][0].begin, 2: seq(sy[1][1].begin, sdx[0][0].late)}, outputs(1))
+        sy[1][2].begin()
         send_dg(1)
-
-        def bb1():
-            sy[1].middle()
-            sdx[0].late()
-
-        def bb3():
-            sy[0].finish(y_out.at[0:r, :])
-
-        phase(1, {1: bb1, 3: bb3}, backward, (0, 1))
-        sdx[1].begin()
-        sy[1].late()
+        sdx[0][1].late()
+        loop(exp_loc, {1: sy[1][0].middle, 2: sdx[0][2].late, 3: seq(sy[1][1].middle, sy[1][2].middle), 4: seq(*[functools.partial(s.finish, y_out) for s in sy[0]])}, hidden_grads(1))
+        loop(tiles, {1: sdx[1][0].begin, 2: seq(sdx[1][1].begin, sdx[1][0].middle, sy[1][0].late)}, input_grads(1))
+        sdx[1][2].begin()
+        sdx[1][1].middle()
+        sy[1][1].late()
+        sy[1][2].late()
+        sdx[1][2].middle()
         for h in range(HALVES):
             xt[:, h * m:(h + 1) * m] = xb[h].T
-        sdx[1].middle()
         saves = [pltpu.make_async_copy(xt, xt_all, out_sems.at[0]), pltpu.make_async_copy(dyb, dy_all, out_sems.at[1]), pltpu.make_async_copy(gcol, gates_out, out_sems.at[2])]
         for save in saves:
             save.start()
-        sdx[0].finish(dx_out.at[0:r, :])
+        for s in sdx[0]:
+            s.finish(dx_out)
+        for s in sdx[1]:
+            s.late()
         for h in range(HALVES):
             for link in dg_links[h]:
                 link.arrive()
@@ -465,16 +476,19 @@
                 for e in range(exp_loc):
                     total = jnp.where(slots == first + e, mine[e:e + 1, :], total)
             dg_out[:, h * r:(h + 1) * r] = total
-        sdx[1].late()
-        for s, out in ((sy[1], y_out), (sdx[1], dx_out)):
-            s.finish(out.at[r:2 * r, :])
+        for s in sy[1]:
+            s.finish(y_out, r)
+        for s in sdx[1]:
+            s.finish(dx_out, r)
         for save in saves:
             save.wait()
+        for e in range(exp_loc):
+            for k in range(2):
+                staged(HALVES - 1, jnp.int32(e), k).wait()
         for h in range(HALVES):
             for e in (exp_loc - 2, exp_loc - 1):
-                for k in range(3):
-                    staged(h, jnp.int32(e), k).wait()
-        for item in gx + gdy + [gxa] + sy + sdx + [sat]:
+                staged(h, jnp.int32(e), 2).wait()
+        for item in gx + gdy + [gxa, sat] + sum(sy + sdx, []):
             item.drain()
         for link in routes + dg_links[0] + dg_links[1]:
             link.sent()
@@ -502,10 +516,14 @@
         return pltpu.make_async_copy(dy_in.at[:, cols], dy.at[:, cols], d_sems.at[n])
 
     g_load = pltpu.make_async_copy(g_in, g, g_sem)
-    for copy in (x_load(0), load(0, 0), load(0, 1), load(0, 2), dy_load(0), g_load):
-        copy.start()
+    x_load(0).start()
+    load(0, 0).start()
+    load(0, 1).start()
     for n in range(1, steps):
         x_load(n).start()
+    load(0, 2).start()
+    g_load.start()
+    for n in range(steps):
         dy_load(n).start()
     for e in range(1, exp_loc):
         for k in range(3):
@@ -516,70 +534,75 @@
     for copy in take:
         copy.start()
 
-    def store(s, k):
-        e, n = lax.div(s, steps), lax.rem(s, steps)
-        slot = lax.rem(s, slots)
-        part = pl.ds(pl.multiple_of(n * width, LANES), width)
+    def store(e, n, k):
+        part = pl.ds(n * width, width)
+        n = lax.rem(e, 2) * steps + n
         if k == 2:
-            return pltpu.make_async_copy(sd.at[slot], dwd.at[e, :, part], o_sems.at[slot, k])
-        return pltpu.make_async_copy((sg, su)[k].at[slot], (dwg, dwu)[k].at[e, part, :], o_sems.at[slot, k])
+            return pltpu.make_async_copy(sd.at[n], dwd.at[e, :, part], o_sems.at[n, k])
+        return pltpu.make_async_copy((sg, su)[k].at[n], (dwg, dwu)[k].at[e, part, :], o_sems.at[n, k])
 
     lane = lax.broadcasted_iota(jnp.int32, g.shape, 1)
 
-    def step(s, _):
-        e, n = lax.div(s, steps), lax.rem(s, steps)
-        slot = lax.rem(s, slots)
-        for k in range(steps):
-            @pl.when(s == k)
-            def _():
-                x_load(k).wait()
-
-        @pl.when(n == 0)
+    def down(e):
+        gate = jnp.sum(jnp.where(lane == e, g[...], 0.0), axis=1, keepdims=True)
+        for n in range(steps):
+            part = pl.ds(n * width, width)
+            sd[lax.rem(e, 2) * steps + n] = dot_nn(ht[e], (gate * dy[:, part].astype(F32)).astype(BF16))
+            store(e, n, 2).start()
+
+    def step(e, _):
+        @pl.when(e == 0)
         def _():
             load(e, 0).wait()
             load(e, 1).wait()
-
-        @pl.when(s >= slots)
+            for n in range(steps):
+                x_load(n).wait()
+
+        @pl.when(e > 0)
         def _():
             for k in range(3):
-                store(s - slots, k).wait()
-
-        part = pl.ds(pl.multiple_of(n * width, LANES), width)
-        sg[slot] = dot_nn(xt[part, :], da[e])
-        store(s, 0).start()
-        su[slot] = dot_nn(xt[part, :], db[e])
-        store(s, 1).start()
-
-        @pl.when(n == 0)
+                load(e, k).wait()
+
+        @pl.when(e > 1)
+        def _():
+            for n in range(steps):
+                for k in range(2):
+                    store(e - 2, n, k).wait()
+
+        for n in range(steps):
+            part = pl.ds(n * width, width)
+            sg[lax.rem(e, 2) * steps + n] = dot_nn(xt[part, :], da[e])
+            store(e, n, 0).start()
+            su[lax.rem(e, 2) * steps + n] = dot_nn(xt[part, :], db[e])
+            store(e, n, 1).start()
+
+        @pl.when(e == 0)
         def _():
             load(e, 2).wait()
-
-        @pl.when(s == 0)
+            g_load.wait()
+            for n in range(steps):
+                dy_load(n).wait()
+
+        @pl.when(e > 1)
         def _():
-            g_load.wait()
-
-        @pl.when(s == 3)
+            for n in range(steps):
+                store(e - 2, n, 2).wait()
+
+        @pl.when(e == 1)
         def _():
             for copy in take:
                 copy.wait()
             for copy in give:
                 copy.start()
 
-        for k in range(steps):
-            @pl.when(s == k)
-            def _():
-                dy_load(k).wait()
-
-        gate = jnp.sum(jnp.where(lane == e, g[...], 0.0), axis=1, keepdims=True)
-        d_o = (gate * dy[:, part].astype(F32)).astype(BF16)
-        sd[slot] = dot_nn(ht[e], d_o)
-        store(s, 2).start()
+        down(e)
         return 0
 
-    lax.fori_loop(0, exp_loc * steps, step, 0)
-    for s in range(exp_loc * steps - slots, exp_loc * steps):
-        for k in range(3):
-            store(jnp.int32(s), k).wait()
+    lax.fori_loop(0, exp_loc, step, 0)
+    for e in (exp_loc - 2, exp_loc - 1):
+        for n in range(steps):
+            for k in range(3):
+                store(jnp.int32(e), n, k).wait()
     for copy in give:
         copy.wait()
 
@@ -596,9 +619,6 @@
         heads, head_dim = w_query.shape[1], w_query.shape[2]
         kv_dim = w_key.shape[1] * head_dim
         q_dim = heads * head_dim
-        ids = jnp.arange(NUM_DEV * exp_loc, dtype=jnp.int32).reshape(NUM_DEV, exp_loc, 1, 1)
-        table = jnp.sum(jnp.where(expert_idx.T[None, None] == ids, gate_vals.T[None, None], 0.0), axis=2)
-        table = jnp.pad(table, ((0, 0), (0, 8 - exp_loc), (0, LANES - tok)))
         wq = w_query.transpose(1, 2, 0).reshape(q_dim, d_model)
         wk = w_key.transpose(1, 2, 0).reshape(kv_dim, d_model)
         wv = w_value.transpose(1, 2, 0).reshape(kv_dim, d_model)
@@ -610,7 +630,7 @@
         total = tok * NUM_DEV
 
         def half_shapes():
-            return [pltpu.VMEM((HALVES,) + s.shape, s.dtype) for s in scatter_shapes(r, d_model)]
+            return [pltpu.VMEM((HALVES, d_model // 512) + s.shape, s.dtype) for s in scatter_shapes(r, 512)]
 
         y, dx, attn, dgt, xt, dy_all, da, db, ht, gates = pl.pallas_call(
             kernel,
@@ -622,19 +642,20 @@
             scratch_shapes=[pltpu.VMEM((HALVES, m, d_model), BF16), pltpu.VMEM((HALVES, m, d_model), BF16), pltpu.VMEM((total, d_model), BF16),
                             pltpu.VMEM((NUM_DEV, 8, LANES), F32), pltpu.VMEM((HALVES, m, LANES), F32),
                             pltpu.VMEM((exp_loc, d_model, d_ff), BF16), pltpu.VMEM((exp_loc, d_model, d_ff), BF16), pltpu.VMEM((exp_loc, d_ff, d_model), BF16),
-                            pltpu.VMEM((HALVES, m, d_model), F32), pltpu.VMEM((HALVES, m, d_model), F32), pltpu.VMEM((total, d_model), F32), pltpu.VMEM((q_dim + 2 * kv_dim, d_model), BF16), pltpu.VMEM((q_dim, d_model), BF16),
+                            pltpu.VMEM((HALVES, m, d_model), F32), pltpu.VMEM((HALVES, m, d_model), F32), pltpu.VMEM((total, d_model), F32), pltpu.VMEM((q_dim + 2 * kv_dim, d_model), BF16), pltpu.VMEM((q_dim, d_model), BF16), pltpu.VMEM((2 * tok, q_dim + 2 * kv_dim), BF16),
                             pltpu.VMEM((exp_loc, m, d_ff), F32), pltpu.VMEM((exp_loc, m, d_ff), F32), pltpu.VMEM((m, d_model), BF16),
-                            pltpu.VMEM((HALVES, m, LANES), F32), pltpu.VMEM((HALVES, 2, 8, LANES), F32), pltpu.VMEM((2 * HALVES, 2, m, d_ff), BF16),
-                            pltpu.VMEM((m, d_ff), BF16), pltpu.VMEM((2 * HALVES, d_ff, m), BF16), pltpu.VMEM((d_model, total), BF16), pltpu.VMEM((NUM_DEV, HALVES, 8, LANES), F32)]
+                            pltpu.VMEM((HALVES, m, LANES), F32), pltpu.VMEM((HALVES, 2, 8, LANES), F32), pltpu.VMEM((exp_loc, m, d_ff), BF16), pltpu.VMEM((exp_loc, m, d_ff), BF16),
+                            pltpu.VMEM((exp_loc, m, d_ff), BF16), pltpu.VMEM((2 * HALVES, d_ff, m), BF16), pltpu.VMEM((d_model, total), BF16), pltpu.VMEM((NUM_DEV, HALVES, 8, LANES), F32), pltpu.VMEM((NUM_DEV, 8, LANES), F32), pltpu.VMEM((HALVES, exp_loc, m, LANES), F32)]
             + half_shapes() + half_shapes() + scatter_shapes(tok, d_model)
             + [pltpu.SemaphoreType.DMA((NUM_LINKS,)), pltpu.SemaphoreType.DMA((NUM_LINKS,)), pltpu.SemaphoreType.DMA((exp_loc, 3)),
-               pltpu.SemaphoreType.DMA((5,)), pltpu.SemaphoreType.DMA((4,)), pltpu.SemaphoreType.DMA((3,)), pltpu.SemaphoreType.DMA((2 * HALVES, 3))],
+               pltpu.SemaphoreType.DMA((5,)), pltpu.SemaphoreType.DMA((4,)), pltpu.SemaphoreType.DMA((3,)), pltpu.SemaphoreType.DMA((2 * HALVES,)), pltpu.SemaphoreType.DMA((exp_loc, 2))],
             compiler_params=pltpu.CompilerParams(collective_id=0, has_side_effects=True, vmem_limit_bytes=67000000),
             name='layer',
-        )(x_tokens, dy_tokens, x_attn.reshape(tok, d_model), table, expert_idx.T, w_gate, w_up, w_down, wq, wk, wv, wo)
-
-        width, slots = 512, 4
+        )(x_tokens, dy_tokens, x_attn.reshape(tok, d_model), expert_idx.T, gate_vals.T, w_gate, w_up, w_down, wq, wk, wv, wo)
+
+        width = 512
         steps = d_model // width
+        slots = 2 * steps
         small = (y, dx, attn, dgt)
         dw_gate, dw_up, dw_down, y, dx, attn, dgt = pl.pallas_call(
             functools.partial(weight_grads, width, slots),

time: 101 us -> 92.1 us (0.912)
  Pallas kernels: 98.7 us -> 91.1 us
    pallas_call x1, Pallas kernels: 75.5 us -> 71 us  [local_step(): pl.pallas_call(kernel, out_shape=(shape((tok, d_model), BF16), shape((tok...]
    pallas_call x1, Pallas kernels: 23.2 us -> 20.1 us  [local_step(): pl.pallas_call(functools.partial(weight_grads, width, slots), out_shape=(...]
where the time goes in v4:
time: 92.1 us; the launch traced here: 91.9 us
  Pallas kernels  91.1 us (99%)
    pallas_call x1, Pallas kernels, local_step(): pl.pallas_call(kernel, out_shape=(shape((tok, d_model), BF16), shape((tok...  71 us
    pallas_call x1, Pallas kernels, local_step(): pl.pallas_call(functools.partial(weight_grads, width, slots), out_shape=(...  20.1 us

profile of v4, /device:TPU:0, one launch (start us, length us, event | category | flops | bytes accessed | tf_op | source)
XLA Modules:
  0.0 91.9 jit_solution(8486552803539724645)
XLA Ops:
  0.6 71.0 %layer.1 = (bf16[64,1536]{1,0:T(8,128)(2,1)}, bf16[64,1536]{1,0:T(8,128)(2,1)}, bf16[64,1536]{1,0:T(8,128)(2,1)}, f32[8,64]{1,0:T(8,128)}, bf16[1536,512]{1,0:T(...) custom-call(bf16[64,1536]{1,0:T(8,128)(2,1)} %x_in.1, ...), custom_call_target="tpu_custom_call" | custom-call | tf_op jit(solution)/shard_map/layer/pallas_call | solution.py:635
  71.7 20.1 %weight_grads.1 = (f32[5,1536,512]{2,1,0:T(8,128)}, f32[5,1536,512]{2,1,0:T(8,128)}, f32[5,512,1536]{2,1,0:T(8,128)}, bf16[64,1536]{1,0:T(8,128)(2,1)}, bf16[64,...) custom-call(bf16[1536,512]{1,0:T(8,128)(2,1)} %get-tuple-element.24.xt_in, ...), custom_call_target="tpu_custom_call" | custom-call | tf_op jit(solution)/shard_map/weight_grads/pallas_call | solution.py:660

commit v5 on v4

--- a/solution.py
+++ b/solution.py
@@ -98,13 +98,19 @@
         self.core_x = Link(pool, at('x'), at('x'), at('xc'), dev['c'])
         self.core_y = Link(pool, at('y'), at('y'), at('yc'), dev['c'])
         self.core_d = Link(pool, at('yx'), at('yx'), at('yxc'), dev['c'])
-        self.early = None
+        self.early = self.relayed = False
         self.links = (self.to_x, self.to_y, self.to_c, self.relay_x, self.relay_y, self.core_x, self.core_y, self.core_d)
 
-    def begin(self):
+    def begin_links(self):
         self.to_x.start()
         self.to_y.start()
+
+    def begin_core(self):
         self.to_c.start()
+
+    def begin(self):
+        self.begin_links()
+        self.begin_core()
 
     def after(self):
         self.early = True
@@ -119,6 +125,11 @@
         self.core_x.start()
         self.core_y.start()
 
+    def relay_left(self):
+        self.relayed = True
+        self.relay_x.sent()
+        self.relay_y.sent()
+
     def last(self):
         self.relay_x.arrive()
         self.relay_y.arrive()
@@ -131,8 +142,9 @@
         self.core_d.arrive()
 
     def drain(self):
-        for link in self.links[0 if self.early is None else 2:]:
-            link.sent()
+        for link in self.links:
+            if not (self.early and link in (self.to_x, self.to_y)) and not (self.relayed and link in (self.relay_x, self.relay_y)):
+                link.sent()
 
 
 class Scatter:
@@ -193,13 +205,40 @@
             link.sent()
 
 
+class ChipSum:
+    def __init__(self, pool, place, part, from_core, rows, first, outs, sems):
+        four = 4 * rows
+        self.part, self.from_core = part, from_core
+        self.mine = pl.multiple_of(place.core * four, 8)
+        self.cols = pl.ds(first, from_core.shape[-1])
+        other = part.at[pl.ds(pl.multiple_of((1 - place.core) * four, 8), four), self.cols]
+        self.core = Link(pool, other, from_core, from_core, place.dev['c'])
+        self.copies = [pltpu.make_async_copy(part.at[pl.ds(pl.multiple_of(place.block[name] * rows, 8), rows), self.cols], out.at[:, self.cols], sems.at[k])
+                       for k, (name, out) in enumerate(outs)]
+
+    def begin(self):
+        self.core.start()
+
+    def middle(self):
+        self.core.arrive()
+        mine = pl.ds(self.mine, self.from_core.shape[0])
+        self.part[mine, self.cols] = self.part[mine, self.cols] + self.from_core[...]
+        for copy in self.copies:
+            copy.start()
+
+    def drain(self):
+        self.core.sent()
+        for copy in self.copies:
+            copy.wait()
+
+
 def scatter_shapes(rows, width):
     half = rows // 2
     return [pltpu.VMEM((4 * rows, width), F32), pltpu.VMEM((2, half, width), F32), pltpu.VMEM((2, half, width), F32),
             pltpu.VMEM((half, width), F32), pltpu.VMEM((half, width), F32)]
 
 
-NUM_LINKS = 7 + 14 + 8 * 5 + 7 * 13
+NUM_LINKS = 7 + 14 + 8 * 5 + 7 * 7 + 6
 
 
 def attention_qkv(xa, wqkv, qkv, chip, seq):
@@ -236,10 +275,10 @@
     tiles = d_model // tile
 
     def kernel(x_in, dy_in, xa_in, idx_in, gate_in, wg_in, wu_in, wd_in, wq_in, wk_in, wv_in, wo_in,
-               y_out, dx_out, attn_out, dg_out, xt_all, dy_all, da_all, db_all, ht_all, gates_out,
+               y_out, dx_out, attn_out, dg_out, xt_all, dy_all, da_all, db_all, ht_all, gates_out, own_out, to_x_out, to_y_out, to_d_out,
                xb, dyb, xab, gtb, gcol, wg, wu, wd, y_part, dx_part, at_part, wqkv, wo, qkv, s1, s2, d_o, dgc, dgt, da, db, hid, stage_t, xt, dgl, gtab, gfull,
-               ry0, ry1, ry2, ry3, ry4, rd0, rd1, rd2, rd3, rd4, ra0, ra1, ra2, ra3, ra4,
-               send_sems, recv_sems, w_sems, in_sems, aw_sems, out_sems, stage_sems, grad_sems):
+               ryc, rdc, ry0, ry1, ry2, ry3, ry4, rd0, rd1, rd2, rd3, rd4, ra0, ra1, ra2, ra3, ra4,
+               send_sems, recv_sems, w_sems, in_sems, aw_sems, out_sems, stage_sems, grad_sems, sum_sems, res_sems, y_res, dx_res, attn_res, dg_res):
         place = Place()
         pool = Pool(send_sems, recv_sems)
         dev, block = place.dev, place.block
@@ -277,14 +316,20 @@
         gx = [Gather(pool, place, xb.at[h], r, block) for h in range(HALVES)]
         gdy = [Gather(pool, place, dyb.at[h], r, block) for h in range(HALVES)]
         gxa = Gather(pool, place, xab, tok, place.pair)
-        sy = [[Scatter(pool, place, y_part.at[h], ry0.at[h, n], ry1.at[h, n], ry2.at[h, n], ry3.at[h, n], ry4.at[h, n], r, n * tile) for n in range(tiles)] for h in range(HALVES)]
-        sdx = [[Scatter(pool, place, dx_part.at[h], rd0.at[h, n], rd1.at[h, n], rd2.at[h, n], rd3.at[h, n], rd4.at[h, n], r, n * tile) for n in range(tiles)] for h in range(HALVES)]
+        def passed(t):
+            return [(name, out.at[t]) for name, out in (('', own_out), ('x', to_x_out), ('y', to_y_out), ('yx', to_d_out))]
+
+        sy = [[Scatter(pool, place, y_part.at[0], ry0.at[n], ry1.at[n], ry2.at[n], ry3.at[n], ry4.at[n], r, n * tile) for n in range(tiles)],
+              [ChipSum(pool, place, y_part.at[1], ryc.at[n], r, n * tile, passed(0), sum_sems.at[0, n]) for n in range(tiles)]]
+        sdx = [[Scatter(pool, place, dx_part.at[0], rd0.at[n], rd1.at[n], rd2.at[n], rd3.at[n], rd4.at[n], r, n * tile) for n in range(tiles)],
+               [ChipSum(pool, place, dx_part.at[1], rdc.at[n], r, n * tile, passed(1), sum_sems.at[1, n]) for n in range(tiles)]]
         sat = Scatter(pool, place, at_part, ra0, ra1, ra2, ra3, ra4, tok)
         dg_links = [[Link(pool, dgt.at[h, 1 - place.core if 'c' in name else place.core], dgl.at[me, h], dgl.at[block[name], h], dev[name]) for name in peers] for h in range(HALVES)]
 
         for load in loads:
             load.wait()
-        gxa.begin()
+        gx[0].begin()
+        gxa.begin_core()
         for link in routes:
             link.start()
         gtb[me] = gtab[place.flat['']]
@@ -296,28 +341,17 @@
         for load in attn_loads:
             load.wait()
 
-        def pair(name, between=None):
-            attention_qkv(xab, wqkv, qkv, place.chips[name], tok)
+        def pairs(names, between=None):
+            for k, name in enumerate(names):
+                attention_qkv(xab, wqkv, qkv.at[k], place.chips[name], tok)
             if between is not None:
                 between()
-            attention_out(qkv, wo, at_part, place.chips[name], NUM_DEV // 2, attn_dims)
+            for k, name in enumerate(names):
+                attention_out(qkv.at[k], wo, at_part, place.chips[name], NUM_DEV // 2, attn_dims)
 
         gxa.to_c.arrive()
-        pair('')
-        gxa.after()
-        gx[0].begin()
-        gxa.relay()
-        gdy[0].begin()
-        gxa.core_x.arrive()
-        pair('x')
-        gxa.core_y.arrive()
-        pair('y', gx[0].relay)
-        gx[1].begin()
-        gxa.last()
-        gdy[0].relay()
-        gxa.core_d.arrive()
-        pair('yx', gx[0].last)
-        sat.begin()
+        pairs(('',))
+        gx[0].relay()
         for link in routes:
             link.arrive()
         wide = jnp.concatenate([gtb[...].reshape(NUM_DEV * 8, LANES), jnp.zeros((LANES - NUM_DEV * 8, LANES), F32)], axis=0).T
@@ -326,6 +360,9 @@
                 gcol[h, b * r:(b + 1) * r, 0:8] = wide[h * r:(h + 1) * r, b * 8:(b + 1) * 8]
             for e in range(exp_loc):
                 gfull[h, e] = jnp.broadcast_to(gcol[h][:, e:e + 1], (m, LANES))
+        gx[0].relay_left()
+        gxa.begin_links()
+        gx[0].last()
         gx[0].finish()
 
         def staged(h, e, k):
@@ -423,6 +460,23 @@
                 link.start()
             dgl[me, h] = dgt[h, place.core]
 
+        def dg_read():
+            for h in range(HALVES):
+                for link in dg_links[h]:
+                    link.arrive()
+            for h in range(HALVES):
+                slots = idx_in[:, h * r:(h + 1) * r]
+                total = jnp.zeros(slots.shape, F32)
+                for b in range(NUM_DEV):
+                    first = ((b // 2) % 2 * 4 + b % 2 * 2 + b // 4) * exp_loc
+                    rows = dgl[b, h]
+                    mine = jnp.zeros((8, r), F32)
+                    for q in range(LANES // r):
+                        mine = jnp.where(place.chip == q, rows[:, q * r:(q + 1) * r], mine)
+                    for e in range(exp_loc):
+                        total = jnp.where(slots == first + e, mine[e:e + 1, :], total)
+                dg_res[:, h * r:(h + 1) * r] = total
+
         def seq(*calls):
             def run():
                 for call in calls:
@@ -430,57 +484,48 @@
 
             return run
 
-        loop(exp_loc, {0: gdy[1].begin, 1: seq(gdy[0].last, gx[1].relay), 2: sat.middle, 4: seq(gdy[1].relay, gx[1].last)}, hidden(0))
+        loop(exp_loc, {2: gdy[0].begin, 3: gxa.relay}, hidden(0))
+        gxa.core_x.arrive()
+        gxa.core_y.arrive()
+        pairs(('x', 'y'), gdy[0].relay)
+        gx[1].begin()
+        gxa.last()
+        gdy[1].begin()
+        gxa.core_d.arrive()
+        pairs(('yx',), gdy[0].last)
+        sat.begin()
         gdy[0].finish()
-        loop(tiles, {1: sy[0][0].begin, 2: sy[0][1].begin}, outputs(0))
+        loop(tiles, {1: seq(gx[1].relay, sy[0][0].begin), 2: seq(gdy[1].relay, sat.middle, sy[0][1].begin)}, outputs(0))
         sy[0][2].begin()
         send_dg(0)
-        gx[1].finish()
-        loop(exp_loc, {1: sy[0][0].middle, 3: sy[0][1].middle, 4: sy[0][2].middle}, hidden_grads(0))
-        loop(tiles, {1: sdx[0][0].begin, 2: seq(sdx[0][1].begin, sat.late)}, input_grads(0))
+        loop(exp_loc, {1: sy[0][0].middle, 2: gx[1].last, 3: sy[0][1].middle, 4: sy[0][2].middle}, hidden_grads(0))
+        loop(tiles, {1: seq(gx[1].finish, sdx[0][0].begin), 2: seq(gdy[1].last, sdx[0][1].begin)}, input_grads(0))
         sdx[0][2].begin()
-        loop(exp_loc, {0: gdy[1].last, 1: seq(sdx[0][0].middle, sdx[0][1].middle, sy[0][0].late), 2: seq(gdy[1].finish, sdx[0][2].middle, sy[0][1].late),
-                       3: sy[0][2].late, 4: functools.partial(sat.finish, attn_out)}, hidden(1))
-        loop(tiles, {1: sy[1][0].begin, 2: seq(sy[1][1].begin, sdx[0][0].late)}, outputs(1))
+        loop(exp_loc, {1: seq(sdx[0][0].middle, sdx[0][1].middle), 2: seq(gdy[1].finish, sdx[0][2].middle)}, hidden(1))
+        sat.late()
+        loop(tiles, {1: seq(sy[0][0].late, sy[1][0].begin), 2: seq(sy[0][1].late, sy[0][2].late, sy[1][1].begin)}, outputs(1))
         sy[1][2].begin()
         send_dg(1)
-        sdx[0][1].late()
-        loop(exp_loc, {1: sy[1][0].middle, 2: sdx[0][2].late, 3: seq(sy[1][1].middle, sy[1][2].middle), 4: seq(*[functools.partial(s.finish, y_out) for s in sy[0]])}, hidden_grads(1))
-        loop(tiles, {1: sdx[1][0].begin, 2: seq(sdx[1][1].begin, sdx[1][0].middle, sy[1][0].late)}, input_grads(1))
-        sdx[1][2].begin()
-        sdx[1][1].middle()
-        sy[1][1].late()
-        sy[1][2].late()
-        sdx[1][2].middle()
         for h in range(HALVES):
             xt[:, h * m:(h + 1) * m] = xb[h].T
         saves = [pltpu.make_async_copy(xt, xt_all, out_sems.at[0]), pltpu.make_async_copy(dyb, dy_all, out_sems.at[1]), pltpu.make_async_copy(gcol, gates_out, out_sems.at[2])]
         for save in saves:
             save.start()
+        loop(exp_loc, {1: sy[1][0].middle, 2: sdx[0][0].late, 3: seq(sy[1][1].middle, sy[1][2].middle), 4: sdx[0][1].late}, hidden_grads(1))
+        loop(tiles, {1: seq(sdx[1][0].begin, sdx[0][2].late), 2: seq(sdx[1][1].begin, sdx[1][0].middle)}, input_grads(1))
+        sdx[1][2].begin()
+        sdx[1][1].middle()
+        for s in sy[0]:
+            s.finish(y_res)
+        sat.finish(attn_res)
         for s in sdx[0]:
-            s.finish(dx_out)
-        for s in sdx[1]:
-            s.late()
-        for h in range(HALVES):
-            for link in dg_links[h]:
-                link.arrive()
-        for h in range(HALVES):
-            slots = idx_in[:, h * r:(h + 1) * r]
-            total = jnp.zeros(slots.shape, F32)
-            for b in range(NUM_DEV):
-                first = ((b // 2) % 2 * 4 + b % 2 * 2 + b // 4) * exp_loc
-                rows = dgl[b, h]
-                mine = jnp.zeros((8, r), F32)
-                for q in range(LANES // r):
-                    mine = jnp.where(place.chip == q, rows[:, q * r:(q + 1) * r], mine)
-                for e in range(exp_loc):
-                    total = jnp.where(slots == first + e, mine[e:e + 1, :], total)
-            dg_out[:, h * r:(h + 1) * r] = total
-        for s in sy[1]:
-            s.finish(y_out, r)
-        for s in sdx[1]:
-            s.finish(dx_out, r)
-        for save in saves:
+            s.finish(dx_res)
+        dg_read()
+        results = [pltpu.make_async_copy(src, dst, res_sems.at[k]) for k, (src, dst) in enumerate(((y_res, y_out), (dx_res, dx_out), (attn_res, attn_out), (dg_res, dg_out)))]
+        for result in results:
+            result.start()
+        sdx[1][2].middle()
+        for save in saves + results:
             save.wait()
         for e in range(exp_loc):
             for k in range(2):
@@ -497,9 +542,9 @@
     return kernel, r, m
 
 
-def weight_grads(width, slots, xt_in, dy_in, g_in, da_in, db_in, ht_in, y_in, dx_in, at_in, dg_in,
-                 dwg, dwu, dwd, y_out, dx_out, at_out, dg_out,
-                 xt, dy, g, da, db, ht, sg, su, sd, y, dx, at, dg, x_sems, d_sems, g_sem, e_sems, o_sems, p_sems):
+def weight_grads(width, slots, xt_in, dy_in, g_in, da_in, db_in, ht_in, at_in, dg_in, y_in, dx_in,
+                 dwg, dwu, dwd, at_out, dg_out, y_out, dx_out,
+                 xt, dy, g, da, db, ht, sg, su, sd, at, dg, y, dx, x_sems, d_sems, g_sem, e_sems, o_sems, p_sems):
     exp_loc = da.shape[0]
     steps = dy.shape[1] // width
 
@@ -528,7 +573,8 @@
     for e in range(1, exp_loc):
         for k in range(3):
             load(e, k).start()
-    passing = ((y_in, y, y_out), (dx_in, dx, dx_out), (at_in, at, at_out), (dg_in, dg, dg_out))
+    rows = slice(0, y.shape[0])
+    passing = ((at_in, at, at_out), (dg_in, dg, dg_out), (y_in, y, y_out.at[rows, :]), (dx_in, dx, dx_out.at[rows, :]))
     take = [pltpu.make_async_copy(src, mid, p_sems.at[k, 0]) for k, (src, mid, _) in enumerate(passing)]
     give = [pltpu.make_async_copy(mid, dst, p_sems.at[k, 1]) for k, (_, mid, dst) in enumerate(passing)]
     for copy in take:
@@ -630,25 +676,26 @@
         total = tok * NUM_DEV
 
         def half_shapes():
-            return [pltpu.VMEM((HALVES, d_model // 512) + s.shape, s.dtype) for s in scatter_shapes(r, 512)]
-
-        y, dx, attn, dgt, xt, dy_all, da, db, ht, gates = pl.pallas_call(
+            return [pltpu.VMEM((d_model // 512,) + s.shape, s.dtype) for s in scatter_shapes(r, 512)]
+
+        y0, dx0, attn, dgt, xt, dy_all, da, db, ht, gates, own, to_x, to_y, to_d = pl.pallas_call(
             kernel,
-            out_shape=(shape((tok, d_model), BF16), shape((tok, d_model), BF16), shape((tok, d_model), BF16), shape((top_k, tok), F32),
+            out_shape=(shape((r, d_model), BF16), shape((r, d_model), BF16), shape((tok, d_model), BF16), shape((top_k, tok), F32),
                        shape((d_model, total), BF16), shape((HALVES, m, d_model), BF16),
-                       shape((exp_loc, total, d_ff), BF16), shape((exp_loc, total, d_ff), BF16), shape((exp_loc, d_ff, total), BF16), shape((HALVES, m, LANES), F32)),
+                       shape((exp_loc, total, d_ff), BF16), shape((exp_loc, total, d_ff), BF16), shape((exp_loc, d_ff, total), BF16), shape((HALVES, m, LANES), F32)) + (shape((2, r, d_model), F32),) * 4,
             in_specs=[any_spec, any_spec, any_spec, vmem_spec, vmem_spec] + [any_spec] * 7,
-            out_specs=(vmem_spec,) * 4 + (any_spec,) * 6,
+            out_specs=(any_spec,) * 14,
             scratch_shapes=[pltpu.VMEM((HALVES, m, d_model), BF16), pltpu.VMEM((HALVES, m, d_model), BF16), pltpu.VMEM((total, d_model), BF16),
                             pltpu.VMEM((NUM_DEV, 8, LANES), F32), pltpu.VMEM((HALVES, m, LANES), F32),
                             pltpu.VMEM((exp_loc, d_model, d_ff), BF16), pltpu.VMEM((exp_loc, d_model, d_ff), BF16), pltpu.VMEM((exp_loc, d_ff, d_model), BF16),
-                            pltpu.VMEM((HALVES, m, d_model), F32), pltpu.VMEM((HALVES, m, d_model), F32), pltpu.VMEM((total, d_model), F32), pltpu.VMEM((q_dim + 2 * kv_dim, d_model), BF16), pltpu.VMEM((q_dim, d_model), BF16), pltpu.VMEM((2 * tok, q_dim + 2 * kv_dim), BF16),
+                            pltpu.VMEM((HALVES, m, d_model), F32), pltpu.VMEM((HALVES, m, d_model), F32), pltpu.VMEM((total, d_model), F32), pltpu.VMEM((q_dim + 2 * kv_dim, d_model), BF16), pltpu.VMEM((q_dim, d_model), BF16), pltpu.VMEM((2, 2 * tok, q_dim + 2 * kv_dim), BF16),
                             pltpu.VMEM((exp_loc, m, d_ff), F32), pltpu.VMEM((exp_loc, m, d_ff), F32), pltpu.VMEM((m, d_model), BF16),
                             pltpu.VMEM((HALVES, m, LANES), F32), pltpu.VMEM((HALVES, 2, 8, LANES), F32), pltpu.VMEM((exp_loc, m, d_ff), BF16), pltpu.VMEM((exp_loc, m, d_ff), BF16),
                             pltpu.VMEM((exp_loc, m, d_ff), BF16), pltpu.VMEM((2 * HALVES, d_ff, m), BF16), pltpu.VMEM((d_model, total), BF16), pltpu.VMEM((NUM_DEV, HALVES, 8, LANES), F32), pltpu.VMEM((NUM_DEV, 8, LANES), F32), pltpu.VMEM((HALVES, exp_loc, m, LANES), F32)]
-            + half_shapes() + half_shapes() + scatter_shapes(tok, d_model)
+            + [pltpu.VMEM((d_model // 512, 4 * r, 512), F32)] * 2 + half_shapes() + half_shapes() + scatter_shapes(tok, d_model)
             + [pltpu.SemaphoreType.DMA((NUM_LINKS,)), pltpu.SemaphoreType.DMA((NUM_LINKS,)), pltpu.SemaphoreType.DMA((exp_loc, 3)),
-               pltpu.SemaphoreType.DMA((5,)), pltpu.SemaphoreType.DMA((4,)), pltpu.SemaphoreType.DMA((3,)), pltpu.SemaphoreType.DMA((2 * HALVES,)), pltpu.SemaphoreType.DMA((exp_loc, 2))],
+               pltpu.SemaphoreType.DMA((5,)), pltpu.SemaphoreType.DMA((4,)), pltpu.SemaphoreType.DMA((3,)), pltpu.SemaphoreType.DMA((2 * HALVES,)), pltpu.SemaphoreType.DMA((exp_loc, 2)), pltpu.SemaphoreType.DMA((2, d_model // 512, 4)), pltpu.SemaphoreType.DMA((4,)),
+               pltpu.VMEM((r, d_model), BF16), pltpu.VMEM((r, d_model), BF16), pltpu.VMEM((tok, d_model), BF16), pltpu.VMEM((top_k, tok), F32)],
             compiler_params=pltpu.CompilerParams(collective_id=0, has_side_effects=True, vmem_limit_bytes=67000000),
             name='layer',
         )(x_tokens, dy_tokens, x_attn.reshape(tok, d_model), expert_idx.T, gate_vals.T, w_gate, w_up, w_down, wq, wk, wv, wo)
@@ -656,10 +703,17 @@
         width = 512
         steps = d_model // width
         slots = 2 * steps
-        small = (y, dx, attn, dgt)
-        dw_gate, dw_up, dw_down, y, dx, attn, dgt = pl.pallas_call(
+        small = (attn, dgt, y0, dx0)
+
+        def swap(value, flip_y, flip_x):
+            eo_size = mesh.shape['eo']
+            pairs = [(g, (g // eo_size ^ flip_y) * eo_size + (g % eo_size ^ 2 * flip_x)) for g in range(NUM_DEV)]
+            return lax.ppermute(value, GROUP_AXES, pairs)
+
+        from_x, from_y, from_d = swap(to_x, 0, 1), swap(to_y, 1, 0), swap(to_d, 1, 1)
+        dw_gate, dw_up, dw_down, attn, dgt, y, dx = pl.pallas_call(
             functools.partial(weight_grads, width, slots),
-            out_shape=(shape((exp_loc, d_model, d_ff), F32), shape((exp_loc, d_model, d_ff), F32), shape((exp_loc, d_ff, d_model), F32)) + tuple(shape(v.shape, v.dtype) for v in small),
+            out_shape=(shape((exp_loc, d_model, d_ff), F32), shape((exp_loc, d_model, d_ff), F32), shape((exp_loc, d_ff, d_model), F32)) + tuple(shape((tok, d_model) if v is y0 or v is dx0 else v.shape, v.dtype) for v in small),
             in_specs=[any_spec] * 10,
             out_specs=(any_spec,) * 7,
             scratch_shapes=[pltpu.VMEM((d_model, total), BF16), pltpu.VMEM((total, d_model), BF16), pltpu.VMEM((total, LANES), F32),
@@ -668,9 +722,11 @@
             + [pltpu.VMEM(v.shape, v.dtype) for v in small]
             + [pltpu.SemaphoreType.DMA((steps,)), pltpu.SemaphoreType.DMA((steps,)), pltpu.SemaphoreType.DMA(()), pltpu.SemaphoreType.DMA((exp_loc, 3)),
                pltpu.SemaphoreType.DMA((slots, 3)), pltpu.SemaphoreType.DMA((4, 2))],
-            compiler_params=pltpu.CompilerParams(vmem_limit_bytes=66000000),
+            compiler_params=pltpu.CompilerParams(vmem_limit_bytes=64500000),
+            cost_estimate=pl.CostEstimate(flops=3 * 2 * total * d_model * d_ff * exp_loc, bytes_accessed=3 * 4 * exp_loc * d_model * d_ff, transcendentals=0),
             name='weight_grads',
-        )(xt, dy_all.reshape(total, d_model), gates.reshape(total, LANES), da, db, ht, y, dx, attn, dgt)
+        )(xt, dy_all.reshape(total, d_model), gates.reshape(total, LANES), da, db, ht, attn, dgt, y0, dx0)
+        y, dx = (lax.dynamic_update_slice(whole, (own[t] + from_x[t] + from_y[t] + from_d[t]).astype(BF16), (r, 0)) for t, whole in enumerate((y, dx)))
         return y, dx, dgt.T, dw_gate, dw_up, dw_down, attn.reshape(x_attn.shape)
 
     spec_rows = P(TOKEN_AXES, None)

time: 92.1 us -> 86.5 us (0.939)
  Pallas kernels: 91.1 us -> 81.4 us
  starting transfers between devices: 0 us -> 3.51 us
    pallas_call x1, Pallas kernels: 71 us -> 61.4 us  [local_step(): pl.pallas_call(kernel, out_shape=(shape((r, d_model), BF16), shape((r, d_...]
    ppermute x0 -> x3, starting transfers between devices: none -> 3.51 us  [swap(): return lax.ppermute(value, GROUP_AXES, pairs)]
  transfers between devices with their start and end apart: 0 -> 3, of which waited for: 0 -> 0; matrix products, arithmetic and copies ran while one was open for 0% -> 0% of each run, Pallas kernels for 0% -> 23%
where the time goes in v5:
time: 86.5 us; the launch traced here: 86.4 us
  Pallas kernels  81.4 us (94%)
  starting transfers between devices  3.51 us (4%)
    pallas_call x1, Pallas kernels, local_step(): pl.pallas_call(kernel, out_shape=(shape((r, d_model), BF16), shape((r, d_...  61.4 us
    pallas_call x1, Pallas kernels, local_step(): pl.pallas_call(functools.partial(weight_grads, width, slots), out_shape=(...  20 us
    ppermute x3, starting transfers between devices, swap(): return lax.ppermute(value, GROUP_AXES, pairs)  3.51 us
  transfers between devices with their start and end apart: 3, of which 0 were waited for; matrix products, arithmetic and copies ran while one was open for 0% of the time, Pallas kernels for 23%

profile of v5, /device:TPU:0, one launch (start us, length us, event | category | flops | bytes accessed | tf_op | source)
XLA Modules:
  0.0 86.4 jit_solution(13127445882822077257)
XLA Ops:
  0.6 61.4 %layer.1 = (bf16[32,1536]{1,0:T(8,128)(2,1)}, bf16[32,1536]{1,0:T(8,128)(2,1)}, bf16[64,1536]{1,0:T(8,128)(2,1)}, f32[8,64]{1,0:T(8,128)}, bf16[1536,512]{1,0:T(...) custom-call(bf16[64,1536]{1,0:T(8,128)(2,1)} %x_in.1, ...), custom_call_target="tpu_custom_call" | custom-call | tf_op jit(solution)/shard_map/layer/pallas_call | solution.py:681
  62.0 0.7 collective-permute-start
  62.7 1.3 %collective-permute-start.1 = (f32[2,32,1536]{2,1,0:T(8,128)}, f32[2,32,1536]{2,1,0:T(8,128)S(1)}, u32[]{:S(2)}, u32[]{:S(2)}) collective-permute-start(f32[2,32,1536]{2,1,0:T(8,128)} %get-tuple-element.41), channel_id=1, source_target_pairs={{0,4},{1,5},{2,6},{3,7},{4,0},{5,1},{6,2},{7,3}} | collective-permute-start | bytes 1179656 | tf_op jit(solution)/shard_map/ppermute | solution.py:711
  64.1 1.5 %collective-permute-start.2 = (f32[2,32,1536]{2,1,0:T(8,128)}, f32[2,32,1536]{2,1,0:T(8,128)S(1)}, u32[]{:S(2)}, u32[]{:S(2)}) collective-permute-start(f32[2,32,1536]{2,1,0:T(8,128)} %get-tuple-element.42), channel_id=1, source_target_pairs={{0,6},{1,7},{2,4},{3,5},{4,2},{5,3},{6,0},{7,1}} | collective-permute-start | bytes 1179656 | tf_op jit(solution)/shard_map/ppermute | solution.py:711
  65.5 0.0 copy-start
  65.5 20.0 %weight_grads.1 = (f32[5,1536,512]{2,1,0:T(8,128)}, f32[5,1536,512]{2,1,0:T(8,128)}, f32[5,512,1536]{2,1,0:T(8,128)}, bf16[64,1536]{1,0:T(8,128)(2,1)}, f32[8,64...) custom-call(bf16[1536,512]{1,0:T(8,128)(2,1)} %get-tuple-element.28.xt_in, ...), custom_call_target="tpu_custom_call" | custom-call | flops 12079595520 | bytes 47185920 | tf_op jit(solution)/shard_map/weight_grads/pallas_call | solution.py:714
  85.6 0.0 collective-permute-done
  85.6 0.0 collective-permute-done.1
  85.6 0.0 collective-permute-done.2
  85.6 0.0 copy-done
  85.6 0.8 fusion.5
Async XLA Ops:
  62.0 23.6 %collective-permute-start = (f32[2,32,1536]{2,1,0:T(8,128)}, f32[2,32,1536]{2,1,0:T(8,128)S(1)}, u32[]{:S(2)}, u32[]{:S(2)}) collective-permute-start(f32[2,32,1536]{2,1,0:T(8,128)} %get-tuple-element.40), channel_id=1, source_target_pairs={{0,2},{1,3},{2,0},{3,1},{4,6},{5,7},{6,4},{7,5}} | collective-permute-start | bytes 1179656 | tf_op jit(solution)/shard_map/ppermute | solution.py:711
  62.7 22.9 %collective-permute-start.1 = (f32[2,32,1536]{2,1,0:T(8,128)}, f32[2,32,1536]{2,1,0:T(8,128)S(1)}, u32[]{:S(2)}, u32[]{:S(2)}) collective-permute-start(f32[2,32,1536]{2,1,0:T(8,128)} %get-tuple-element.41), channel_id=1, source_target_pairs={{0,4},{1,5},{2,6},{3,7},{4,0},{5,1},{6,2},{7,3}} | collective-permute-start | bytes 1179656 | tf_op jit(solution)/shard_map/ppermute | solution.py:711
  64.1 21.5 %collective-permute-start.2 = (f32[2,32,1536]{2,1,0:T(8,128)}, f32[2,32,1536]{2,1,0:T(8,128)S(1)}, u32[]{:S(2)}, u32[]{:S(2)}) collective-permute-start(f32[2,32,1536]{2,1,0:T(8,128)} %get-tuple-element.42), channel_id=1, source_target_pairs={{0,6},{1,7},{2,4},{3,5},{4,2},{5,3},{6,0},{7,1}} | collective-permute-start | bytes 1179656 | tf_op jit(solution)/shard_map/ppermute | solution.py:711
  65.5 20.1 %copy-start = (f32[2,32,1536]{2,1,0:T(8,128)S(1)}, f32[2,32,1536]{2,1,0:T(8,128)}, u32[]{:S(2)}) copy-start(f32[2,32,1536]{2,1,0:T(8,128)} %get-tuple-element.39) | copy-start | bytes 1179652

commit v6 on v5

--- a/solution.py
+++ b/solution.py
@@ -56,50 +56,45 @@
                     self.chips[name] = yy * 2 + xx
 
 
-class Link:
-    def __init__(self, pool, src, dst, land, device):
-        send, recv = pool.take()
-        self.out = pltpu.make_async_remote_copy(src_ref=src, dst_ref=dst, send_sem=send, recv_sem=recv, device_id=device, device_id_type=MESH_ID)
-        self.inn = pltpu.make_async_remote_copy(src_ref=land, dst_ref=land, send_sem=send, recv_sem=recv, device_id=device, device_id_type=MESH_ID)
-
-    def start(self):
-        self.out.start()
-
-    def arrive(self):
-        self.inn.wait_recv()
-
-    def sent(self):
-        self.out.wait_send()
-
-
 class Pool:
-    def __init__(self, sends, recvs):
-        self.sends, self.recvs, self.used = sends, recvs, 0
+    def __init__(self, sems):
+        self.sems, self.used = sems, 0
 
     def take(self):
-        k = self.used
         self.used += 1
-        return self.sends.at[k], self.recvs.at[k]
+        return self.sems.at[self.used - 1]
+
+
+def send(src, dst, device, sent, landed):
+    return pltpu.make_async_remote_copy(src_ref=src, dst_ref=dst, send_sem=sent, recv_sem=landed, device_id=device, device_id_type=MESH_ID)
+
+
+def wait_for(ref, sem):
+    pltpu.make_async_copy(ref, ref, sem).wait()
 
 
 class Gather:
-    def __init__(self, pool, place, buf, rows, index):
+    def __init__(self, pool, place, buf, rows, index, split=False):
         def at(name, lo=0, n=rows):
             return buf.at[pl.ds(pl.multiple_of(index[name] * rows + lo, 8), n), :]
 
         half = rows // 2
         own = at('')
         dev = place.dev
-        self.to_x = Link(pool, own, own, at('x'), dev['x'])
-        self.to_y = Link(pool, own, own, at('y'), dev['y'])
-        self.to_c = Link(pool, own, own, at('c'), dev['c'])
-        self.relay_x = Link(pool, at('y', 0, half), at('y', 0, half), at('yx', 0, half), dev['x'])
-        self.relay_y = Link(pool, at('x', half, half), at('x', half, half), at('yx', half, half), dev['y'])
-        self.core_x = Link(pool, at('x'), at('x'), at('xc'), dev['c'])
-        self.core_y = Link(pool, at('y'), at('y'), at('yc'), dev['c'])
-        self.core_d = Link(pool, at('yx'), at('yx'), at('yxc'), dev['c'])
-        self.early = self.relayed = False
-        self.links = (self.to_x, self.to_y, self.to_c, self.relay_x, self.relay_y, self.core_x, self.core_y, self.core_d)
+        self.buf, self.rows, self.relayed = buf, rows, False
+        self.sent, self.relays_sent, self.near, self.relays = (pool.take() for _ in range(4))
+        self.over = [pool.take() for _ in range(4)] if split else [pool.take()] * 4
+        self.to_x = send(own, own, dev['x'], self.sent, self.near)
+        self.to_y = send(own, own, dev['y'], self.sent, self.near)
+        self.to_c = send(own, own, dev['c'], self.sent, self.over[0])
+        self.relay_x = send(at('y', 0, half), at('y', 0, half), dev['x'], self.relays_sent, self.relays)
+        self.relay_y = send(at('x', half, half), at('x', half, half), dev['y'], self.relays_sent, self.relays)
+        self.core_x = send(at('x'), at('x'), dev['c'], self.sent, self.over[1])
+        self.core_y = send(at('y'), at('y'), dev['c'], self.sent, self.over[2])
+        self.core_d = send(at('yx'), at('yx'), dev['c'], self.sent, self.over[3])
+
+    def blocks(self, count):
+        return self.buf.at[0:count * self.rows, :]
 
     def begin_links(self):
         self.to_x.start()
@@ -112,39 +107,31 @@
         self.begin_links()
         self.begin_core()
 
-    def after(self):
-        self.early = True
-        self.to_x.sent()
-        self.to_y.sent()
-
     def relay(self):
-        self.to_y.arrive()
+        wait_for(self.blocks(2), self.near)
         self.relay_x.start()
-        self.to_x.arrive()
         self.relay_y.start()
         self.core_x.start()
         self.core_y.start()
 
     def relay_left(self):
         self.relayed = True
-        self.relay_x.sent()
-        self.relay_y.sent()
+        wait_for(self.blocks(1), self.relays_sent)
 
     def last(self):
-        self.relay_x.arrive()
-        self.relay_y.arrive()
+        wait_for(self.blocks(1), self.relays)
         self.core_d.start()
 
+    def crossed(self, k):
+        wait_for(self.blocks(1), self.over[k])
+
     def finish(self):
-        self.to_c.arrive()
-        self.core_x.arrive()
-        self.core_y.arrive()
-        self.core_d.arrive()
+        wait_for(self.blocks(4), self.over[0])
 
     def drain(self):
-        for link in self.links:
-            if not (self.early and link in (self.to_x, self.to_y)) and not (self.relayed and link in (self.relay_x, self.relay_y)):
-                link.sent()
+        wait_for(self.blocks(6), self.sent)
+        if not self.relayed:
+            wait_for(self.blocks(1), self.relays_sent)
 
 
 class Scatter:
@@ -157,14 +144,14 @@
         self.cols = pl.ds(first, from_core.shape[-1])
         other = part.at[pl.ds(pl.multiple_of((1 - place.core) * four, 8), four), self.cols]
         dev = place.dev
-        self.core = Link(pool, other, from_core, from_core, dev['c'])
-        self.x0 = Link(pool, self.at('x', 0), from_x.at[0], from_x.at[0], dev['x'])
-        self.x1 = Link(pool, self.at('yx', 0), from_x.at[1], from_x.at[1], dev['x'])
-        self.y0 = Link(pool, self.at('y', half), from_y.at[0], from_y.at[0], dev['y'])
-        self.y1 = Link(pool, self.at('yx', half), from_y.at[1], from_y.at[1], dev['y'])
-        self.end_y = Link(pool, self.at('y', 0), last_y, last_y, dev['y'])
-        self.end_x = Link(pool, self.at('x', half), last_x, last_x, dev['x'])
-        self.links = (self.core, self.x0, self.x1, self.y0, self.y1, self.end_y, self.end_x)
+        self.sent, self.crossed, self.first_x, self.first_y, self.rest = (pool.take() for _ in range(5))
+        self.core = send(other, from_core, dev['c'], self.sent, self.crossed)
+        self.x0 = send(self.at('x', 0), from_x.at[0], dev['x'], self.sent, self.rest)
+        self.x1 = send(self.at('yx', 0), from_x.at[1], dev['x'], self.sent, self.first_x)
+        self.y0 = send(self.at('y', half), from_y.at[0], dev['y'], self.sent, self.rest)
+        self.y1 = send(self.at('yx', half), from_y.at[1], dev['y'], self.sent, self.first_y)
+        self.end_y = send(self.at('y', 0), last_y, dev['y'], self.sent, self.rest)
+        self.end_x = send(self.at('x', half), last_x, dev['x'], self.sent, self.rest)
 
     def at(self, name, lo):
         return self.part.at[pl.ds(pl.multiple_of(self.place.block[name] * self.rows + lo, 8), self.half), self.cols]
@@ -173,7 +160,7 @@
         self.core.start()
 
     def middle(self):
-        self.core.arrive()
+        wait_for(self.from_core, self.crossed)
         mine = pl.ds(self.mine, 4 * self.rows)
         self.part[mine, self.cols] = self.part[mine, self.cols] + self.from_core[...]
         self.x1.start()
@@ -182,54 +169,50 @@
         self.y0.start()
 
     def late(self):
-        self.x1.arrive()
+        wait_for(self.from_x.at[1], self.first_x)
         here = self.at('y', 0)
         here[...] = here[...] + self.from_x[1]
         self.end_y.start()
-        self.y1.arrive()
+        wait_for(self.from_y.at[1], self.first_y)
         here = self.at('x', self.half)
         here[...] = here[...] + self.from_y[1]
         self.end_x.start()
 
     def finish(self, out, row=0):
         half = self.half
-        self.x0.arrive()
-        self.y0.arrive()
-        self.end_y.arrive()
-        self.end_x.arrive()
+        wait_for(self.part.at[0:4 * half, self.cols], self.rest)
         out[row:row + half, self.cols] = (self.at('', 0)[...] + self.from_x[0] + self.last_y[...]).astype(BF16)
         out[row + half:row + 2 * half, self.cols] = (self.at('', half)[...] + self.from_y[0] + self.last_x[...]).astype(BF16)
 
     def drain(self):
-        for link in self.links:
-            link.sent()
+        wait_for(self.part.at[0:7 * self.rows, self.cols], self.sent)
 
 
 class ChipSum:
-    def __init__(self, pool, place, part, from_core, rows, first, outs, sems):
+    def __init__(self, pool, place, part, from_core, rows, first, outs, sem):
         four = 4 * rows
-        self.part, self.from_core = part, from_core
+        self.part, self.from_core, self.sem = part, from_core, sem
         self.mine = pl.multiple_of(place.core * four, 8)
         self.cols = pl.ds(first, from_core.shape[-1])
         other = part.at[pl.ds(pl.multiple_of((1 - place.core) * four, 8), four), self.cols]
-        self.core = Link(pool, other, from_core, from_core, place.dev['c'])
-        self.copies = [pltpu.make_async_copy(part.at[pl.ds(pl.multiple_of(place.block[name] * rows, 8), rows), self.cols], out.at[:, self.cols], sems.at[k])
-                       for k, (name, out) in enumerate(outs)]
+        self.sent, self.crossed = pool.take(), pool.take()
+        self.core = send(other, from_core, place.dev['c'], self.sent, self.crossed)
+        self.copies = [pltpu.make_async_copy(part.at[pl.ds(pl.multiple_of(place.block[name] * rows, 8), rows), self.cols], out.at[:, self.cols], sem)
+                       for name, out in outs]
 
     def begin(self):
         self.core.start()
 
     def middle(self):
-        self.core.arrive()
+        wait_for(self.from_core, self.crossed)
         mine = pl.ds(self.mine, self.from_core.shape[0])
         self.part[mine, self.cols] = self.part[mine, self.cols] + self.from_core[...]
         for copy in self.copies:
             copy.start()
 
     def drain(self):
-        self.core.sent()
-        for copy in self.copies:
-            copy.wait()
+        wait_for(self.from_core, self.sent)
+        wait_for(self.from_core, self.sem)
 
 
 def scatter_shapes(rows, width):
@@ -238,7 +221,7 @@
             pltpu.VMEM((half, width), F32), pltpu.VMEM((half, width), F32)]
 
 
-NUM_LINKS = 7 + 14 + 8 * 5 + 7 * 7 + 6
+NUM_SEMS = 2 + 4 + 5 * 4 + 8 + 5 * 7 + 2 * 6
 
 
 def attention_qkv(xa, wqkv, qkv, chip, seq):
@@ -278,9 +261,9 @@
                y_out, dx_out, attn_out, dg_out, xt_all, dy_all, da_all, db_all, ht_all, gates_out, own_out, to_x_out, to_y_out, to_d_out,
                xb, dyb, xab, gtb, gcol, wg, wu, wd, y_part, dx_part, at_part, wqkv, wo, qkv, s1, s2, d_o, dgc, dgt, da, db, hid, stage_t, xt, dgl, gtab, gfull,
                ryc, rdc, ry0, ry1, ry2, ry3, ry4, rd0, rd1, rd2, rd3, rd4, ra0, ra1, ra2, ra3, ra4,
-               send_sems, recv_sems, w_sems, in_sems, aw_sems, out_sems, stage_sems, grad_sems, sum_sems, res_sems, y_res, dx_res, attn_res, dg_res):
+               sems, w_sems, in_sems, aw_sems, out_sems, stage_sems, grad_sems, sum_sems, res_sems, y_res, dx_res, attn_res, dg_res):
         place = Place()
-        pool = Pool(send_sems, recv_sems)
+        pool = Pool(sems)
         dev, block = place.dev, place.block
         me = block['']
 
@@ -289,19 +272,19 @@
 
         loads = []
         for h in range(HALVES):
-            loads.append(pltpu.make_async_copy(x_in.at[h * r:(h + 1) * r, :], own_rows(xb.at[h], r), in_sems.at[h]))
-            loads.append(pltpu.make_async_copy(dy_in.at[h * r:(h + 1) * r, :], own_rows(dyb.at[h], r), in_sems.at[2 + h]))
-        loads.append(pltpu.make_async_copy(xa_in, own_rows(xab, tok, place.pair['']), in_sems.at[4]))
+            loads.append(pltpu.make_async_copy(x_in.at[h * r:(h + 1) * r, :], own_rows(xb.at[h], r), in_sems))
+            loads.append(pltpu.make_async_copy(dy_in.at[h * r:(h + 1) * r, :], own_rows(dyb.at[h], r), in_sems))
+        loads.append(pltpu.make_async_copy(xa_in, own_rows(xab, tok, place.pair['']), in_sems))
         for load in loads:
             load.start()
         q_dim, kv_dim = wq_in.shape[0], wk_in.shape[0]
-        attn_loads = [pltpu.make_async_copy(wq_in, wqkv.at[0:q_dim, :], aw_sems.at[0]), pltpu.make_async_copy(wk_in, wqkv.at[q_dim:q_dim + kv_dim, :], aw_sems.at[1]),
-                      pltpu.make_async_copy(wv_in, wqkv.at[q_dim + kv_dim:q_dim + 2 * kv_dim, :], aw_sems.at[2]), pltpu.make_async_copy(wo_in, wo, aw_sems.at[3])]
+        attn_loads = [pltpu.make_async_copy(wq_in, wqkv.at[0:q_dim, :], aw_sems), pltpu.make_async_copy(wk_in, wqkv.at[q_dim:q_dim + kv_dim, :], aw_sems),
+                      pltpu.make_async_copy(wv_in, wqkv.at[q_dim + kv_dim:q_dim + 2 * kv_dim, :], aw_sems), pltpu.make_async_copy(wo_in, wo, aw_sems)]
         for load in attn_loads:
             load.start()
         weights = []
         for e in range(exp_loc):
-            weights.append([pltpu.make_async_copy(src.at[e], dst.at[e], w_sems.at[e, k]) for k, (src, dst) in enumerate(((wg_in, wg), (wu_in, wu), (wd_in, wd)))])
+            weights.append([pltpu.make_async_copy(src.at[e], dst.at[e], w_sems.at[e]) for src, dst in ((wg_in, wg), (wu_in, wu), (wd_in, wd))])
         barrier = pltpu.get_barrier_semaphore()
         peers = [name for name in dev if name]
         for name in peers:
@@ -312,10 +295,11 @@
                 gtab[g, e:e + 1, 0:tok] = jnp.sum(jnp.where(idx_in[...] == g * exp_loc + e, gate_in[...], 0.0), axis=0, keepdims=True)
         pl.semaphore_wait(barrier, len(peers))
 
-        routes = [Link(pool, gtab.at[place.flat[name]], gtb.at[me], gtb.at[block[name]], dev[name]) for name in peers]
+        routes_sent, routes_in = pool.take(), pool.take()
+        routes = [send(gtab.at[place.flat[name]], gtb.at[me], dev[name], routes_sent, routes_in) for name in peers]
         gx = [Gather(pool, place, xb.at[h], r, block) for h in range(HALVES)]
         gdy = [Gather(pool, place, dyb.at[h], r, block) for h in range(HALVES)]
-        gxa = Gather(pool, place, xab, tok, place.pair)
+        gxa = Gather(pool, place, xab, tok, place.pair, split=True)
         def passed(t):
             return [(name, out.at[t]) for name, out in (('', own_out), ('x', to_x_out), ('y', to_y_out), ('yx', to_d_out))]
 
@@ -324,10 +308,10 @@
         sdx = [[Scatter(pool, place, dx_part.at[0], rd0.at[n], rd1.at[n], rd2.at[n], rd3.at[n], rd4.at[n], r, n * tile) for n in range(tiles)],
                [ChipSum(pool, place, dx_part.at[1], rdc.at[n], r, n * tile, passed(1), sum_sems.at[1, n]) for n in range(tiles)]]
         sat = Scatter(pool, place, at_part, ra0, ra1, ra2, ra3, ra4, tok)
-        dg_links = [[Link(pool, dgt.at[h, 1 - place.core if 'c' in name else place.core], dgl.at[me, h], dgl.at[block[name], h], dev[name]) for name in peers] for h in range(HALVES)]
-
-        for load in loads:
-            load.wait()
+        dg_sems = [(pool.take(), pool.take()) for _ in range(HALVES)]
+        dg_links = [[send(dgt.at[h, 1 - place.core if 'c' in name else place.core], dgl.at[me, h], dev[name], *dg_sems[h]) for name in peers] for h in range(HALVES)]
+
+        wait_for(xab.at[0:3 * tok, :], in_sems)
         gx[0].begin()
         gxa.begin_core()
         for link in routes:
@@ -338,8 +322,7 @@
                 w.start()
         dgc[...] = jnp.zeros_like(dgc)
         gcol[...] = jnp.zeros_like(gcol)
-        for load in attn_loads:
-            load.wait()
+        wait_for(xab, aw_sems)
 
         def pairs(names, between=None):
             for k, name in enumerate(names):
@@ -349,11 +332,10 @@
             for k, name in enumerate(names):
                 attention_out(qkv.at[k], wo, at_part, place.chips[name], NUM_DEV // 2, attn_dims)
 
-        gxa.to_c.arrive()
+        gxa.crossed(0)
         pairs(('',))
         gx[0].relay()
-        for link in routes:
-            link.arrive()
+        wait_for(gtb.at[0:7], routes_in)
         wide = jnp.concatenate([gtb[...].reshape(NUM_DEV * 8, LANES), jnp.zeros((LANES - NUM_DEV * 8, LANES), F32)], axis=0).T
         for h in range(HALVES):
             for b in range(NUM_DEV):
@@ -370,7 +352,7 @@
             if k == 2:
                 slot = h * 2 + lax.rem(e, 2)
                 return pltpu.make_async_copy(stage_t.at[slot], ht_all.at[e, :, part], stage_sems.at[slot])
-            return pltpu.make_async_copy((da, db)[k].at[e], (da_all, db_all)[k].at[e, part, :], grad_sems.at[e, k])
+            return pltpu.make_async_copy((da, db)[k].at[e], (da_all, db_all)[k].at[e, part, :], grad_sems.at[e])
 
         lane = lax.broadcasted_iota(jnp.int32, (m, LANES), 1)
 
@@ -389,8 +371,7 @@
         def hidden(h):
             def body(e):
                 if h == 0:
-                    for k, (src, dst) in enumerate(((wg_in, wg), (wu_in, wu), (wd_in, wd))):
-                        pltpu.make_async_copy(src.at[e], dst.at[e], w_sems.at[e, k]).wait()
+                    wait_for(wg.at[0:3], w_sems.at[e])
 
                 @pl.when(e >= 2)
                 def _():
@@ -430,8 +411,7 @@
         def hidden_grads(h):
             def body(e):
                 if h:
-                    for k in range(2):
-                        staged(h - 1, e, k).wait()
+                    wait_for(da.at[0:2], grad_sems.at[e])
                 for n in range(tiles):
                     cols = pl.ds(n * tile, tile)
                     d_o[:, cols] = (gate_of(h, e) * dyb[h, :, cols].astype(F32)).astype(BF16)
@@ -462,8 +442,7 @@
 
         def dg_read():
             for h in range(HALVES):
-                for link in dg_links[h]:
-                    link.arrive()
+                wait_for(gtb.at[0:7], dg_sems[h][1])
             for h in range(HALVES):
                 slots = idx_in[:, h * r:(h + 1) * r]
                 total = jnp.zeros(slots.shape, F32)
@@ -485,13 +464,13 @@
             return run
 
         loop(exp_loc, {2: gdy[0].begin, 3: gxa.relay}, hidden(0))
-        gxa.core_x.arrive()
-        gxa.core_y.arrive()
+        gxa.crossed(1)
+        gxa.crossed(2)
         pairs(('x', 'y'), gdy[0].relay)
         gx[1].begin()
         gxa.last()
         gdy[1].begin()
-        gxa.core_d.arrive()
+        gxa.crossed(3)
         pairs(('yx',), gdy[0].last)
         sat.begin()
         gdy[0].finish()
@@ -511,8 +490,8 @@
         saves = [pltpu.make_async_copy(xt, xt_all, out_sems.at[0]), pltpu.make_async_copy(dyb, dy_all, out_sems.at[1]), pltpu.make_async_copy(gcol, gates_out, out_sems.at[2])]
         for save in saves:
             save.start()
-        loop(exp_loc, {1: sy[1][0].middle, 2: sdx[0][0].late, 3: seq(sy[1][1].middle, sy[1][2].middle), 4: sdx[0][1].late}, hidden_grads(1))
-        loop(tiles, {1: seq(sdx[1][0].begin, sdx[0][2].late), 2: seq(sdx[1][1].begin, sdx[1][0].middle)}, input_grads(1))
+        loop(exp_loc, {0: sdx[0][0].late, 1: seq(sy[1][0].middle, sdx[0][1].late), 3: seq(sy[1][1].middle, sy[1][2].middle, sdx[0][2].late)}, hidden_grads(1))
+        loop(tiles, {1: sdx[1][0].begin, 2: seq(sdx[1][1].begin, sdx[1][0].middle)}, input_grads(1))
         sdx[1][2].begin()
         sdx[1][1].middle()
         for s in sy[0]:
@@ -528,16 +507,15 @@
         for save in saves + results:
             save.wait()
         for e in range(exp_loc):
-            for k in range(2):
-                staged(HALVES - 1, jnp.int32(e), k).wait()
+            wait_for(da.at[0:2], grad_sems.at[e])
         for h in range(HALVES):
             for e in (exp_loc - 2, exp_loc - 1):
                 staged(h, jnp.int32(e), 2).wait()
         for item in gx + gdy + [gxa, sat] + sum(sy + sdx, []):
             item.drain()
-        for link in routes + dg_links[0] + dg_links[1]:
-            link.sent()
-        assert pool.used == NUM_LINKS
+        for sem in (routes_sent, dg_sems[0][0], dg_sems[1][0]):
+            wait_for(gtb.at[0:7], sem)
+        assert pool.used == NUM_SEMS, pool.used
 
     return kernel, r, m
 
@@ -693,8 +671,8 @@
                             pltpu.VMEM((HALVES, m, LANES), F32), pltpu.VMEM((HALVES, 2, 8, LANES), F32), pltpu.VMEM((exp_loc, m, d_ff), BF16), pltpu.VMEM((exp_loc, m, d_ff), BF16),
                             pltpu.VMEM((exp_loc, m, d_ff), BF16), pltpu.VMEM((2 * HALVES, d_ff, m), BF16), pltpu.VMEM((d_model, total), BF16), pltpu.VMEM((NUM_DEV, HALVES, 8, LANES), F32), pltpu.VMEM((NUM_DEV, 8, LANES), F32), pltpu.VMEM((HALVES, exp_loc, m, LANES), F32)]
             + [pltpu.VMEM((d_model // 512, 4 * r, 512), F32)] * 2 + half_shapes() + half_shapes() + scatter_shapes(tok, d_model)
-            + [pltpu.SemaphoreType.DMA((NUM_LINKS,)), pltpu.SemaphoreType.DMA((NUM_LINKS,)), pltpu.SemaphoreType.DMA((exp_loc, 3)),
-               pltpu.SemaphoreType.DMA((5,)), pltpu.SemaphoreType.DMA((4,)), pltpu.SemaphoreType.DMA((3,)), pltpu.SemaphoreType.DMA((2 * HALVES,)), pltpu.SemaphoreType.DMA((exp_loc, 2)), pltpu.SemaphoreType.DMA((2, d_model // 512, 4)), pltpu.SemaphoreType.DMA((4,)),
+            + [pltpu.SemaphoreType.DMA((NUM_SEMS,)), pltpu.SemaphoreType.DMA((exp_loc,)),
+               pltpu.SemaphoreType.DMA(()), pltpu.SemaphoreType.DMA(()), pltpu.SemaphoreType.DMA((3,)), pltpu.SemaphoreType.DMA((2 * HALVES,)), pltpu.SemaphoreType.DMA((exp_loc,)), pltpu.SemaphoreType.DMA((2, d_model // 512)), pltpu.SemaphoreType.DMA((4,)),
                pltpu.VMEM((r, d_model), BF16), pltpu.VMEM((r, d_model), BF16), pltpu.VMEM((tok, d_model), BF16), pltpu.VMEM((top_k, tok), F32)],
             compiler_params=pltpu.CompilerParams(collective_id=0, has_side_effects=True, vmem_limit_bytes=67000000),
             name='layer',

time: 86.5 us -> 84.7 us (0.979)
  Pallas kernels: 81.4 us -> 79.6 us
    pallas_call x1, Pallas kernels: 61.4 us -> 59.6 us  [local_step(): pl.pallas_call(kernel, out_shape=(shape((r, d_model), BF16), shape((r, d_...]
  transfers between devices with their start and end apart: 3 -> 3, of which waited for: 0 -> 0; matrix products, arithmetic and copies ran while one was open for 0% -> 0% of each run, Pallas kernels for 23% -> 24%
where the time goes in v6:
time: 84.7 us; the launch traced here: 84.5 us
  Pallas kernels  79.6 us (94%)
  starting transfers between devices  3.51 us (4%)
    pallas_call x1, Pallas kernels, local_step(): pl.pallas_call(kernel, out_shape=(shape((r, d_model), BF16), shape((r, d_...  59.6 us
    pallas_call x1, Pallas kernels, local_step(): pl.pallas_call(functools.partial(weight_grads, width, slots), out_shape=(...  20 us
    ppermute x3, starting transfers between devices, swap(): return lax.ppermute(value, GROUP_AXES, pairs)  3.51 us
  transfers between devices with their start and end apart: 3, of which 0 were waited for; matrix products, arithmetic and copies ran while one was open for 0% of the time, Pallas kernels for 24%

profile of v6, /device:TPU:0, one launch (start us, length us, event | category | flops | bytes accessed | tf_op | source)
XLA Modules:
  0.0 84.5 jit_solution(16135773517265798283)
XLA Ops:
  0.6 59.6 %layer.1 = (bf16[32,1536]{1,0:T(8,128)(2,1)}, bf16[32,1536]{1,0:T(8,128)(2,1)}, bf16[64,1536]{1,0:T(8,128)(2,1)}, f32[8,64]{1,0:T(8,128)}, bf16[1536,512]{1,0:T(...) custom-call(bf16[64,1536]{1,0:T(8,128)(2,1)} %x_in.1, ...), custom_call_target="tpu_custom_call" | custom-call | tf_op jit(solution)/shard_map/layer/pallas_call | solution.py:659
  60.2 0.7 collective-permute-start
  60.9 1.3 %collective-permute-start.1 = (f32[2,32,1536]{2,1,0:T(8,128)}, f32[2,32,1536]{2,1,0:T(8,128)S(1)}, u32[]{:S(2)}, u32[]{:S(2)}) collective-permute-start(f32[2,32,1536]{2,1,0:T(8,128)} %get-tuple-element.41), channel_id=1, source_target_pairs={{0,4},{1,5},{2,6},{3,7},{4,0},{5,1},{6,2},{7,3}} | collective-permute-start | bytes 1179656 | tf_op jit(solution)/shard_map/ppermute | solution.py:689
  62.2 1.5 %collective-permute-start.2 = (f32[2,32,1536]{2,1,0:T(8,128)}, f32[2,32,1536]{2,1,0:T(8,128)S(1)}, u32[]{:S(2)}, u32[]{:S(2)}) collective-permute-start(f32[2,32,1536]{2,1,0:T(8,128)} %get-tuple-element.42), channel_id=1, source_target_pairs={{0,6},{1,7},{2,4},{3,5},{4,2},{5,3},{6,0},{7,1}} | collective-permute-start | bytes 1179656 | tf_op jit(solution)/shard_map/ppermute | solution.py:689
  63.7 0.0 copy-start
  63.7 20.0 %weight_grads.1 = (f32[5,1536,512]{2,1,0:T(8,128)}, f32[5,1536,512]{2,1,0:T(8,128)}, f32[5,512,1536]{2,1,0:T(8,128)}, bf16[64,1536]{1,0:T(8,128)(2,1)}, f32[8,64...) custom-call(bf16[1536,512]{1,0:T(8,128)(2,1)} %get-tuple-element.28.xt_in, ...), custom_call_target="tpu_custom_call" | custom-call | flops 12079595520 | bytes 47185920 | tf_op jit(solution)/shard_map/weight_grads/pallas_call | solution.py:692
  83.7 0.0 collective-permute-done
  83.8 0.0 collective-permute-done.1
  83.8 0.0 collective-permute-done.2
  83.8 0.0 copy-done
  83.8 0.8 fusion.5
Async XLA Ops:
  60.2 23.6 %collective-permute-start = (f32[2,32,1536]{2,1,0:T(8,128)}, f32[2,32,1536]{2,1,0:T(8,128)S(1)}, u32[]{:S(2)}, u32[]{:S(2)}) collective-permute-start(f32[2,32,1536]{2,1,0:T(8,128)} %get-tuple-element.40), channel_id=1, source_target_pairs={{0,2},{1,3},{2,0},{3,1},{4,6},{5,7},{6,4},{7,5}} | collective-permute-start | bytes 1179656 | tf_op jit(solution)/shard_map/ppermute | solution.py:689
  60.9 22.9 %collective-permute-start.1 = (f32[2,32,1536]{2,1,0:T(8,128)}, f32[2,32,1536]{2,1,0:T(8,128)S(1)}, u32[]{:S(2)}, u32[]{:S(2)}) collective-permute-start(f32[2,32,1536]{2,1,0:T(8,128)} %get-tuple-element.41), channel_id=1, source_target_pairs={{0,4},{1,5},{2,6},{3,7},{4,0},{5,1},{6,2},{7,3}} | collective-permute-start | bytes 1179656 | tf_op jit(solution)/shard_map/ppermute | solution.py:689
  62.2 21.5 %collective-permute-start.2 = (f32[2,32,1536]{2,1,0:T(8,128)}, f32[2,32,1536]{2,1,0:T(8,128)S(1)}, u32[]{:S(2)}, u32[]{:S(2)}) collective-permute-start(f32[2,32,1536]{2,1,0:T(8,128)} %get-tuple-element.42), channel_id=1, source_target_pairs={{0,6},{1,7},{2,4},{3,5},{4,2},{5,3},{6,0},{7,1}} | collective-permute-start | bytes 1179656 | tf_op jit(solution)/shard_map/ppermute | solution.py:689
  63.7 20.1 %copy-start = (f32[2,32,1536]{2,1,0:T(8,128)S(1)}, f32[2,32,1536]{2,1,0:T(8,128)}, u32[]{:S(2)}) copy-start(f32[2,32,1536]{2,1,0:T(8,128)} %get-tuple-element.39) | copy-start | bytes 1179652

commit v7 on v6

--- a/solution.py
+++ b/solution.py
@@ -197,7 +197,7 @@
         other = part.at[pl.ds(pl.multiple_of((1 - place.core) * four, 8), four), self.cols]
         self.sent, self.crossed = pool.take(), pool.take()
         self.core = send(other, from_core, place.dev['c'], self.sent, self.crossed)
-        self.copies = [pltpu.make_async_copy(part.at[pl.ds(pl.multiple_of(place.block[name] * rows, 8), rows), self.cols], out.at[:, self.cols], sem)
+        self.copies = [pltpu.make_async_copy(part.at[pl.ds(pl.multiple_of(place.block[name] * rows, 8), rows), self.cols], out, sem)
                        for name, out in outs]
 
     def begin(self):
@@ -221,7 +221,7 @@
             pltpu.VMEM((half, width), F32), pltpu.VMEM((half, width), F32)]
 
 
-NUM_SEMS = 2 + 4 + 5 * 4 + 8 + 5 * 7 + 2 * 6
+NUM_SEMS = 2 + 4 + 5 * 4 + 8 + 5 * 6 + 2 * 7
 
 
 def attention_qkv(xa, wqkv, qkv, chip, seq):
@@ -300,13 +300,17 @@
         gx = [Gather(pool, place, xb.at[h], r, block) for h in range(HALVES)]
         gdy = [Gather(pool, place, dyb.at[h], r, block) for h in range(HALVES)]
         gxa = Gather(pool, place, xab, tok, place.pair, split=True)
-        def passed(t):
-            return [(name, out.at[t]) for name, out in (('', own_out), ('x', to_x_out), ('y', to_y_out), ('yx', to_d_out))]
+        def passed(k):
+            return [(name, out.at[:, k * tile:(k + 1) * tile]) for name, out in (('', own_out), ('x', to_x_out), ('y', to_y_out), ('yx', to_d_out))]
+
+        def chip_sum(part, from_core, n, k):
+            return ChipSum(pool, place, part, from_core, r, n * tile, passed(k), sum_sems.at[k])
 
         sy = [[Scatter(pool, place, y_part.at[0], ry0.at[n], ry1.at[n], ry2.at[n], ry3.at[n], ry4.at[n], r, n * tile) for n in range(tiles)],
-              [ChipSum(pool, place, y_part.at[1], ryc.at[n], r, n * tile, passed(0), sum_sems.at[0, n]) for n in range(tiles)]]
-        sdx = [[Scatter(pool, place, dx_part.at[0], rd0.at[n], rd1.at[n], rd2.at[n], rd3.at[n], rd4.at[n], r, n * tile) for n in range(tiles)],
-               [ChipSum(pool, place, dx_part.at[1], rdc.at[n], r, n * tile, passed(1), sum_sems.at[1, n]) for n in range(tiles)]]
+              [chip_sum(y_part.at[1], ryc.at[n], n, n) for n in range(tiles)]]
+        sdx = [[Scatter(pool, place, dx_part.at[0], rd0.at[n], rd1.at[n], rd2.at[n], rd3.at[n], rd4.at[n], r, n * tile) for n in range(tiles - 1)]
+               + [chip_sum(dx_part.at[0], rd0.at[tiles - 1], tiles - 1, 2 * tiles)],
+               [chip_sum(dx_part.at[1], rdc.at[n], n, tiles + n) for n in range(tiles)]]
         sat = Scatter(pool, place, at_part, ra0, ra1, ra2, ra3, ra4, tok)
         dg_sems = [(pool.take(), pool.take()) for _ in range(HALVES)]
         dg_links = [[send(dgt.at[h, 1 - place.core if 'c' in name else place.core], dgl.at[me, h], dev[name], *dg_sems[h]) for name in peers] for h in range(HALVES)]
@@ -463,12 +467,11 @@
 
             return run
 
-        loop(exp_loc, {2: gdy[0].begin, 3: gxa.relay}, hidden(0))
+        loop(exp_loc, {0: gdy[0].begin, 3: gxa.relay}, hidden(0))
         gxa.crossed(1)
         gxa.crossed(2)
-        pairs(('x', 'y'), gdy[0].relay)
+        pairs(('x', 'y'), seq(gdy[0].relay, gxa.last))
         gx[1].begin()
-        gxa.last()
         gdy[1].begin()
         gxa.crossed(3)
         pairs(('yx',), gdy[0].last)
@@ -490,15 +493,16 @@
         saves = [pltpu.make_async_copy(xt, xt_all, out_sems.at[0]), pltpu.make_async_copy(dyb, dy_all, out_sems.at[1]), pltpu.make_async_copy(gcol, gates_out, out_sems.at[2])]
         for save in saves:
             save.start()
-        loop(exp_loc, {0: sdx[0][0].late, 1: seq(sy[1][0].middle, sdx[0][1].late), 3: seq(sy[1][1].middle, sy[1][2].middle, sdx[0][2].late)}, hidden_grads(1))
+        loop(exp_loc, {0: sdx[0][0].late, 1: seq(sy[1][0].middle, sdx[0][1].late), 3: seq(sy[1][1].middle, sy[1][2].middle)}, hidden_grads(1))
         loop(tiles, {1: sdx[1][0].begin, 2: seq(sdx[1][1].begin, sdx[1][0].middle)}, input_grads(1))
         sdx[1][2].begin()
         sdx[1][1].middle()
         for s in sy[0]:
             s.finish(y_res)
         sat.finish(attn_res)
-        for s in sdx[0]:
+        for s in sdx[0][:-1]:
             s.finish(dx_res)
+        dx_res[:, (tiles - 1) * tile:] = jnp.zeros((r, tile), BF16)
         dg_read()
         results = [pltpu.make_async_copy(src, dst, res_sems.at[k]) for k, (src, dst) in enumerate(((y_res, y_out), (dx_res, dx_out), (attn_res, attn_out), (dg_res, dg_out)))]
         for result in results:
@@ -520,9 +524,9 @@
     return kernel, r, m
 
 
-def weight_grads(width, slots, xt_in, dy_in, g_in, da_in, db_in, ht_in, at_in, dg_in, y_in, dx_in,
-                 dwg, dwu, dwd, at_out, dg_out, y_out, dx_out,
-                 xt, dy, g, da, db, ht, sg, su, sd, at, dg, y, dx, x_sems, d_sems, g_sem, e_sems, o_sems, p_sems):
+def weight_grads(width, slots, xt_in, dy_in, g_in, da_in, db_in, ht_in, at_in, dg_in,
+                 dwg, dwu, dwd, at_out, dg_out,
+                 xt, dy, g, da, db, ht, sg, su, sd, at, dg, x_sems, d_sems, g_sem, e_sems, o_sems, p_sems):
     exp_loc = da.shape[0]
     steps = dy.shape[1] // width
 
@@ -551,8 +555,7 @@
     for e in range(1, exp_loc):
         for k in range(3):
             load(e, k).start()
-    rows = slice(0, y.shape[0])
-    passing = ((at_in, at, at_out), (dg_in, dg, dg_out), (y_in, y, y_out.at[rows, :]), (dx_in, dx, dx_out.at[rows, :]))
+    passing = ((at_in, at, at_out), (dg_in, dg, dg_out))
     take = [pltpu.make_async_copy(src, mid, p_sems.at[k, 0]) for k, (src, mid, _) in enumerate(passing)]
     give = [pltpu.make_async_copy(mid, dst, p_sems.at[k, 1]) for k, (_, mid, dst) in enumerate(passing)]
     for copy in take:
@@ -660,7 +663,7 @@
             kernel,
             out_shape=(shape((r, d_model), BF16), shape((r, d_model), BF16), shape((tok, d_model), BF16), shape((top_k, tok), F32),
                        shape((d_model, total), BF16), shape((HALVES, m, d_model), BF16),
-                       shape((exp_loc, total, d_ff), BF16), shape((exp_loc, total, d_ff), BF16), shape((exp_loc, d_ff, total), BF16), shape((HALVES, m, LANES), F32)) + (shape((2, r, d_model), F32),) * 4,
+                       shape((exp_loc, total, d_ff), BF16), shape((exp_loc, total, d_ff), BF16), shape((exp_loc, d_ff, total), BF16), shape((HALVES, m, LANES), F32)) + (shape((r, 2 * d_model + 512), F32),) * 4,
             in_specs=[any_spec, any_spec, any_spec, vmem_spec, vmem_spec] + [any_spec] * 7,
             out_specs=(any_spec,) * 14,
             scratch_shapes=[pltpu.VMEM((HALVES, m, d_model), BF16), pltpu.VMEM((HALVES, m, d_model), BF16), pltpu.VMEM((total, d_model), BF16),
@@ -672,7 +675,7 @@
                             pltpu.VMEM((exp_loc, m, d_ff), BF16), pltpu.VMEM((2 * HALVES, d_ff, m), BF16), pltpu.VMEM((d_model, total), BF16), pltpu.VMEM((NUM_DEV, HALVES, 8, LANES), F32), pltpu.VMEM((NUM_DEV, 8, LANES), F32), pltpu.VMEM((HALVES, exp_loc, m, LANES), F32)]
             + [pltpu.VMEM((d_model // 512, 4 * r, 512), F32)] * 2 + half_shapes() + half_shapes() + scatter_shapes(tok, d_model)
             + [pltpu.SemaphoreType.DMA((NUM_SEMS,)), pltpu.SemaphoreType.DMA((exp_loc,)),
-               pltpu.SemaphoreType.DMA(()), pltpu.SemaphoreType.DMA(()), pltpu.SemaphoreType.DMA((3,)), pltpu.SemaphoreType.DMA((2 * HALVES,)), pltpu.SemaphoreType.DMA((exp_loc,)), pltpu.SemaphoreType.DMA((2, d_model // 512)), pltpu.SemaphoreType.DMA((4,)),
+               pltpu.SemaphoreType.DMA(()), pltpu.SemaphoreType.DMA(()), pltpu.SemaphoreType.DMA((3,)), pltpu.SemaphoreType.DMA((2 * HALVES,)), pltpu.SemaphoreType.DMA((exp_loc,)), pltpu.SemaphoreType.DMA((2 * (d_model // 512) + 1,)), pltpu.SemaphoreType.DMA((4,)),
                pltpu.VMEM((r, d_model), BF16), pltpu.VMEM((r, d_model), BF16), pltpu.VMEM((tok, d_model), BF16), pltpu.VMEM((top_k, tok), F32)],
             compiler_params=pltpu.CompilerParams(collective_id=0, has_side_effects=True, vmem_limit_bytes=67000000),
             name='layer',
@@ -681,7 +684,7 @@
         width = 512
         steps = d_model // width
         slots = 2 * steps
-        small = (attn, dgt, y0, dx0)
+        small = (attn, dgt)
 
         def swap(value, flip_y, flip_x):
             eo_size = mesh.shape['eo']
@@ -689,22 +692,27 @@
             return lax.ppermute(value, GROUP_AXES, pairs)
 
         from_x, from_y, from_d = swap(to_x, 0, 1), swap(to_y, 1, 0), swap(to_d, 1, 1)
-        dw_gate, dw_up, dw_down, attn, dgt, y, dx = pl.pallas_call(
+        dw_gate, dw_up, dw_down, attn, dgt = pl.pallas_call(
             functools.partial(weight_grads, width, slots),
-            out_shape=(shape((exp_loc, d_model, d_ff), F32), shape((exp_loc, d_model, d_ff), F32), shape((exp_loc, d_ff, d_model), F32)) + tuple(shape((tok, d_model) if v is y0 or v is dx0 else v.shape, v.dtype) for v in small),
-            in_specs=[any_spec] * 10,
-            out_specs=(any_spec,) * 7,
+            out_shape=(shape((exp_loc, d_model, d_ff), F32), shape((exp_loc, d_model, d_ff), F32), shape((exp_loc, d_ff, d_model), F32)) + tuple(shape(v.shape, v.dtype) for v in small),
+            in_specs=[any_spec] * 8,
+            out_specs=(any_spec,) * 5,
             scratch_shapes=[pltpu.VMEM((d_model, total), BF16), pltpu.VMEM((total, d_model), BF16), pltpu.VMEM((total, LANES), F32),
                             pltpu.VMEM((exp_loc, total, d_ff), BF16), pltpu.VMEM((exp_loc, total, d_ff), BF16), pltpu.VMEM((exp_loc, d_ff, total), BF16),
                             pltpu.VMEM((slots, width, d_ff), F32), pltpu.VMEM((slots, width, d_ff), F32), pltpu.VMEM((slots, d_ff, width), F32)]
             + [pltpu.VMEM(v.shape, v.dtype) for v in small]
             + [pltpu.SemaphoreType.DMA((steps,)), pltpu.SemaphoreType.DMA((steps,)), pltpu.SemaphoreType.DMA(()), pltpu.SemaphoreType.DMA((exp_loc, 3)),
-               pltpu.SemaphoreType.DMA((slots, 3)), pltpu.SemaphoreType.DMA((4, 2))],
+               pltpu.SemaphoreType.DMA((slots, 3)), pltpu.SemaphoreType.DMA((2, 2))],
             compiler_params=pltpu.CompilerParams(vmem_limit_bytes=64500000),
             cost_estimate=pl.CostEstimate(flops=3 * 2 * total * d_model * d_ff * exp_loc, bytes_accessed=3 * 4 * exp_loc * d_model * d_ff, transcendentals=0),
             name='weight_grads',
-        )(xt, dy_all.reshape(total, d_model), gates.reshape(total, LANES), da, db, ht, attn, dgt, y0, dx0)
-        y, dx = (lax.dynamic_update_slice(whole, (own[t] + from_x[t] + from_y[t] + from_d[t]).astype(BF16), (r, 0)) for t, whole in enumerate((y, dx)))
+        )(xt, dy_all.reshape(total, d_model), gates.reshape(total, LANES), da, db, ht, attn, dgt)
+        def summed(first, width):
+            cols = slice(first, first + width)
+            return (own[:, cols] + from_x[:, cols] + from_y[:, cols] + from_d[:, cols]).astype(BF16)
+
+        y = jnp.concatenate([y0, summed(0, d_model)], axis=0)
+        dx = jnp.concatenate([jnp.concatenate([dx0[:, :d_model - 512], summed(2 * d_model, 512)], axis=1), summed(d_model, d_model)], axis=0)
         return y, dx, dgt.T, dw_gate, dw_up, dw_down, attn.reshape(x_attn.shape)
 
     spec_rows = P(TOKEN_AXES, None)

time: 84.7 us -> 83.8 us (0.989)
  Pallas kernels: 79.6 us -> 77.9 us
    pallas_call x1, Pallas kernels: 59.6 us -> 57.9 us  [local_step(): pl.pallas_call(kernel, out_shape=(shape((r, d_model), BF16), shape((r, d_...]
  transfers between devices with their start and end apart: 3 -> 3, of which waited for: 0 -> 1; matrix products, arithmetic and copies ran while one was open for 0% -> 0% of each run, Pallas kernels for 24% -> 24%
where the time goes in v7:
time: 83.8 us; the launch traced here: 83.6 us
  Pallas kernels  77.9 us (93%)
  starting transfers between devices  3.51 us (4%)
  other arithmetic  0.87 us (1%)
    pallas_call x1, Pallas kernels, local_step(): pl.pallas_call(kernel, out_shape=(shape((r, d_model), BF16), shape((r, d_...  57.9 us
    pallas_call x1, Pallas kernels, local_step(): pl.pallas_call(functools.partial(weight_grads, width, slots), out_shape=(...  20 us
    ppermute x3, starting transfers between devices, swap(): return lax.ppermute(value, GROUP_AXES, pairs)  3.51 us
  transfers between devices with their start and end apart: 3, of which 1 were waited for; matrix products, arithmetic and copies ran while one was open for 0% of the time, Pallas kernels for 24%

profile of v7, /device:TPU:0, one launch (start us, length us, event | category | flops | bytes accessed | tf_op | source)
XLA Modules:
  0.0 83.6 jit_solution(13211065406677446249)
XLA Ops:
  0.6 57.9 %layer.1 = (bf16[32,1536]{1,0:T(8,128)(2,1)}, bf16[32,1536]{1,0:T(8,128)(2,1)}, bf16[64,1536]{1,0:T(8,128)(2,1)}, f32[8,64]{1,0:T(8,128)}, bf16[1536,512]{1,0:T(...) custom-call(bf16[64,1536]{1,0:T(8,128)(2,1)} %x_in.1, ...), custom_call_target="tpu_custom_call" | custom-call | tf_op jit(solution)/shard_map/layer/pallas_call | solution.py:662
  58.5 1.7 %collective-permute-start = (f32[32,3584]{1,0:T(8,128)}, f32[32,3584]{1,0:T(8,128)S(1)}, u32[]{:S(2)}, u32[]{:S(2)}) collective-permute-start(f32[32,3584]{1,0:T(8,128)} %get-tuple-element.28), channel_id=1, source_target_pairs={{0,2},{1,3},{2,0},{3,1},{4,6},{5,7},{6,4},{7,5}} | collective-permute-start | bytes 1376264 | tf_op jit(solution)/shard_map/ppermute | solution.py:692
  60.2 0.4 collective-permute-start.1
  60.6 1.5 %collective-permute-start.2 = (f32[32,3584]{1,0:T(8,128)}, f32[32,3584]{1,0:T(8,128)S(1)}, u32[]{:S(2)}, u32[]{:S(2)}) collective-permute-start(f32[32,3584]{1,0:T(8,128)} %get-tuple-element.30), channel_id=1, source_target_pairs={{0,6},{1,7},{2,4},{3,5},{4,2},{5,3},{6,0},{7,1}} | collective-permute-start | bytes 1376264 | tf_op jit(solution)/shard_map/ppermute | solution.py:692
  62.0 0.0 copy-start.2
  62.0 0.0 copy-start
  62.1 0.0 copy-start.1
  62.1 20.0 %weight_grads.1 = (f32[5,1536,512]{2,1,0:T(8,128)}, f32[5,1536,512]{2,1,0:T(8,128)}, f32[5,512,1536]{2,1,0:T(8,128)}, bf16[64,1536]{1,0:T(8,128)(2,1)}, f32[8,64]{1,0:T(8,128)}) custom-call(bf16[1536,512]{1,0:T(8,128)(2,1)} %get-tuple-element.32.xt_in, bf16[512,1536]{1,0:T(8,128)(2,1)} %bitcast.24, f32[512,128]{1,0:T(8,128)} %bitcast.25, ...), custom_call_target="tpu_custom_call" | custom-call | flops 12079595520 | bytes 47185920 | tf_op jit(solution)/shard_map/weight_grads/pallas_call | solution.py:695
  82.0 0.0 copy-done.2
  82.1 0.0 collective-permute-done
  82.1 0.7 collective-permute-done.1
  82.7 0.0 collective-permute-done.2
  82.8 0.0 copy-done
  82.8 0.1 fusion
  82.9 0.0 copy-done.1
  82.9 0.8 pad_maximum_fusion
  (2 shorter events, 0.0 us)
Async XLA Ops:
  58.5 23.5 %collective-permute-start = (f32[32,3584]{1,0:T(8,128)}, f32[32,3584]{1,0:T(8,128)S(1)}, u32[]{:S(2)}, u32[]{:S(2)}) collective-permute-start(f32[32,3584]{1,0:T(8,128)} %get-tuple-element.28), channel_id=1, source_target_pairs={{0,2},{1,3},{2,0},{3,1},{4,6},{5,7},{6,4},{7,5}} | collective-permute-start | bytes 1376264 | tf_op jit(solution)/shard_map/ppermute | solution.py:692
  60.2 22.5 %collective-permute-start.1 = (f32[32,3584]{1,0:T(8,128)}, f32[32,3584]{1,0:T(8,128)S(1)}, u32[]{:S(2)}, u32[]{:S(2)}) collective-permute-start(f32[32,3584]{1,0:T(8,128)} %get-tuple-element.29), channel_id=1, source_target_pairs={{0,4},{1,5},{2,6},{3,7},{4,0},{5,1},{6,2},{7,3}} | collective-permute-start | bytes 1376264 | tf_op jit(solution)/shard_map/ppermute | solution.py:692
  60.6 22.2 %collective-permute-start.2 = (f32[32,3584]{1,0:T(8,128)}, f32[32,3584]{1,0:T(8,128)S(1)}, u32[]{:S(2)}, u32[]{:S(2)}) collective-permute-start(f32[32,3584]{1,0:T(8,128)} %get-tuple-element.30), channel_id=1, source_target_pairs={{0,6},{1,7},{2,4},{3,5},{4,2},{5,3},{6,0},{7,1}} | collective-permute-start | bytes 1376264 | tf_op jit(solution)/shard_map/ppermute | solution.py:692
  62.0 20.0 %copy-start.2 = (bf16[32,1536]{1,0:T(8,128)(2,1)S(1)}, bf16[32,1536]{1,0:T(8,128)(2,1)}, u32[]{:S(2)}) copy-start(bf16[32,1536]{1,0:T(8,128)(2,1)} %get-tuple-element.31) | copy-start | bytes 294916
  62.0 20.7 %copy-start = (f32[32,3584]{1,0:T(8,128)S(1)}, f32[32,3584]{1,0:T(8,128)}, u32[]{:S(2)}) copy-start(f32[32,3584]{1,0:T(8,128)} %get-tuple-element.27) | copy-start | bytes 1376260
  62.1 20.8 %copy-start.1 = (bf16[32,1536]{1,0:T(8,128)(2,1)S(1)}, bf16[32,1536]{1,0:T(8,128)(2,1)}, u32[]{:S(2)}) copy-start(bf16[32,1536]{1,0:T(8,128)(2,1)} %get-tuple-element.26) | copy-start | bytes 294916

commit v8 on v7

--- a/solution.py
+++ b/solution.py
@@ -292,7 +292,7 @@
         gtab[...] = jnp.zeros_like(gtab)
         for g in range(NUM_DEV):
             for e in range(exp_loc):
-                gtab[g, e:e + 1, 0:tok] = jnp.sum(jnp.where(idx_in[...] == g * exp_loc + e, gate_in[...], 0.0), axis=0, keepdims=True)
+                gtab[g, e:e + 1, 0:tok] = jnp.max(jnp.where(idx_in[...] == g * exp_loc + e, gate_in[...], -1.0), axis=0, keepdims=True)
         pl.semaphore_wait(barrier, len(peers))
 
         routes_sent, routes_in = pool.take(), pool.take()
@@ -361,7 +361,7 @@
         lane = lax.broadcasted_iota(jnp.int32, (m, LANES), 1)
 
         def gate_of(h, e):
-            return jnp.concatenate([gfull[h, e]] * (tile // LANES), axis=1)
+            return jnp.concatenate([jnp.maximum(gfull[h, e], 0.0)] * (tile // LANES), axis=1)
 
         def loop(count, events, body):
             def step(k, _):
@@ -381,7 +381,7 @@
                 def _():
                     staged(h, e - 2, 2).wait()
 
-                mask = gate_of(h, e) > 0.0
+                mask = jnp.concatenate([gfull[h, e]] * (tile // LANES), axis=1) >= 0.0
                 a = jnp.where(mask, dot_nn(xb[h], wg[e]), 0.0)
                 b = jnp.where(mask, dot_nn(xb[h], wu[e]), 0.0)
                 sig = jax.nn.sigmoid(a)
@@ -571,7 +571,7 @@
     lane = lax.broadcasted_iota(jnp.int32, g.shape, 1)
 
     def down(e):
-        gate = jnp.sum(jnp.where(lane == e, g[...], 0.0), axis=1, keepdims=True)
+        gate = jnp.maximum(jnp.sum(jnp.where(lane == e, g[...], 0.0), axis=1, keepdims=True), 0.0)
         for n in range(steps):
             part = pl.ds(n * width, width)
             sd[lax.rem(e, 2) * steps + n] = dot_nn(ht[e], (gate * dy[:, part].astype(F32)).astype(BF16))

time: 83.8 us -> 83.9 us (level)
  no operation moved by 1% of the time
where the time goes in v8:
time: 83.9 us; the launch traced here: 83.7 us
  Pallas kernels  78 us (93%)
  starting transfers between devices  3.51 us (4%)
  other arithmetic  0.87 us (1%)
    pallas_call x1, Pallas kernels, local_step(): pl.pallas_call(kernel, out_shape=(shape((r, d_model), BF16), shape((r, d_...  58 us
    pallas_call x1, Pallas kernels, local_step(): pl.pallas_call(functools.partial(weight_grads, width, slots), out_shape=(...  20 us
    ppermute x3, starting transfers between devices, swap(): return lax.ppermute(value, GROUP_AXES, pairs)  3.51 us
  transfers between devices with their start and end apart: 3, of which 1 were waited for; matrix products, arithmetic and copies ran while one was open for 0% of the time, Pallas kernels for 24%

profile of v8, /device:TPU:0, one launch (start us, length us, event | category | flops | bytes accessed | tf_op | source)
XLA Modules:
  0.0 83.7 jit_solution(8207706449653695319)
XLA Ops:
  0.6 58.0 %layer.1 = (bf16[32,1536]{1,0:T(8,128)(2,1)}, bf16[32,1536]{1,0:T(8,128)(2,1)}, bf16[64,1536]{1,0:T(8,128)(2,1)}, f32[8,64]{1,0:T(8,128)}, bf16[1536,512]{1,0:T(...) custom-call(bf16[64,1536]{1,0:T(8,128)(2,1)} %x_in.1, ...), custom_call_target="tpu_custom_call" | custom-call | tf_op jit(solution)/shard_map/layer/pallas_call | solution.py:662
  58.6 1.6 %collective-permute-start = (f32[32,3584]{1,0:T(8,128)}, f32[32,3584]{1,0:T(8,128)S(1)}, u32[]{:S(2)}, u32[]{:S(2)}) collective-permute-start(f32[32,3584]{1,0:T(8,128)} %get-tuple-element.28), channel_id=1, source_target_pairs={{0,2},{1,3},{2,0},{3,1},{4,6},{5,7},{6,4},{7,5}} | collective-permute-start | bytes 1376264 | tf_op jit(solution)/shard_map/ppermute | solution.py:692
  60.3 0.4 collective-permute-start.1
  60.7 1.5 %collective-permute-start.2 = (f32[32,3584]{1,0:T(8,128)}, f32[32,3584]{1,0:T(8,128)S(1)}, u32[]{:S(2)}, u32[]{:S(2)}) collective-permute-start(f32[32,3584]{1,0:T(8,128)} %get-tuple-element.30), channel_id=1, source_target_pairs={{0,6},{1,7},{2,4},{3,5},{4,2},{5,3},{6,0},{7,1}} | collective-permute-start | bytes 1376264 | tf_op jit(solution)/shard_map/ppermute | solution.py:692
  62.1 0.0 copy-start.2
  62.1 0.0 copy-start
  62.2 0.0 copy-start.1
  62.2 20.0 %weight_grads.1 = (f32[5,1536,512]{2,1,0:T(8,128)}, f32[5,1536,512]{2,1,0:T(8,128)}, f32[5,512,1536]{2,1,0:T(8,128)}, bf16[64,1536]{1,0:T(8,128)(2,1)}, f32[8,64]{1,0:T(8,128)}) custom-call(bf16[1536,512]{1,0:T(8,128)(2,1)} %get-tuple-element.32.xt_in, bf16[512,1536]{1,0:T(8,128)(2,1)} %bitcast.24, f32[512,128]{1,0:T(8,128)} %bitcast.25, ...), custom_call_target="tpu_custom_call" | custom-call | flops 12079595520 | bytes 47185920 | tf_op jit(solution)/shard_map/weight_grads/pallas_call | solution.py:695
  82.2 0.0 copy-done.2
  82.2 0.0 collective-permute-done
  82.2 0.6 collective-permute-done.1
  82.8 0.0 collective-permute-done.2
  82.8 0.0 copy-done
  82.8 0.1 fusion
  82.9 0.0 copy-done.1
  82.9 0.8 pad_maximum_fusion
  (2 shorter events, 0.0 us)
Async XLA Ops:
  58.6 23.5 %collective-permute-start = (f32[32,3584]{1,0:T(8,128)}, f32[32,3584]{1,0:T(8,128)S(1)}, u32[]{:S(2)}, u32[]{:S(2)}) collective-permute-start(f32[32,3584]{1,0:T(8,128)} %get-tuple-element.28), channel_id=1, source_target_pairs={{0,2},{1,3},{2,0},{3,1},{4,6},{5,7},{6,4},{7,5}} | collective-permute-start | bytes 1376264 | tf_op jit(solution)/shard_map/ppermute | solution.py:692
  60.3 22.5 %collective-permute-start.1 = (f32[32,3584]{1,0:T(8,128)}, f32[32,3584]{1,0:T(8,128)S(1)}, u32[]{:S(2)}, u32[]{:S(2)}) collective-permute-start(f32[32,3584]{1,0:T(8,128)} %get-tuple-element.29), channel_id=1, source_target_pairs={{0,4},{1,5},{2,6},{3,7},{4,0},{5,1},{6,2},{7,3}} | collective-permute-start | bytes 1376264 | tf_op jit(solution)/shard_map/ppermute | solution.py:692
  60.7 22.1 %collective-permute-start.2 = (f32[32,3584]{1,0:T(8,128)}, f32[32,3584]{1,0:T(8,128)S(1)}, u32[]{:S(2)}, u32[]{:S(2)}) collective-permute-start(f32[32,3584]{1,0:T(8,128)} %get-tuple-element.30), channel_id=1, source_target_pairs={{0,6},{1,7},{2,4},{3,5},{4,2},{5,3},{6,0},{7,1}} | collective-permute-start | bytes 1376264 | tf_op jit(solution)/shard_map/ppermute | solution.py:692
  62.1 20.0 %copy-start.2 = (bf16[32,1536]{1,0:T(8,128)(2,1)S(1)}, bf16[32,1536]{1,0:T(8,128)(2,1)}, u32[]{:S(2)}) copy-start(bf16[32,1536]{1,0:T(8,128)(2,1)} %get-tuple-element.31) | copy-start | bytes 294916
  62.1 20.7 %copy-start = (f32[32,3584]{1,0:T(8,128)S(1)}, f32[32,3584]{1,0:T(8,128)}, u32[]{:S(2)}) copy-start(f32[32,3584]{1,0:T(8,128)} %get-tuple-element.27) | copy-start | bytes 1376260
  62.2 20.8 %copy-start.1 = (bf16[32,1536]{1,0:T(8,128)(2,1)S(1)}, bf16[32,1536]{1,0:T(8,128)(2,1)}, u32[]{:S(2)}) copy-start(bf16[32,1536]{1,0:T(8,128)(2,1)} %get-tuple-element.26) | copy-start | bytes 294916
